TPU v7x, 128 devices: a whole 4x4x4 slice. The times are simulated.
128 devices in a mesh: seq: 64 (over x, y, z), head: 2 (over core).
Axes of the slice: x: 4, y: 4, z: 4, core: 2. Of those that a mesh axis runs over, the one named last changes fastest.
Arguments:
- tokens: bfloat16 [65536, 2048], P('seq'), may hold values from -6 to 6
- w_query: bfloat16 [2048, 256], P(None, 'head'), may hold values from -0.25 to 0.25
- w_key: bfloat16 [2048, 256], P(None, 'head'), may hold values from -0.25 to 0.25
- w_value: bfloat16 [2048, 2048], P(None, 'head'), may hold values from -0.125 to 0.125
- w_out: bfloat16 [2048, 2048], replicated, may hold values from -1.796875 to 1.796875
Outputs:
- mixed: bfloat16 [65536, 2048], P('seq', 'head')
All inputs are finite; a program needn't handle non-finite values.
Results may differ from a plain program's by a relative error of at most 0.011.
Values may be sent and summed in bfloat16 or wider, within the bound.
No kernel may reach another device: no remote copies, remote signals or barrier semaphores. Data moves between devices by JAX's collectives and lax.ppermute only.
A program may use at most 128 MiB of HBM per device.

v0:
```python
import functools

import jax
import jax.numpy as jnp
import numpy as np
from jax import lax
from jax.experimental import pallas as pl
from jax.experimental.pallas import tpu as pltpu
from jax.sharding import Mesh
from jax.sharding import PartitionSpec as P


ROWS = 160
CHUNK = 256
SEQ = ("seq_0", "seq_1", "seq_2")
STEPS = (2, 1, 3)
MIB = 2**20
HEAD_LIMIT, FETCH_LIMIT, OUT_LIMIT = (48 * MIB, 44 * MIB, 20 * MIB)
SLOTS = (0, 2, 1, 3)
OUT_STEPS = (0, 1, 3, 2)
F32, BF16 = (jnp.float32, jnp.bfloat16)
VMEM = pl.BlockSpec(memory_space=pltpu.VMEM)
SMEM = pl.BlockSpec(memory_space=pltpu.SMEM)
ANY = pl.BlockSpec(memory_space=pl.ANY)
NN = (((1,), (0,)), ((), ()))


def mm(a, b):
    return lax.dot_general(a, b, NN, preferred_element_type=F32)


def quarter_of(step):
    return lax.axis_index(SEQ[2]) ^ step


def feature_tables():
    first, second, scale = ([-1] * ROWS, [-1] * ROWS, [0.0] * ROWS)
    for d in range(9):
        for a in range(16 if d < 8 else 8):
            row = 16 * d + a
            first[row], second[row] = (a, (a + d) % 16)
            scale[row] = 1.0 / 32.0 if d == 0 else 1.0 / 16.0
    for a in range(16):
        first[136 + a], scale[136 + a] = (a, 0.25)
    scale[152] = 1.0
    table = np.zeros((8, ROWS), np.float32)
    table[0], table[1], table[2] = (first, second, scale)
    table[3, 152] = 1.0
    table[4, 136:153] = scale[136:153]
    return table


def key_features(u):
    tok = u.shape[1]
    blocks = [u * u]
    for d in range(1, 9):
        blocks.append(u * pltpu.roll(u, 16 - d, 0))
    blocks[8] = blocks[8][:8]
    row = lax.broadcasted_iota(jnp.int32, (8, tok), 0)
    tail = jnp.where(row == 0, 1.0, 0.0)
    return jnp.concatenate(blocks + [u, tail], axis=0).astype(BF16)


def norm_rows(norm):
    top = jnp.transpose(norm[:128])[:1]
    rest = jnp.concatenate([norm[128:], jnp.zeros((96, 128), F32)], axis=0)
    low = jnp.transpose(rest)[:1]
    row = lax.broadcasted_iota(jnp.int32, (8, 128), 0)
    return jnp.where(row == 1, top, jnp.where(row == 2, low, 0.0))


def head_kernel(
    x_hbm, wk_hbm, wq_hbm, wv_hbm,
    q_out, kt_out, val_out, local_out, s0, s1, s2, s3,
    x, wkq, wv, acc, kt, x_sem, w_sem, v_sem,
):
    tok, width = x.shape
    cuts = 4
    cut = width // cuts
    kd = wk_hbm.shape[1]

    def wcopy(j, src, half):
        rows = pl.ds(j * cut, cut)
        return pltpu.make_async_copy(
            src.at[rows], wkq.at[rows, pl.ds(half * kd, kd)], w_sem.at[2 * j + half]
        )

    def xcopy(j):
        cols = pl.ds(j * cut, cut)
        return pltpu.make_async_copy(x_hbm.at[:, cols], x.at[:, cols], x_sem.at[j])

    def vcopy(s):
        start = pl.multiple_of(quarter_of(SLOTS[s]) * 256, 256)
        return pltpu.make_async_copy(
            wv_hbm.at[:, pl.ds(start, 256)],
            wv.at[s // 2, :, pl.ds(s % 2 * 256, 256)],
            v_sem.at[s],
        )

    for j in range(cuts):
        wcopy(j, wk_hbm, 0).start()
        wcopy(j, wq_hbm, 1).start()
        xcopy(j).start()
    for s in range(4):
        vcopy(s).start()
    for j in range(cuts):
        wcopy(j, wk_hbm, 0).wait()
        wcopy(j, wq_hbm, 1).wait()
        xcopy(j).wait()
        cols = slice(j * cut, (j + 1) * cut)
        for rows in (slice(0, tok // 2), slice(tok // 2, tok)):
            part = mm(x[rows, cols], wkq[cols])
            acc[rows] = part if j == 0 else acc[rows] + part
    q_out[...] = acc[:, kd:].astype(BF16)
    keys = jnp.transpose(acc[:, :kd].astype(BF16).astype(F32))
    kt[...] = keys
    kt_out[...] = keys.astype(BF16)
    ones = jnp.ones((CHUNK, 128), BF16)
    for s, state in enumerate((s0, s1, s2, s3)):
        if s % 2 == 0:
            vcopy(s).wait()
            vcopy(s + 1).wait()
            pair = mm(x[...], wv[s // 2]).astype(BF16)
        val = pair[:, s % 2 * 256 : s % 2 * 256 + 256]
        val_out[s] = val
        for h in range(2):
            at = pl.multiple_of((quarter_of(SLOTS[s]) * 2 + h) * 16, 16)
            feat = key_features(kt[pl.ds(at, 16), :])
            run = None
            for c in range(tok // CHUNK):
                rows = slice(c * CHUNK, (c + 1) * CHUNK)
                right = jnp.concatenate([val[rows, h * 128 : (h + 1) * 128], ones], axis=1)
                part = mm(feat[:, rows], right)
                run = part if c == 0 else run + part
                if c < tok // CHUNK - 1:
                    local_out[s, h, c] = run.astype(BF16)
            state[h, :152] = run[:152, :128].astype(BF16)
            extra = norm_rows(run[:, 128:])
            row = lax.broadcasted_iota(jnp.int32, (8, 128), 0)
            state[h, 152:] = jnp.where(row == 0, run[152:, :128], extra).astype(BF16)


def head_stage(tokens, w_key, w_query, w_value):
    tok, width = tokens.shape
    kd = w_key.shape[1]
    chunks = tok // CHUNK
    shape = jax.ShapeDtypeStruct
    return pl.pallas_call(
        head_kernel,
        out_shape=[
            shape((tok, kd), BF16),
            shape((kd, tok), BF16),
            shape((4, tok, 256), BF16),
            shape((4, 2, chunks - 1, ROWS, 256), BF16),
        ]
        + [shape((2, ROWS, 128), BF16)] * 4,
        in_specs=[ANY] * 4,
        out_specs=[VMEM] * 8,
        scratch_shapes=[
            pltpu.VMEM((tok, width), BF16),
            pltpu.VMEM((width, 2 * kd), BF16),
            pltpu.VMEM((2, width, 512), BF16),
            pltpu.VMEM((tok, 2 * kd), F32),
            pltpu.VMEM((kd, tok), F32),
            pltpu.SemaphoreType.DMA((4,)),
            pltpu.SemaphoreType.DMA((8,)),
            pltpu.SemaphoreType.DMA((4,)),
        ],
        compiler_params=pltpu.CompilerParams(vmem_limit_bytes=HEAD_LIMIT),
        cost_estimate=pl.CostEstimate(
            flops=6 * 10**9, bytes_accessed=12 * 2**20, transcendentals=0
        ),
        name="head_stage",
    )(tokens, w_key, w_query, w_value)


def inner_kernel(slot, q_ref, kt_ref, val_ref, local_ref, table_ref, feat_out, part_out):
    tok = q_ref.shape[0]
    ones = jnp.ones((CHUNK, 128), BF16)
    below = lax.broadcasted_iota(jnp.int32, (CHUNK, CHUNK), 0) >= lax.broadcasted_iota(
        jnp.int32, (CHUNK, CHUNK), 1
    )
    first, second, scale = (table_ref[0:1], table_ref[1:2], table_ref[2:3])
    add_first, add_second = (table_ref[3:4], table_ref[4:5])
    entry = lax.broadcasted_iota(jnp.int32, (128, ROWS), 0).astype(F32)
    lane = lax.broadcasted_iota(jnp.int32, (CHUNK, 128), 1)
    for h in range(2):
        at = (quarter_of(SLOTS[slot]) * 2 + h) * 16
        base = at.astype(F32)
        pick_first = jnp.where((entry == first + base) & (first >= 0), 1.0, 0.0).astype(BF16)
        pick_second = jnp.where((entry == second + base) & (second >= 0), scale, 0.0).astype(BF16)
        mine = (lane >= at) & (lane < at + 16)
        for c in range(tok // CHUNK):
            rows = slice(c * CHUNK, (c + 1) * CHUNK)
            q = q_ref[rows]
            feat = (mm(q, pick_first) + add_first) * (mm(q, pick_second) + add_second)
            feat = feat.astype(BF16)
            feat_out[h, rows] = feat
            own = jnp.where(mine, q.astype(F32) * 0.25, 0.0).astype(BF16)
            s = mm(own, kt_ref[:, rows])
            taylor = jnp.where(below, (0.5 * s + 1.0) * s + 1.0, 0.0).astype(BF16)
            right = jnp.concatenate([val_ref[0, rows, h * 128 : (h + 1) * 128], ones], axis=1)
            part = mm(taylor, right)
            if c > 0:
                part = part + mm(feat, local_ref[0, h, c - 1])
            part_out[h, rows] = part


def inner_stage(slot, q, kt, val, local, table):
    tok = q.shape[0]
    shape = jax.ShapeDtypeStruct
    return pl.pallas_call(
        functools.partial(inner_kernel, slot),
        grid=(1,),
        out_shape=[shape((2, tok, ROWS), BF16), shape((2, tok, 256), F32)],
        in_specs=[
            pl.BlockSpec(q.shape, lambda i: (0, 0)),
            pl.BlockSpec(kt.shape, lambda i: (0, 0)),
            pl.BlockSpec((1,) + val.shape[1:], lambda i: (slot, 0, 0)),
            pl.BlockSpec((1,) + local.shape[1:], lambda i: (slot, 0, 0, 0, 0)),
            pl.BlockSpec(table.shape, lambda i: (0, 0)),
        ],
        out_specs=[
            pl.BlockSpec((2, tok, ROWS), lambda i: (0, 0, 0)),
            pl.BlockSpec((2, tok, 256), lambda i: (0, 0, 0)),
        ],
        compiler_params=pltpu.CompilerParams(vmem_limit_bytes=16 * 2**20),
        cost_estimate=pl.CostEstimate(
            flops=2 * 10**9, bytes_accessed=4 * 2**20, transcendentals=0
        ),
        name="inner_stage",
    )(q, kt, val, local, table)


def outer_kernel(count, *refs):
    prefixes, feats, parts, out = (
        refs[:count], refs[count : 2 * count], refs[2 * count : 3 * count], refs[3 * count]
    )
    for i in range(count):
        for h in range(2):
            low = prefixes[i][h]
            wide = low[152:].astype(F32)
            top = jnp.transpose(jnp.broadcast_to(wide[1:2], (128, 128)))
            rest = jnp.transpose(jnp.broadcast_to(wide[2:3], (128, 128)))[:32]
            norm = jnp.concatenate([top, rest], axis=0).astype(BF16)
            right = jnp.concatenate([low, norm], axis=1)
            both = mm(feats[i][h], right) + parts[i][h]
            cols = slice(i * 256 + h * 128, i * 256 + (h + 1) * 128)
            out[:, cols] = (both[:, :128] / both[:, 128:]).astype(BF16)


def outer_stage(prefixes, feats, parts):
    count = len(prefixes)
    tok = feats[0].shape[1]
    return pl.pallas_call(
        functools.partial(outer_kernel, count),
        out_shape=jax.ShapeDtypeStruct((tok, 256 * count), BF16),
        in_specs=[VMEM] * (3 * count),
        out_specs=VMEM,
        compiler_params=pltpu.CompilerParams(vmem_limit_bytes=24 * 2**20),
        cost_estimate=pl.CostEstimate(
            flops=3 * 10**8 * count, bytes_accessed=2**20 * count, transcendentals=0
        ),
        name="outer_stage",
    )(*prefixes, *feats, *parts)


def fetch_kernel(w_hbm, out, sem):
    own = lax.axis_index("head")
    cols = pl.ds(pl.multiple_of(own * 1024, 1024), 1024)

    def copy(half, s):
        start = pl.multiple_of((own ^ half) * 1024 + quarter_of(OUT_STEPS[s]) * 256, 256)
        return pltpu.make_async_copy(
            w_hbm.at[pl.ds(start, 256), cols],
            out.at[half, pl.ds(s * 256, 256)],
            sem.at[half * 4 + s],
        )

    pieces = [copy(half, s) for half in range(2) for s in range(4)]
    for piece in pieces:
        piece.start()
    for piece in pieces:
        piece.wait()


def fetch_stage(w_out):
    return pl.pallas_call(
        fetch_kernel,
        out_shape=jax.ShapeDtypeStruct((2, 1024, 1024), BF16),
        in_specs=[ANY],
        out_specs=VMEM,
        scratch_shapes=[pltpu.SemaphoreType.DMA((8,))],
        compiler_params=pltpu.CompilerParams(vmem_limit_bytes=FETCH_LIMIT),
        cost_estimate=pl.CostEstimate(
            flops=10**9, bytes_accessed=8 * 2**20, transcendentals=0
        ),
        name="fetch_stage",
    )(w_out)


def out_kernel(half, a_ref, b_ref, w_ref, *rest):
    wide = a_ref.shape[1]
    blocks = a_ref.shape[0] // CHUNK
    for c in range(blocks):
        rows = slice(c * CHUNK, (c + 1) * CHUNK)
        part = mm(a_ref[rows], w_ref[half, :wide]) + mm(b_ref[rows], w_ref[half, wide:])
        if half == 0:
            rest[0][rows] = part
        else:
            acc, out, stage, sem = rest
            stage[rows] = (part + acc[rows]).astype(BF16)
            pltpu.make_async_copy(stage.at[rows], out.at[rows], sem.at[c]).start()
    if half == 1:
        acc, out, stage, sem = rest
        for c in range(blocks):
            rows = slice(c * CHUNK, (c + 1) * CHUNK)
            pltpu.make_async_copy(stage.at[rows], out.at[rows], sem.at[c]).wait()


def out_stage(half, most, rest, columns, acc=None):
    tok = most.shape[0]
    first = half == 0
    return pl.pallas_call(
        functools.partial(out_kernel, half),
        out_shape=jax.ShapeDtypeStruct((tok, 1024), F32 if first else BF16),
        in_specs=[VMEM] * (3 if first else 4),
        out_specs=VMEM if first else ANY,
        scratch_shapes=[]
        if first
        else [pltpu.VMEM((tok, 1024), BF16), pltpu.SemaphoreType.DMA((tok // CHUNK,))],
        compiler_params=pltpu.CompilerParams(vmem_limit_bytes=OUT_LIMIT),
        cost_estimate=pl.CostEstimate(
            flops=2 * 10**9, bytes_accessed=8 * 2**20, transcendentals=0
        ),
        name="out_stage",
    )(*([most, rest, columns] + ([] if first else [acc])))


def partner(x, axis, step):
    pairs = [(i, i ^ step) for i in range(4)]
    return lax.ppermute(x, axis, pairs)


def total_kernel(p0, p1, p2, p3, out):
    total = p0[...].astype(F32) + p1[...].astype(F32)
    out[...] = (total + p2[...].astype(F32) + p3[...].astype(F32)).astype(BF16)


def level_kernel(axis, own, g0, g1, g2, base_in, total, base):
    at = lax.axis_index(axis)
    run, before = (own[...].astype(F32), jnp.zeros(own.shape, F32))
    if base_in is not None:
        before = base_in[...]
    for step, ref in zip(STEPS, (g0, g1, g2)):
        got = ref[...].astype(F32)
        run = run + got
        before = before + got * ((at ^ step) < at).astype(F32)
    if total is not None:
        total[...] = run.astype(BF16)
    base[...] = before


def spread_kernel(own, g0, g1, g2, base_in, p0, p1, p2, p3, o0, o1, o2, o3, base):
    level_kernel(SEQ[0], own, g0, g1, g2, base_in, None, base)
    at = lax.axis_index(SEQ[2])
    parts = [p[...].astype(F32) for p in (p0, p1, p2, p3)]
    for mine, out in zip(SLOTS, (o0, o1, o2, o3)):
        run = base[...]
        for step, part in zip(SLOTS, parts):
            run = run + part * ((at ^ step) < (at ^ mine)).astype(F32)
        out[...] = run.astype(BF16)


def small_call(kernel, outs, *args, scratch=(), after=()):
    shape = args[0].shape
    return pl.pallas_call(
        kernel,
        out_shape=[jax.ShapeDtypeStruct(shape, kind) for kind in outs],
        in_specs=[VMEM] * len(args) + [ANY] * len(after),
        out_specs=[VMEM] * len(outs),
        scratch_shapes=list(scratch),
        compiler_params=pltpu.CompilerParams(vmem_limit_bytes=4 * 2**20),
        cost_estimate=pl.CostEstimate(flops=10**6, bytes_accessed=2**20, transcendentals=0),
    )(*args, *after)


def middle_kernel(own, g0, g1, g2, columns, total, base):
    level_kernel(SEQ[1], own, g0, g1, g2, None, total, base)


def exclusive_prefix(states, columns):
    parts = [states[0]] + [partner(state, SEQ[2], step) for step, state in zip(STEPS, states[1:])]
    (low,) = small_call(total_kernel, [BF16], *parts)
    got = [partner(low, SEQ[1], step) for step in STEPS]
    total, base = small_call(middle_kernel, [BF16, F32], low, *got, after=[columns])
    got = [partner(total, SEQ[0], step) for step in STEPS]
    scratch = [pltpu.VMEM(low.shape, F32)]
    outs = small_call(spread_kernel, [BF16] * 4, total, *got, base, *parts, scratch=scratch)
    back = {0: outs[0]}
    for step, out in zip(STEPS, outs[1:]):
        back[step] = partner(out, SEQ[2], step)
    return back


def per_device(tokens, w_query, w_key, w_value, w_out):
    table = jnp.asarray(feature_tables())
    q, kt, val, local, *states = head_stage(tokens, w_key, w_query, w_value)
    columns = fetch_stage(w_out)
    back = exclusive_prefix(states, columns)
    inner = {}
    for slot, step in enumerate(SLOTS):
        inner[step] = inner_stage(slot, q, kt, val, local, table)

    def outer(steps):
        return outer_stage(
            [back[step] for step in steps],
            [inner[step][0] for step in steps],
            [inner[step][1] for step in steps],
        )

    most, rest = (outer(OUT_STEPS[:3]), outer(OUT_STEPS[3:]))
    swap = [(0, 1), (1, 0)]
    other_most = lax.ppermute(most, "head", swap)
    other_rest = lax.ppermute(rest, "head", swap)
    acc = out_stage(0, most, rest, columns)
    return out_stage(1, other_most, other_rest, columns, acc)


def solution(mesh):
    split = Mesh(
        mesh.devices.reshape(4, 4, 4, mesh.shape["head"]), ("seq_0", "seq_1", "seq_2", "head")
    )
    in_specs = (P(SEQ, None), P(None, "head"), P(None, "head"), P(None, "head"), P())
    out_specs = P(SEQ, "head")
    return jax.shard_map(
        per_device, mesh=split, in_specs=in_specs, out_specs=out_specs, check_vma=False
    )
```

profile of v0, /device:TPU:1, one launch (start us, length us, event | category | flops | bytes accessed | tf_op | source)
XLA Modules:
  0.0 61.9 jit_solution(3194809199410785413)
XLA Ops:
  0.0 0.0 copy-start
  0.0 1.0 %copy-done = bf16[2048,128]{1,0:T(8,128)(2,1)S(1)} copy-done((bf16[2048,128]{1,0:T(8,128)(2,1)S(1)}, bf16[2048,128]{1,0:T(8,128)(2,1)}, u32[]{:S(2)}) %copy-start) | copy-done | bytes 524312
  1.0 0.0 copy-start.1
  1.0 1.0 %copy-done.1 = bf16[2048,128]{1,0:T(8,128)(2,1)S(1)} copy-done((bf16[2048,128]{1,0:T(8,128)(2,1)S(1)}, bf16[2048,128]{1,0:T(8,128)(2,1)}, u32[]{:S(2)}) %copy-start.1) | copy-done | bytes 524312
  2.1 0.0 copy-start.2
  2.1 8.7 %head_stage.1 = (bf16[1024,128]{1,0:T(8,128)(2,1)S(1)}, bf16[128,1024]{1,0:T(8,128)(2,1)S(1)}, bf16[4,1024,256]{2,1,0:T(8,128)(2,1)S(1)}, bf16[4,2,3,160,256]{4,...) custom-call(bf16[1024,2048]{1,0:T(8,128)(2,1)} %x_hbm.1, ...), custom_call_target="tpu_custom_call" | custom-call | flops 6000000000 | bytes 12582912 | tf_op jit(solution)/shard_map/head_stage/pallas_call | solution.py:148
  10.8 4.5 %collective-permute-start = (bf16[2,160,128]{2,1,0:T(8,128)(2,1)S(1)}, bf16[2,160,128]{2,1,0:T(8,128)(2,1)S(1)}, u32[]{:S(2)}, u32[]{:S(2)}) collective-permute-start(bf16[2,160,128]{2,1,0:T(8,128)(2,1)S(1)} %get-tuple-element.28), channel_id=1, source_target_pairs={{0,4},{2,6},{4,0},{6,2},{1,5},{3,7},{5,1},{7,3},{8,12},{10,14},{12... | collective-permute-start | bytes 245768 | tf_op jit(solution)/shard_map/ppermute | solution.py:342
  15.3 0.8 %collective-permute-start.1 = (bf16[2,160,128]{2,1,0:T(8,128)(2,1)S(1)}, bf16[2,160,128]{2,1,0:T(8,128)(2,1)S(1)}, u32[]{:S(2)}, u32[]{:S(2)}) collective-permute-start(bf16[2,160,128]{2,1,0:T(8,128)(2,1)S(1)} %get-tuple-element.29), channel_id=1, source_target_pairs={{0,2},{2,0},{4,6},{6,4},{1,3},{3,1},{5,7},{7,5},{8,10},{10,8},{12,... | collective-permute-start | bytes 245768 | tf_op jit(solution)/shard_map/ppermute | solution.py:342
  16.1 0.0 collective-permute-start.2
  16.1 0.0 copy-done.2
  16.1 1.9 %inner_stage.6 = (bf16[2,1024,160]{2,1,0:T(8,128)(2,1)S(1)}, f32[2,1024,256]{2,1,0:T(8,128)S(1)}) custom-call(bf16[1024,128]{1,0:T(8,128)(2,1)S(1)} %get-tuple-element.36.q_ref, bf16[128,1024]{1,0:T(8,128)(2,1)S(1)} %get-tuple-element.37.kt_ref, bf16[4,1024,256]{2,1,0:T(8,128)(2,1)S(1)} %get-tuple-element.38.val_ref, ...), custom_call_target="tpu_custom_call" | custom-call | flops 2000000000 | bytes 4194304 | tf_op jit(solution)/shard_map/inner_stage/pallas_call | solution.py:212
  18.0 0.0 collective-permute-done.p1
  18.0 1.4 %collective-permute-done.1.p2 = bf16[2,160,128]{2,1,0:T(8,128)(2,1)S(1)} collective-permute-done((bf16[2,160,128]{2,1,0:T(8,128)(2,1)S(1)}, bf16[2,160,128]{2,1,0:T(8,128)(2,1)S(1)}, u32[]{:S(2)}, u32[]{:S(2)}) %collective-permute-start.1) | collective-permute-done | bytes 81952 | tf_op jit(solution)/shard_map/ppermute | solution.py:342
  19.4 1.2 %collective-permute-done.2.p3 = bf16[2,160,128]{2,1,0:T(8,128)(2,1)S(1)} collective-permute-done((bf16[2,160,128]{2,1,0:T(8,128)(2,1)S(1)}, bf16[2,160,128]{2,1,0:T(8,128)(2,1)S(1)}, u32[]{:S(2)}, u32[]{:S(2)}) %collective-permute-start.2) | collective-permute-done | bytes 81952 | tf_op jit(solution)/shard_map/ppermute | solution.py:342
  20.6 3.0 %collective-permute-start.3 = (bf16[2,160,128]{2,1,0:T(8,128)(2,1)S(1)}, bf16[2,160,128]{2,1,0:T(8,128)(2,1)S(1)}, u32[]{:S(2)}, u32[]{:S(2)}) collective-permute-start(bf16[2,160,128]{2,1,0:T(8,128)(2,1)S(1)} %shard_map.64.own), channel_id=1, source_target_pairs={{0,16},{8,24},{16,0},{24,8},{1,17},{9,25},{17,1},{25,9},{2,18},{10... | collective-permute-start | bytes 245768 | tf_op jit(solution)/shard_map/ppermute | solution.py:342
  23.6 0.4 collective-permute-start.4
  24.0 0.4 collective-permute-start.5
  24.4 2.2 %fetch_stage.1.columns.w_ref = bf16[2,1024,1024]{2,1,0:T(8,128)(2,1)S(1)} custom-call(bf16[2048,2048]{1,0:T(8,128)(2,1)} %w_hbm.1), custom_call_target="tpu_custom_call" | custom-call | flops 1000000000 | bytes 8388608 | tf_op jit(solution)/shard_map/fetch_stage/pallas_call | solution.py:288
  26.6 0.0 collective-permute-done.3.g0
  26.6 0.3 collective-permute-done.4.g1
  26.9 2.3 %collective-permute-done.5.g2 = bf16[2,160,128]{2,1,0:T(8,128)(2,1)S(1)} collective-permute-done((bf16[2,160,128]{2,1,0:T(8,128)(2,1)S(1)}, bf16[2,160,128]{2,1,0:T(8,128)(2,1)S(1)}, u32[]{:S(2)}, u32[]{:S(2)}) %collective-permute-start.5) | collective-permute-done | bytes 81952 | tf_op jit(solution)/shard_map/ppermute | solution.py:342
  29.2 0.1 shard_map.65
  29.3 2.8 %collective-permute-start.6 = (bf16[2,160,128]{2,1,0:T(8,128)(2,1)S(1)}, bf16[2,160,128]{2,1,0:T(8,128)(2,1)S(1)}, u32[]{:S(2)}, u32[]{:S(2)}) collective-permute-start(bf16[2,160,128]{2,1,0:T(8,128)(2,1)S(1)} %get-tuple-element.31.own), channel_id=1, source_target_pairs={{0,64},{32,96},{64,0},{96,32},{1,65},{33,97},{65,1},{97,33},{2,66}... | collective-permute-start | bytes 245768 | tf_op jit(solution)/shard_map/ppermute | solution.py:342
  32.1 0.3 collective-permute-start.7
  32.4 0.5 collective-permute-start.8
  33.0 1.9 %inner_stage.5 = (bf16[2,1024,160]{2,1,0:T(8,128)(2,1)S(1)}, f32[2,1024,256]{2,1,0:T(8,128)S(1)}) custom-call(bf16[1024,128]{1,0:T(8,128)(2,1)S(1)} %get-tuple-element.36.q_ref, bf16[128,1024]{1,0:T(8,128)(2,1)S(1)} %get-tuple-element.37.kt_ref, bf16[4,1024,256]{2,1,0:T(8,128)(2,1)S(1)} %get-tuple-element.38.val_ref, ...), custom_call_target="tpu_custom_call" | custom-call | flops 2000000000 | bytes 4194304 | tf_op jit(solution)/shard_map/inner_stage/pallas_call | solution.py:212
  34.9 0.0 collective-permute-done.6.g0
  34.9 0.5 collective-permute-done.7.g1
  35.4 1.5 %collective-permute-done.8.g2 = bf16[2,160,128]{2,1,0:T(8,128)(2,1)S(1)} collective-permute-done((bf16[2,160,128]{2,1,0:T(8,128)(2,1)S(1)}, bf16[2,160,128]{2,1,0:T(8,128)(2,1)S(1)}, u32[]{:S(2)}, u32[]{:S(2)}) %collective-permute-start.8) | collective-permute-done | bytes 81952 | tf_op jit(solution)/shard_map/ppermute | solution.py:342
  36.9 0.3 shard_map.66
  37.2 2.3 %collective-permute-start.10 = (bf16[2,160,128]{2,1,0:T(8,128)(2,1)S(1)}, bf16[2,160,128]{2,1,0:T(8,128)(2,1)S(1)}, u32[]{:S(2)}, u32[]{:S(2)}) collective-permute-start(bf16[2,160,128]{2,1,0:T(8,128)(2,1)S(1)} %get-tuple-element.35), channel_id=1, source_target_pairs={{0,6},{2,4},{4,2},{6,0},{1,7},{3,5},{5,3},{7,1},{8,14},{10,12},{12... | collective-permute-start | bytes 245768 | tf_op jit(solution)/shard_map/ppermute | solution.py:342
  39.5 0.0 collective-permute-start.9
  39.5 1.9 %inner_stage.4 = (bf16[2,1024,160]{2,1,0:T(8,128)(2,1)S(1)}, f32[2,1024,256]{2,1,0:T(8,128)S(1)}) custom-call(bf16[1024,128]{1,0:T(8,128)(2,1)S(1)} %get-tuple-element.36.q_ref, bf16[128,1024]{1,0:T(8,128)(2,1)S(1)} %get-tuple-element.37.kt_ref, bf16[4,1024,256]{2,1,0:T(8,128)(2,1)S(1)} %get-tuple-element.38.val_ref, ...), custom_call_target="tpu_custom_call" | custom-call | flops 2000000000 | bytes 4194304 | tf_op jit(solution)/shard_map/inner_stage/pallas_call | solution.py:212
  41.4 0.4 collective-permute-done.10.refs_2_
  41.8 1.0 %collective-permute-done.9.refs_1_ = bf16[2,160,128]{2,1,0:T(8,128)(2,1)S(1)} collective-permute-done((bf16[2,160,128]{2,1,0:T(8,128)(2,1)S(1)}, bf16[2,160,128]{2,1,0:T(8,128)(2,1)S(1)}, u32[]{:S(2)}, u32[]{:S(2)}) %collective-permute-start.9) | collective-permute-done | bytes 81952 | tf_op jit(solution)/shard_map/ppermute | solution.py:342
  42.8 1.1 %outer_stage.2.a_ref = bf16[1024,768]{1,0:T(8,128)(2,1)S(1)} custom-call(bf16[2,160,128]{2,1,0:T(8,128)(2,1)S(1)} %get-tuple-element.33.refs_0_, bf16[2,160,128]{2,1,0:T(8,128)(2,1)S(1)} %collective-permute-done.9.refs_1_, bf16[2,160,128]{2,1,0:T(8,128)(2,1)S(1)} %collective-permute-done.10.refs_2_, bf16[2,1024,160]{2,1,0:T(8,128)(2,1)S(1)} %get-tuple-element.40.refs_3_, ...), custom_call_target="tpu_custom_call" | custom-call | flops 900000000 | bytes 3145728 | tf_op jit(solution)/shard_map/outer_stage/pallas_call | solution.py:255
  43.9 5.3 %collective-permute-start.11 = (bf16[1024,768]{1,0:T(8,128)(2,1)S(1)}, bf16[1024,768]{1,0:T(8,128)(2,1)S(1)}, u32[]{:S(2)}, u32[]{:S(2)}) collective-permute-start(bf16[1024,768]{1,0:T(8,128)(2,1)S(1)} %outer_stage.2.a_ref), channel_id=1, source_target_pairs={{0,1},{1,0},{2,3},{3,2},{4,5},{5,4},{6,7},{7,6},{8,9},{9,8},{10,11... | collective-permute-start | bytes 4718600 | tf_op jit(solution)/shard_map/ppermute | solution.py:424
  49.2 1.2 %collective-permute-start.12 = (bf16[2,160,128]{2,1,0:T(8,128)(2,1)S(1)}, bf16[2,160,128]{2,1,0:T(8,128)(2,1)S(1)}, u32[]{:S(2)}, u32[]{:S(2)}) collective-permute-start(bf16[2,160,128]{2,1,0:T(8,128)(2,1)S(1)} %get-tuple-element.46), channel_id=1, source_target_pairs={{0,4},{2,6},{4,0},{6,2},{1,5},{3,7},{5,1},{7,3},{8,12},{10,14},{12... | collective-permute-start | bytes 245768 | tf_op jit(solution)/shard_map/ppermute | solution.py:342
  50.4 1.9 %inner_stage.7 = (bf16[2,1024,160]{2,1,0:T(8,128)(2,1)S(1)}, f32[2,1024,256]{2,1,0:T(8,128)S(1)}) custom-call(bf16[1024,128]{1,0:T(8,128)(2,1)S(1)} %get-tuple-element.36.q_ref, bf16[128,1024]{1,0:T(8,128)(2,1)S(1)} %get-tuple-element.37.kt_ref, bf16[4,1024,256]{2,1,0:T(8,128)(2,1)S(1)} %get-tuple-element.38.val_ref, ...), custom_call_target="tpu_custom_call" | custom-call | flops 2000000000 | bytes 4194304 | tf_op jit(solution)/shard_map/inner_stage/pallas_call | solution.py:212
  52.3 2.3 %collective-permute-done.12.refs_0_ = bf16[2,160,128]{2,1,0:T(8,128)(2,1)S(1)} collective-permute-done((bf16[2,160,128]{2,1,0:T(8,128)(2,1)S(1)}, bf16[2,160,128]{2,1,0:T(8,128)(2,1)S(1)}, u32[]{:S(2)}, u32[]{:S(2)}) %collective-permute-start.12) | collective-permute-done | bytes 81952 | tf_op jit(solution)/shard_map/ppermute | solution.py:342
  54.6 0.5 outer_stage.3.b_ref
  55.1 1.0 %collective-permute-start.13 = (bf16[1024,256]{1,0:T(8,128)(2,1)S(1)}, bf16[1024,256]{1,0:T(8,128)(2,1)S(1)}, u32[]{:S(2)}, u32[]{:S(2)}) collective-permute-start(bf16[1024,256]{1,0:T(8,128)(2,1)S(1)} %outer_stage.3.b_ref), channel_id=1, source_target_pairs={{0,1},{1,0},{2,3},{3,2},{4,5},{5,4},{6,7},{7,6},{8,9},{9,8},{10,11... | collective-permute-start | bytes 1572872 | tf_op jit(solution)/shard_map/ppermute | solution.py:425
  56.2 2.3 %out_stage.2.rest_0_ = f32[1024,1024]{1,0:T(8,128)S(1)} custom-call(bf16[1024,768]{1,0:T(8,128)(2,1)S(1)} %outer_stage.2.a_ref, bf16[1024,256]{1,0:T(8,128)(2,1)S(1)} %outer_stage.3.b_ref, bf16[2,1024,1024]{2,1,0:T(8,128)(2,1)S(1)} %fetch_stage.1.columns.w_ref), custom_call_target="tpu_custom_call" | custom-call | flops 2000000000 | bytes 8388608 | tf_op jit(solution)/shard_map/out_stage/pallas_call | solution.py:324
  58.5 0.0 collective-permute-done.13.b_ref
  58.5 0.0 collective-permute-done.11.a_ref
  58.5 3.2 %out_stage.3 = bf16[1024,1024]{1,0:T(8,128)(2,1)} custom-call(bf16[1024,768]{1,0:T(8,128)(2,1)S(1)} %collective-permute-done.11.a_ref, bf16[1024,256]{1,0:T(8,128)(2,1)S(1)} %collective-permute-done.13.b_ref, bf16[2,1024,1024]{2,1,0:T(8,128)(2,1)S(1)} %fetch_stage.1.columns.w_ref, f32[1024,1024]{1,0:T(8,128)S(1)} %out_stage.2.rest_0_), custom_call_target="tpu_custom_call" | custom-call | flops 2000000000 | bytes 8388608 | tf_op jit(solution)/shard_map/out_stage/pallas_call | solution.py:324
  (1 shorter events, 0.0 us)
Async XLA Ops:
  0.0 1.0 %copy-start = (bf16[2048,128]{1,0:T(8,128)(2,1)S(1)}, bf16[2048,128]{1,0:T(8,128)(2,1)}, u32[]{:S(2)}) copy-start(bf16[2048,128]{1,0:T(8,128)(2,1)} %wk_hbm.1) | copy-start | bytes 1572868
  1.0 1.0 %copy-start.1 = (bf16[2048,128]{1,0:T(8,128)(2,1)S(1)}, bf16[2048,128]{1,0:T(8,128)(2,1)}, u32[]{:S(2)}) copy-start(bf16[2048,128]{1,0:T(8,128)(2,1)} %wq_hbm.1) | copy-start | bytes 1572868
  2.1 14.0 %copy-start.2 = (f32[8,160]{1,0:T(8,128)S(1)}, f32[8,160]{1,0:T(8,128)}, u32[]{:S(2)}) copy-start(f32[8,160]{1,0:T(8,128)} %constant.2.clone.table_ref) | copy-start | bytes 15364
  10.8 7.2 %collective-permute-start = (bf16[2,160,128]{2,1,0:T(8,128)(2,1)S(1)}, bf16[2,160,128]{2,1,0:T(8,128)(2,1)S(1)}, u32[]{:S(2)}, u32[]{:S(2)}) collective-permute-start(bf16[2,160,128]{2,1,0:T(8,128)(2,1)S(1)} %get-tuple-element.28), channel_id=1, source_target_pairs={{0,4},{2,6},{4,0},{6,2},{1,5},{3,7},{5,1},{7,3},{8,12},{10,14},{12... | collective-permute-start | bytes 245768 | tf_op jit(solution)/shard_map/ppermute | solution.py:342
  15.3 4.1 %collective-permute-start.1 = (bf16[2,160,128]{2,1,0:T(8,128)(2,1)S(1)}, bf16[2,160,128]{2,1,0:T(8,128)(2,1)S(1)}, u32[]{:S(2)}, u32[]{:S(2)}) collective-permute-start(bf16[2,160,128]{2,1,0:T(8,128)(2,1)S(1)} %get-tuple-element.29), channel_id=1, source_target_pairs={{0,2},{2,0},{4,6},{6,4},{1,3},{3,1},{5,7},{7,5},{8,10},{10,8},{12,... | collective-permute-start | bytes 245768 | tf_op jit(solution)/shard_map/ppermute | solution.py:342
  16.1 4.5 %collective-permute-start.2 = (bf16[2,160,128]{2,1,0:T(8,128)(2,1)S(1)}, bf16[2,160,128]{2,1,0:T(8,128)(2,1)S(1)}, u32[]{:S(2)}, u32[]{:S(2)}) collective-permute-start(bf16[2,160,128]{2,1,0:T(8,128)(2,1)S(1)} %get-tuple-element.30), channel_id=1, source_target_pairs={{0,6},{2,4},{4,2},{6,0},{1,7},{3,5},{5,3},{7,1},{8,14},{10,12},{12... | collective-permute-start | bytes 245768 | tf_op jit(solution)/shard_map/ppermute | solution.py:342
  20.6 6.0 %collective-permute-start.3 = (bf16[2,160,128]{2,1,0:T(8,128)(2,1)S(1)}, bf16[2,160,128]{2,1,0:T(8,128)(2,1)S(1)}, u32[]{:S(2)}, u32[]{:S(2)}) collective-permute-start(bf16[2,160,128]{2,1,0:T(8,128)(2,1)S(1)} %shard_map.64.own), channel_id=1, source_target_pairs={{0,16},{8,24},{16,0},{24,8},{1,17},{9,25},{17,1},{25,9},{2,18},{10... | collective-permute-start | bytes 245768 | tf_op jit(solution)/shard_map/ppermute | solution.py:342
  23.6 3.3 %collective-permute-start.4 = (bf16[2,160,128]{2,1,0:T(8,128)(2,1)S(1)}, bf16[2,160,128]{2,1,0:T(8,128)(2,1)S(1)}, u32[]{:S(2)}, u32[]{:S(2)}) collective-permute-start(bf16[2,160,128]{2,1,0:T(8,128)(2,1)S(1)} %shard_map.64.own), channel_id=1, source_target_pairs={{0,8},{8,0},{16,24},{24,16},{1,9},{9,1},{17,25},{25,17},{2,10},{10... | collective-permute-start | bytes 245768 | tf_op jit(solution)/shard_map/ppermute | solution.py:342
  24.0 5.2 %collective-permute-start.5 = (bf16[2,160,128]{2,1,0:T(8,128)(2,1)S(1)}, bf16[2,160,128]{2,1,0:T(8,128)(2,1)S(1)}, u32[]{:S(2)}, u32[]{:S(2)}) collective-permute-start(bf16[2,160,128]{2,1,0:T(8,128)(2,1)S(1)} %shard_map.64.own), channel_id=1, source_target_pairs={{0,24},{8,16},{16,8},{24,0},{1,25},{9,17},{17,9},{25,1},{2,26},{10... | collective-permute-start | bytes 245768 | tf_op jit(solution)/shard_map/ppermute | solution.py:342
  29.3 5.6 %collective-permute-start.6 = (bf16[2,160,128]{2,1,0:T(8,128)(2,1)S(1)}, bf16[2,160,128]{2,1,0:T(8,128)(2,1)S(1)}, u32[]{:S(2)}, u32[]{:S(2)}) collective-permute-start(bf16[2,160,128]{2,1,0:T(8,128)(2,1)S(1)} %get-tuple-element.31.own), channel_id=1, source_target_pairs={{0,64},{32,96},{64,0},{96,32},{1,65},{33,97},{65,1},{97,33},{2,66}... | collective-permute-start | bytes 245768 | tf_op jit(solution)/shard_map/ppermute | solution.py:342
  32.1 3.3 %collective-permute-start.7 = (bf16[2,160,128]{2,1,0:T(8,128)(2,1)S(1)}, bf16[2,160,128]{2,1,0:T(8,128)(2,1)S(1)}, u32[]{:S(2)}, u32[]{:S(2)}) collective-permute-start(bf16[2,160,128]{2,1,0:T(8,128)(2,1)S(1)} %get-tuple-element.31.own), channel_id=1, source_target_pairs={{0,32},{32,0},{64,96},{96,64},{1,33},{33,1},{65,97},{97,65},{2,34}... | collective-permute-start | bytes 245768 | tf_op jit(solution)/shard_map/ppermute | solution.py:342
  32.4 4.5 %collective-permute-start.8 = (bf16[2,160,128]{2,1,0:T(8,128)(2,1)S(1)}, bf16[2,160,128]{2,1,0:T(8,128)(2,1)S(1)}, u32[]{:S(2)}, u32[]{:S(2)}) collective-permute-start(bf16[2,160,128]{2,1,0:T(8,128)(2,1)S(1)} %get-tuple-element.31.own), channel_id=1, source_target_pairs={{0,96},{32,64},{64,32},{96,0},{1,97},{33,65},{65,33},{97,1},{2,98}... | collective-permute-start | bytes 245768 | tf_op jit(solution)/shard_map/ppermute | solution.py:342
  37.2 4.6 %collective-permute-start.10 = (bf16[2,160,128]{2,1,0:T(8,128)(2,1)S(1)}, bf16[2,160,128]{2,1,0:T(8,128)(2,1)S(1)}, u32[]{:S(2)}, u32[]{:S(2)}) collective-permute-start(bf16[2,160,128]{2,1,0:T(8,128)(2,1)S(1)} %get-tuple-element.35), channel_id=1, source_target_pairs={{0,6},{2,4},{4,2},{6,0},{1,7},{3,5},{5,3},{7,1},{8,14},{10,12},{12... | collective-permute-start | bytes 245768 | tf_op jit(solution)/shard_map/ppermute | solution.py:342
  39.5 3.3 %collective-permute-start.9 = (bf16[2,160,128]{2,1,0:T(8,128)(2,1)S(1)}, bf16[2,160,128]{2,1,0:T(8,128)(2,1)S(1)}, u32[]{:S(2)}, u32[]{:S(2)}) collective-permute-start(bf16[2,160,128]{2,1,0:T(8,128)(2,1)S(1)} %get-tuple-element.34), channel_id=1, source_target_pairs={{0,2},{2,0},{4,6},{6,4},{1,3},{3,1},{5,7},{7,5},{8,10},{10,8},{12,... | collective-permute-start | bytes 245768 | tf_op jit(solution)/shard_map/ppermute | solution.py:342
  43.9 14.6 %collective-permute-start.11 = (bf16[1024,768]{1,0:T(8,128)(2,1)S(1)}, bf16[1024,768]{1,0:T(8,128)(2,1)S(1)}, u32[]{:S(2)}, u32[]{:S(2)}) collective-permute-start(bf16[1024,768]{1,0:T(8,128)(2,1)S(1)} %outer_stage.2.a_ref), channel_id=1, source_target_pairs={{0,1},{1,0},{2,3},{3,2},{4,5},{5,4},{6,7},{7,6},{8,9},{9,8},{10,11... | collective-permute-start | bytes 4718600 | tf_op jit(solution)/shard_map/ppermute | solution.py:424
  49.2 5.4 %collective-permute-start.12 = (bf16[2,160,128]{2,1,0:T(8,128)(2,1)S(1)}, bf16[2,160,128]{2,1,0:T(8,128)(2,1)S(1)}, u32[]{:S(2)}, u32[]{:S(2)}) collective-permute-start(bf16[2,160,128]{2,1,0:T(8,128)(2,1)S(1)} %get-tuple-element.46), channel_id=1, source_target_pairs={{0,4},{2,6},{4,0},{6,2},{1,5},{3,7},{5,1},{7,3},{8,12},{10,14},{12... | collective-permute-start | bytes 245768 | tf_op jit(solution)/shard_map/ppermute | solution.py:342
  55.1 3.4 %collective-permute-start.13 = (bf16[1024,256]{1,0:T(8,128)(2,1)S(1)}, bf16[1024,256]{1,0:T(8,128)(2,1)S(1)}, u32[]{:S(2)}, u32[]{:S(2)}) collective-permute-start(bf16[1024,256]{1,0:T(8,128)(2,1)S(1)} %outer_stage.3.b_ref), channel_id=1, source_target_pairs={{0,1},{1,0},{2,3},{3,2},{4,5},{5,4},{6,7},{7,6},{8,9},{9,8},{10,11... | collective-permute-start | bytes 1572872 | tf_op jit(solution)/shard_map/ppermute | solution.py:425
where the time goes:
time: 62.1 us; the launch traced here: 61.9 us
  Pallas kernels  25.9 us (42%)
  starting transfers between devices  22.5 us (36%)
  waiting for transfers between devices  11 us (18%)
  local copies, waits for them, and re-layouts  2.09 us (3%)
    ppermute x12, starting transfers between devices, partner(): return lax.ppermute(x, axis, pairs)  16.2 us
    ppermute x12, waiting for transfers between devices, partner(): return lax.ppermute(x, axis, pairs)  11 us
    pallas_call x1, Pallas kernels, head_stage(): pl.pallas_call(head_kernel, out_shape=[shape((tok, kd), BF16), shape((kd,...  8.73 us
    pallas_call x4, Pallas kernels, inner_stage(): pl.pallas_call(functools.partial(inner_kernel, slot), grid=(1,), out_shap...  7.52 us
    pallas_call x2, Pallas kernels, out_stage(): pl.pallas_call(functools.partial(out_kernel, half), out_shape=jax.ShapeDt...  5.49 us
    ppermute x1, starting transfers between devices, per_device(): other_most = lax.ppermute(most, 'head', swap)  5.29 us
    pallas_call x1, Pallas kernels, fetch_stage(): pl.pallas_call(fetch_kernel, out_shape=jax.ShapeDtypeStruct((2, 1024, 102...  2.21 us
    unnamed x6, local copies, waits for them, and re-layouts  2.09 us
  transfers between devices with their start and end apart: 14, of which 9 were waited for; matrix products, arithmetic and copies ran while one was open for 0% of the time, Pallas kernels for 20%

commit v1 on v0

--- a/solution.py
+++ b/solution.py
@@ -18,6 +18,7 @@
 HEAD_LIMIT, FETCH_LIMIT, OUT_LIMIT = (48 * MIB, 44 * MIB, 20 * MIB)
 SLOTS = (0, 2, 1, 3)
 OUT_STEPS = (0, 1, 3, 2)
+GROUPS = ((0,), (1, 3), (2,))
 F32, BF16 = (jnp.float32, jnp.bfloat16)
 VMEM = pl.BlockSpec(memory_space=pltpu.VMEM)
 SMEM = pl.BlockSpec(memory_space=pltpu.SMEM)
@@ -299,42 +300,53 @@
     )(w_out)
 
 
-def out_kernel(half, a_ref, b_ref, w_ref, *rest):
-    wide = a_ref.shape[1]
-    blocks = a_ref.shape[0] // CHUNK
+def out_kernel(places, last, *refs):
+    count = len(places)
+    groups, (w_ref, *rest) = (refs[:count], refs[count:])
+    tok = groups[0].shape[0]
+    blocks = tok // CHUNK
+    if last:
+        acc, out, stage, sem = rest
+        copies = []
+        for c in range(blocks):
+            rows = pl.ds(c * CHUNK, CHUNK)
+            copies.append(pltpu.make_async_copy(stage.at[rows], out.at[rows], sem.at[c]))
+    else:
+        acc, out = (None, rest[0]) if len(rest) == 1 else rest
     for c in range(blocks):
         rows = slice(c * CHUNK, (c + 1) * CHUNK)
-        part = mm(a_ref[rows], w_ref[half, :wide]) + mm(b_ref[rows], w_ref[half, wide:])
-        if half == 0:
-            rest[0][rows] = part
+        part = None if acc is None else acc[rows]
+        for group, (half, start, width) in zip(groups, places):
+            more = mm(group[rows], w_ref[half, start : start + width])
+            part = more if part is None else part + more
+        if last:
+            stage[rows] = part.astype(BF16)
+            copies[c].start()
         else:
-            acc, out, stage, sem = rest
-            stage[rows] = (part + acc[rows]).astype(BF16)
-            pltpu.make_async_copy(stage.at[rows], out.at[rows], sem.at[c]).start()
-    if half == 1:
-        acc, out, stage, sem = rest
-        for c in range(blocks):
-            rows = slice(c * CHUNK, (c + 1) * CHUNK)
-            pltpu.make_async_copy(stage.at[rows], out.at[rows], sem.at[c]).wait()
-
-
-def out_stage(half, most, rest, columns, acc=None):
-    tok = most.shape[0]
-    first = half == 0
-    return pl.pallas_call(
-        functools.partial(out_kernel, half),
-        out_shape=jax.ShapeDtypeStruct((tok, 1024), F32 if first else BF16),
-        in_specs=[VMEM] * (3 if first else 4),
-        out_specs=VMEM if first else ANY,
-        scratch_shapes=[]
-        if first
-        else [pltpu.VMEM((tok, 1024), BF16), pltpu.SemaphoreType.DMA((tok // CHUNK,))],
+            out[rows] = part
+    if last:
+        for copy in copies:
+            copy.wait()
+
+
+def out_stage(groups, places, columns, acc=None, last=False):
+    tok = groups[0].shape[0]
+    args = [*groups, columns] + ([] if acc is None else [acc])
+    depth = sum(width for _, _, width in places)
+    return pl.pallas_call(
+        functools.partial(out_kernel, places, last),
+        out_shape=jax.ShapeDtypeStruct((tok, 1024), BF16 if last else F32),
+        in_specs=[VMEM] * len(args),
+        out_specs=ANY if last else VMEM,
+        scratch_shapes=[pltpu.VMEM((tok, 1024), BF16), pltpu.SemaphoreType.DMA((tok // CHUNK,))]
+        if last
+        else [],
         compiler_params=pltpu.CompilerParams(vmem_limit_bytes=OUT_LIMIT),
         cost_estimate=pl.CostEstimate(
-            flops=2 * 10**9, bytes_accessed=8 * 2**20, transcendentals=0
+            flops=2 * tok * 1024 * depth, bytes_accessed=2**20, transcendentals=0
         ),
         name="out_stage",
-    )(*([most, rest, columns] + ([] if first else [acc])))
+    )(*args)
 
 
 def partner(x, axis, step):
@@ -404,6 +416,10 @@
 
 
 def per_device(tokens, w_query, w_key, w_value, w_out):
+    tokens, w_query, w_key, w_value, w_out = (
+        pltpu.with_memory_space_constraint(x, pltpu.HBM)
+        for x in (tokens, w_query, w_key, w_value, w_out)
+    )
     table = jnp.asarray(feature_tables())
     q, kt, val, local, *states = head_stage(tokens, w_key, w_query, w_value)
     columns = fetch_stage(w_out)
@@ -419,12 +435,19 @@
             [inner[step][1] for step in steps],
         )
 
-    most, rest = (outer(OUT_STEPS[:3]), outer(OUT_STEPS[3:]))
-    swap = [(0, 1), (1, 0)]
-    other_most = lax.ppermute(most, "head", swap)
-    other_rest = lax.ppermute(rest, "head", swap)
-    acc = out_stage(0, most, rest, columns)
-    return out_stage(1, other_most, other_rest, columns, acc)
+    places, start = ([], 0)
+    for steps in GROUPS:
+        places.append((start, 256 * len(steps)))
+        start += 256 * len(steps)
+    own, other = ([], [])
+    for steps in GROUPS:
+        own.append(outer(steps))
+        other.append(lax.ppermute(own[-1], "head", [(0, 1), (1, 0)]))
+    mine = [(0, *place) for place in places]
+    theirs = [(1, *place) for place in places]
+    acc = out_stage(own[:1], mine[:1], columns)
+    acc = out_stage([*own[1:], other[0]], (*mine[1:], theirs[0]), columns, acc)
+    return out_stage(other[1:], theirs[1:], columns, acc, last=True)
 
 
 def solution(mesh):

time: 62.1 us -> 63.2 us (1.018)
  local copies, waits for them, and re-layouts: 2.09 us -> 0.01 us
  Pallas kernels: 25.9 us -> 27.5 us
  waiting for transfers between devices: 11 us -> 12.3 us
    unnamed x6 -> x2, local copies, waits for them, and re-layouts: 2.09 us -> 0.01 us
    ppermute x12, waiting for transfers between devices: 11 us -> 12.2 us  [partner(): return lax.ppermute(x, axis, pairs)]
    pallas_call x1, Pallas kernels: 8.73 us -> 9.94 us  [head_stage(): pl.pallas_call(head_kernel, out_shape=[shape((tok, kd), BF16), shape((kd,...]
    ppermute x2 -> x3, starting transfers between devices: 6.33 us -> 7.06 us  [per_device(): other.append(lax.ppermute(own[-1], 'head', [(0, 1), (1, 0)]))]
    pallas_call x2 -> x3, Pallas kernels: 1.58 us -> 1.81 us  [outer_stage(): pl.pallas_call(functools.partial(outer_kernel, count), out_shape=jax.Shap...]
    pallas_call x2 -> x3, Pallas kernels: 5.49 us -> 5.67 us  [out_stage(): pl.pallas_call(functools.partial(out_kernel, places, last), out_shape=jax...]
  transfers between devices with their start and end apart: 14 -> 15, of which waited for: 9 -> 9; matrix products, arithmetic and copies ran while one was open for 0% -> 0% of each run, Pallas kernels for 20% -> 22%
where the time goes in v1:
time: 63.2 us; the launch traced here: 63.1 us
  Pallas kernels  27.5 us (44%)
  starting transfers between devices  23.1 us (37%)
  waiting for transfers between devices  12.3 us (19%)
    ppermute x12, starting transfers between devices, partner(): return lax.ppermute(x, axis, pairs)  16 us
    ppermute x12, waiting for transfers between devices, partner(): return lax.ppermute(x, axis, pairs)  12.2 us
    pallas_call x1, Pallas kernels, head_stage(): pl.pallas_call(head_kernel, out_shape=[shape((tok, kd), BF16), shape((kd,...  9.94 us
    pallas_call x4, Pallas kernels, inner_stage(): pl.pallas_call(functools.partial(inner_kernel, slot), grid=(1,), out_shap...  7.43 us
    ppermute x3, starting transfers between devices, per_device(): other.append(lax.ppermute(own[-1], 'head', [(0, 1), (1, 0)]))  7.06 us
    pallas_call x3, Pallas kernels, out_stage(): pl.pallas_call(functools.partial(out_kernel, places, last), out_shape=jax...  5.67 us
    pallas_call x1, Pallas kernels, fetch_stage(): pl.pallas_call(fetch_kernel, out_shape=jax.ShapeDtypeStruct((2, 1024, 102...  2.21 us
    pallas_call x3, Pallas kernels, outer_stage(): pl.pallas_call(functools.partial(outer_kernel, count), out_shape=jax.Shap...  1.81 us
  transfers between devices with their start and end apart: 15, of which 9 were waited for; matrix products, arithmetic and copies ran while one was open for 0% of the time, Pallas kernels for 22%

profile of v1, /device:TPU:1, one launch (start us, length us, event | category | flops | bytes accessed | tf_op | source)
XLA Modules:
  0.0 63.1 jit_solution(5809821387670042667)
XLA Ops:
  0.0 9.9 %head_stage.1 = (bf16[1024,128]{1,0:T(8,128)(2,1)S(1)}, bf16[128,1024]{1,0:T(8,128)(2,1)S(1)}, bf16[4,1024,256]{2,1,0:T(8,128)(2,1)S(1)}, bf16[4,2,3,160,256]{4,...) custom-call(bf16[1024,2048]{1,0:T(8,128)(2,1)} %x_hbm.1, ...), custom_call_target="tpu_custom_call" | custom-call | flops 6000000000 | bytes 12582912 | tf_op jit(solution)/shard_map/head_stage/pallas_call | solution.py:149
  10.0 4.5 %collective-permute-start = (bf16[2,160,128]{2,1,0:T(8,128)(2,1)S(1)}, bf16[2,160,128]{2,1,0:T(8,128)(2,1)S(1)}, u32[]{:S(2)}, u32[]{:S(2)}) collective-permute-start(bf16[2,160,128]{2,1,0:T(8,128)(2,1)S(1)} %get-tuple-element.28), channel_id=1, source_target_pairs={{0,4},{2,6},{4,0},{6,2},{1,5},{3,7},{5,1},{7,3},{8,12},{10,14},{12... | collective-permute-start | bytes 245768 | tf_op jit(solution)/shard_map/ppermute | solution.py:354
  14.4 0.7 %collective-permute-start.1 = (bf16[2,160,128]{2,1,0:T(8,128)(2,1)S(1)}, bf16[2,160,128]{2,1,0:T(8,128)(2,1)S(1)}, u32[]{:S(2)}, u32[]{:S(2)}) collective-permute-start(bf16[2,160,128]{2,1,0:T(8,128)(2,1)S(1)} %get-tuple-element.29), channel_id=1, source_target_pairs={{0,2},{2,0},{4,6},{6,4},{1,3},{3,1},{5,7},{7,5},{8,10},{10,8},{12,... | collective-permute-start | bytes 245768 | tf_op jit(solution)/shard_map/ppermute | solution.py:354
  15.2 0.0 collective-permute-start.2
  15.2 1.4 %collective-permute-done.p1 = bf16[2,160,128]{2,1,0:T(8,128)(2,1)S(1)} collective-permute-done((bf16[2,160,128]{2,1,0:T(8,128)(2,1)S(1)}, bf16[2,160,128]{2,1,0:T(8,128)(2,1)S(1)}, u32[]{:S(2)}, u32[]{:S(2)}) %collective-permute-start) | collective-permute-done | bytes 81952 | tf_op jit(solution)/shard_map/ppermute | solution.py:354
  16.6 1.9 %collective-permute-done.1.p2 = bf16[2,160,128]{2,1,0:T(8,128)(2,1)S(1)} collective-permute-done((bf16[2,160,128]{2,1,0:T(8,128)(2,1)S(1)}, bf16[2,160,128]{2,1,0:T(8,128)(2,1)S(1)}, u32[]{:S(2)}, u32[]{:S(2)}) %collective-permute-start.1) | collective-permute-done | bytes 81952 | tf_op jit(solution)/shard_map/ppermute | solution.py:354
  18.5 1.2 %collective-permute-done.2.p3 = bf16[2,160,128]{2,1,0:T(8,128)(2,1)S(1)} collective-permute-done((bf16[2,160,128]{2,1,0:T(8,128)(2,1)S(1)}, bf16[2,160,128]{2,1,0:T(8,128)(2,1)S(1)}, u32[]{:S(2)}, u32[]{:S(2)}) %collective-permute-start.2) | collective-permute-done | bytes 81952 | tf_op jit(solution)/shard_map/ppermute | solution.py:354
  19.7 3.0 %collective-permute-start.3 = (bf16[2,160,128]{2,1,0:T(8,128)(2,1)S(1)}, bf16[2,160,128]{2,1,0:T(8,128)(2,1)S(1)}, u32[]{:S(2)}, u32[]{:S(2)}) collective-permute-start(bf16[2,160,128]{2,1,0:T(8,128)(2,1)S(1)} %shard_map.64.own), channel_id=1, source_target_pairs={{0,16},{8,24},{16,0},{24,8},{1,17},{9,25},{17,1},{25,9},{2,18},{10... | collective-permute-start | bytes 245768 | tf_op jit(solution)/shard_map/ppermute | solution.py:354
  22.7 0.4 collective-permute-start.4
  23.1 0.4 collective-permute-start.5
  23.5 2.2 %fetch_stage.1.columns.refs_1_.refs_3_.refs_2_ = bf16[2,1024,1024]{2,1,0:T(8,128)(2,1)S(1)} custom-call(bf16[2048,2048]{1,0:T(8,128)(2,1)} %w_hbm.1), custom_call_target="tpu_custom_call" | custom-call | flops 1000000000 | bytes 8388608 | tf_op jit(solution)/shard_map/fetch_stage/pallas_call | solution.py:289
  25.7 0.0 copy-start
  25.7 0.0 collective-permute-done.3.g0
  25.7 0.3 collective-permute-done.4.g1
  26.0 2.3 %collective-permute-done.5.g2 = bf16[2,160,128]{2,1,0:T(8,128)(2,1)S(1)} collective-permute-done((bf16[2,160,128]{2,1,0:T(8,128)(2,1)S(1)}, bf16[2,160,128]{2,1,0:T(8,128)(2,1)S(1)}, u32[]{:S(2)}, u32[]{:S(2)}) %collective-permute-start.5) | collective-permute-done | bytes 81952 | tf_op jit(solution)/shard_map/ppermute | solution.py:354
  28.3 0.1 shard_map.65
  28.4 2.8 %collective-permute-start.6 = (bf16[2,160,128]{2,1,0:T(8,128)(2,1)S(1)}, bf16[2,160,128]{2,1,0:T(8,128)(2,1)S(1)}, u32[]{:S(2)}, u32[]{:S(2)}) collective-permute-start(bf16[2,160,128]{2,1,0:T(8,128)(2,1)S(1)} %get-tuple-element.31.own), channel_id=1, source_target_pairs={{0,64},{32,96},{64,0},{96,32},{1,65},{33,97},{65,1},{97,33},{2,66}... | collective-permute-start | bytes 245768 | tf_op jit(solution)/shard_map/ppermute | solution.py:354
  31.2 0.3 collective-permute-start.7
  31.6 0.5 collective-permute-start.8
  32.1 0.0 copy-done
  32.1 1.9 %inner_stage.4 = (bf16[2,1024,160]{2,1,0:T(8,128)(2,1)S(1)}, f32[2,1024,256]{2,1,0:T(8,128)S(1)}) custom-call(bf16[1024,128]{1,0:T(8,128)(2,1)S(1)} %get-tuple-element.35.q_ref, bf16[128,1024]{1,0:T(8,128)(2,1)S(1)} %get-tuple-element.36.kt_ref, bf16[4,1024,256]{2,1,0:T(8,128)(2,1)S(1)} %get-tuple-element.37.val_ref, ...), custom_call_target="tpu_custom_call" | custom-call | flops 2000000000 | bytes 4194304 | tf_op jit(solution)/shard_map/inner_stage/pallas_call | solution.py:213
  34.0 0.0 collective-permute-done.6.g0
  34.0 0.6 collective-permute-done.7.g1
  34.5 1.5 %collective-permute-done.8.g2 = bf16[2,160,128]{2,1,0:T(8,128)(2,1)S(1)} collective-permute-done((bf16[2,160,128]{2,1,0:T(8,128)(2,1)S(1)}, bf16[2,160,128]{2,1,0:T(8,128)(2,1)S(1)}, u32[]{:S(2)}, u32[]{:S(2)}) %collective-permute-start.8) | collective-permute-done | bytes 81952 | tf_op jit(solution)/shard_map/ppermute | solution.py:354
  36.1 0.3 shard_map.66
  36.3 1.0 %collective-permute-start.9 = (bf16[2,160,128]{2,1,0:T(8,128)(2,1)S(1)}, bf16[2,160,128]{2,1,0:T(8,128)(2,1)S(1)}, u32[]{:S(2)}, u32[]{:S(2)}) collective-permute-start(bf16[2,160,128]{2,1,0:T(8,128)(2,1)S(1)} %get-tuple-element.33), channel_id=1, source_target_pairs={{0,2},{2,0},{4,6},{6,4},{1,3},{3,1},{5,7},{7,5},{8,10},{10,8},{12,... | collective-permute-start | bytes 245768 | tf_op jit(solution)/shard_map/ppermute | solution.py:354
  37.3 1.7 %collective-permute-start.10 = (bf16[2,160,128]{2,1,0:T(8,128)(2,1)S(1)}, bf16[2,160,128]{2,1,0:T(8,128)(2,1)S(1)}, u32[]{:S(2)}, u32[]{:S(2)}) collective-permute-start(bf16[2,160,128]{2,1,0:T(8,128)(2,1)S(1)} %get-tuple-element.34), channel_id=1, source_target_pairs={{0,6},{2,4},{4,2},{6,0},{1,7},{3,5},{5,3},{7,1},{8,14},{10,12},{12... | collective-permute-start | bytes 245768 | tf_op jit(solution)/shard_map/ppermute | solution.py:354
  38.9 1.9 %inner_stage.5 = (bf16[2,1024,160]{2,1,0:T(8,128)(2,1)S(1)}, f32[2,1024,256]{2,1,0:T(8,128)S(1)}) custom-call(bf16[1024,128]{1,0:T(8,128)(2,1)S(1)} %get-tuple-element.35.q_ref, bf16[128,1024]{1,0:T(8,128)(2,1)S(1)} %get-tuple-element.36.kt_ref, bf16[4,1024,256]{2,1,0:T(8,128)(2,1)S(1)} %get-tuple-element.37.val_ref, ...), custom_call_target="tpu_custom_call" | custom-call | flops 2000000000 | bytes 4194304 | tf_op jit(solution)/shard_map/inner_stage/pallas_call | solution.py:213
  40.8 0.0 collective-permute-done.9.refs_0_
  40.8 1.0 %collective-permute-done.10.refs_1_ = bf16[2,160,128]{2,1,0:T(8,128)(2,1)S(1)} collective-permute-done((bf16[2,160,128]{2,1,0:T(8,128)(2,1)S(1)}, bf16[2,160,128]{2,1,0:T(8,128)(2,1)S(1)}, u32[]{:S(2)}, u32[]{:S(2)}) %collective-permute-start.10) | collective-permute-done | bytes 81952 | tf_op jit(solution)/shard_map/ppermute | solution.py:354
  41.8 0.8 %outer_stage.3.refs_0_ = bf16[1024,512]{1,0:T(8,128)(2,1)S(1)} custom-call(bf16[2,160,128]{2,1,0:T(8,128)(2,1)S(1)} %collective-permute-done.9.refs_0_, bf16[2,160,128]{2,1,0:T(8,128)(2,1)S(1)} %collective-permute-done.10.refs_1_, bf16[2,1024,160]{2,1,0:T(8,128)(2,1)S(1)} %get-tuple-element.39.refs_2_, bf16[2,1024,160]{2,1,0:T(8,128)(2,1)S(1)} %get-tuple-element.40.refs_3_, ...), custom_call_target="tpu_custom_call" | custom-call | flops 600000000 | bytes 2097152 | tf_op jit(solution)/shard_map/outer_stage/pallas_call | solution.py:256
  42.6 5.7 %collective-permute-start.11 = (bf16[1024,512]{1,0:T(8,128)(2,1)S(1)}, bf16[1024,512]{1,0:T(8,128)(2,1)S(1)}, u32[]{:S(2)}, u32[]{:S(2)}) collective-permute-start(bf16[1024,512]{1,0:T(8,128)(2,1)S(1)} %outer_stage.3.refs_0_), channel_id=1, source_target_pairs={{0,1},{1,0},{2,3},{3,2},{4,5},{5,4},{6,7},{7,6},{8,9},{9,8},{10,11... | collective-permute-start | bytes 3145736 | tf_op jit(solution)/shard_map/ppermute | solution.py:445
  48.3 1.9 %inner_stage.7 = (bf16[2,1024,160]{2,1,0:T(8,128)(2,1)S(1)}, f32[2,1024,256]{2,1,0:T(8,128)S(1)}) custom-call(bf16[1024,128]{1,0:T(8,128)(2,1)S(1)} %get-tuple-element.35.q_ref, bf16[128,1024]{1,0:T(8,128)(2,1)S(1)} %get-tuple-element.36.kt_ref, bf16[4,1024,256]{2,1,0:T(8,128)(2,1)S(1)} %get-tuple-element.37.val_ref, ...), custom_call_target="tpu_custom_call" | custom-call | flops 2000000000 | bytes 4194304 | tf_op jit(solution)/shard_map/inner_stage/pallas_call | solution.py:213
  50.2 0.7 %collective-permute-start.12 = (bf16[2,160,128]{2,1,0:T(8,128)(2,1)S(1)}, bf16[2,160,128]{2,1,0:T(8,128)(2,1)S(1)}, u32[]{:S(2)}, u32[]{:S(2)}) collective-permute-start(bf16[2,160,128]{2,1,0:T(8,128)(2,1)S(1)} %get-tuple-element.43), channel_id=1, source_target_pairs={{0,4},{2,6},{4,0},{6,2},{1,5},{3,7},{5,1},{7,3},{8,12},{10,14},{12... | collective-permute-start | bytes 245768 | tf_op jit(solution)/shard_map/ppermute | solution.py:354
  50.9 0.5 outer_stage.5.refs_0_
  51.4 0.4 collective-permute-start.14
  51.8 1.9 %inner_stage.6 = (bf16[2,1024,160]{2,1,0:T(8,128)(2,1)S(1)}, f32[2,1024,256]{2,1,0:T(8,128)S(1)}) custom-call(bf16[1024,128]{1,0:T(8,128)(2,1)S(1)} %get-tuple-element.35.q_ref, bf16[128,1024]{1,0:T(8,128)(2,1)S(1)} %get-tuple-element.36.kt_ref, bf16[4,1024,256]{2,1,0:T(8,128)(2,1)S(1)} %get-tuple-element.37.val_ref, ...), custom_call_target="tpu_custom_call" | custom-call | flops 2000000000 | bytes 4194304 | tf_op jit(solution)/shard_map/inner_stage/pallas_call | solution.py:213
  53.7 2.1 %collective-permute-done.12.refs_0_ = bf16[2,160,128]{2,1,0:T(8,128)(2,1)S(1)} collective-permute-done((bf16[2,160,128]{2,1,0:T(8,128)(2,1)S(1)}, bf16[2,160,128]{2,1,0:T(8,128)(2,1)S(1)}, u32[]{:S(2)}, u32[]{:S(2)}) %collective-permute-start.12) | collective-permute-done | bytes 81952 | tf_op jit(solution)/shard_map/ppermute | solution.py:354
  55.8 0.5 outer_stage.4.refs_1_
  56.3 1.0 %collective-permute-start.13 = (bf16[1024,256]{1,0:T(8,128)(2,1)S(1)}, bf16[1024,256]{1,0:T(8,128)(2,1)S(1)}, u32[]{:S(2)}, u32[]{:S(2)}) collective-permute-start(bf16[1024,256]{1,0:T(8,128)(2,1)S(1)} %outer_stage.4.refs_1_), channel_id=1, source_target_pairs={{0,1},{1,0},{2,3},{3,2},{4,5},{5,4},{6,7},{7,6},{8,9},{9,8},{10,11... | collective-permute-start | bytes 1572872 | tf_op jit(solution)/shard_map/ppermute | solution.py:445
  57.2 0.7 %out_stage.3.refs_4_ = f32[1024,1024]{1,0:T(8,128)S(1)} custom-call(bf16[1024,256]{1,0:T(8,128)(2,1)S(1)} %outer_stage.5.refs_0_, bf16[2,1024,1024]{2,1,0:T(8,128)(2,1)S(1)} %fetch_stage.1.columns.refs_1_.refs_3_.refs_2_), custom_call_target="tpu_custom_call" | custom-call | flops 536870912 | bytes 1048576 | tf_op jit(solution)/shard_map/out_stage/pallas_call | solution.py:336
  57.9 0.0 collective-permute-done.14.refs_2_
  58.0 2.3 %out_stage.4.refs_3_ = f32[1024,1024]{1,0:T(8,128)S(1)} custom-call(bf16[1024,512]{1,0:T(8,128)(2,1)S(1)} %outer_stage.3.refs_0_, bf16[1024,256]{1,0:T(8,128)(2,1)S(1)} %outer_stage.4.refs_1_, bf16[1024,256]{1,0:T(8,128)(2,1)S(1)} %collective-permute-done.14.refs_2_, bf16[2,1024,1024]{2,1,0:T(8,128)(2,1)S(1)} %fetch_stage.1.columns.refs_1_.refs_3_.refs_2_, ...), custom_call_target="tpu_custom_call" | custom-call | flops 2147483648 | bytes 1048576 | tf_op jit(solution)/shard_map/out_stage/pallas_call | solution.py:336
  60.3 0.0 collective-permute-done.13.refs_1_
  60.3 0.0 collective-permute-done.11.refs_0_
  60.3 2.6 %out_stage.5 = bf16[1024,1024]{1,0:T(8,128)(2,1)} custom-call(bf16[1024,512]{1,0:T(8,128)(2,1)S(1)} %collective-permute-done.11.refs_0_, bf16[1024,256]{1,0:T(8,128)(2,1)S(1)} %collective-permute-done.13.refs_1_, bf16[2,1024,1024]{2,1,0:T(8,128)(2,1)S(1)} %fetch_stage.1.columns.refs_1_.refs_3_.refs_2_, f32[1024,1024]{1,0:T(8,128)S(1)} %out_stage.4.refs_3_), custom_call_target="tpu_custom_call" | custom-call | flops 1610612736 | bytes 1048576 | tf_op jit(solution)/shard_map/out_stage/pallas_call | solution.py:336
  (1 shorter events, 0.0 us)
Async XLA Ops:
  10.0 6.6 %collective-permute-start = (bf16[2,160,128]{2,1,0:T(8,128)(2,1)S(1)}, bf16[2,160,128]{2,1,0:T(8,128)(2,1)S(1)}, u32[]{:S(2)}, u32[]{:S(2)}) collective-permute-start(bf16[2,160,128]{2,1,0:T(8,128)(2,1)S(1)} %get-tuple-element.28), channel_id=1, source_target_pairs={{0,4},{2,6},{4,0},{6,2},{1,5},{3,7},{5,1},{7,3},{8,12},{10,14},{12... | collective-permute-start | bytes 245768 | tf_op jit(solution)/shard_map/ppermute | solution.py:354
  14.4 4.1 %collective-permute-start.1 = (bf16[2,160,128]{2,1,0:T(8,128)(2,1)S(1)}, bf16[2,160,128]{2,1,0:T(8,128)(2,1)S(1)}, u32[]{:S(2)}, u32[]{:S(2)}) collective-permute-start(bf16[2,160,128]{2,1,0:T(8,128)(2,1)S(1)} %get-tuple-element.29), channel_id=1, source_target_pairs={{0,2},{2,0},{4,6},{6,4},{1,3},{3,1},{5,7},{7,5},{8,10},{10,8},{12,... | collective-permute-start | bytes 245768 | tf_op jit(solution)/shard_map/ppermute | solution.py:354
  15.2 4.5 %collective-permute-start.2 = (bf16[2,160,128]{2,1,0:T(8,128)(2,1)S(1)}, bf16[2,160,128]{2,1,0:T(8,128)(2,1)S(1)}, u32[]{:S(2)}, u32[]{:S(2)}) collective-permute-start(bf16[2,160,128]{2,1,0:T(8,128)(2,1)S(1)} %get-tuple-element.30), channel_id=1, source_target_pairs={{0,6},{2,4},{4,2},{6,0},{1,7},{3,5},{5,3},{7,1},{8,14},{10,12},{12... | collective-permute-start | bytes 245768 | tf_op jit(solution)/shard_map/ppermute | solution.py:354
  19.7 6.0 %collective-permute-start.3 = (bf16[2,160,128]{2,1,0:T(8,128)(2,1)S(1)}, bf16[2,160,128]{2,1,0:T(8,128)(2,1)S(1)}, u32[]{:S(2)}, u32[]{:S(2)}) collective-permute-start(bf16[2,160,128]{2,1,0:T(8,128)(2,1)S(1)} %shard_map.64.own), channel_id=1, source_target_pairs={{0,16},{8,24},{16,0},{24,8},{1,17},{9,25},{17,1},{25,9},{2,18},{10... | collective-permute-start | bytes 245768 | tf_op jit(solution)/shard_map/ppermute | solution.py:354
  22.7 3.3 %collective-permute-start.4 = (bf16[2,160,128]{2,1,0:T(8,128)(2,1)S(1)}, bf16[2,160,128]{2,1,0:T(8,128)(2,1)S(1)}, u32[]{:S(2)}, u32[]{:S(2)}) collective-permute-start(bf16[2,160,128]{2,1,0:T(8,128)(2,1)S(1)} %shard_map.64.own), channel_id=1, source_target_pairs={{0,8},{8,0},{16,24},{24,16},{1,9},{9,1},{17,25},{25,17},{2,10},{10... | collective-permute-start | bytes 245768 | tf_op jit(solution)/shard_map/ppermute | solution.py:354
  23.1 5.2 %collective-permute-start.5 = (bf16[2,160,128]{2,1,0:T(8,128)(2,1)S(1)}, bf16[2,160,128]{2,1,0:T(8,128)(2,1)S(1)}, u32[]{:S(2)}, u32[]{:S(2)}) collective-permute-start(bf16[2,160,128]{2,1,0:T(8,128)(2,1)S(1)} %shard_map.64.own), channel_id=1, source_target_pairs={{0,24},{8,16},{16,8},{24,0},{1,25},{9,17},{17,9},{25,1},{2,26},{10... | collective-permute-start | bytes 245768 | tf_op jit(solution)/shard_map/ppermute | solution.py:354
  25.7 6.4 %copy-start = (f32[8,160]{1,0:T(8,128)S(1)}, f32[8,160]{1,0:T(8,128)}, u32[]{:S(2)}) copy-start(f32[8,160]{1,0:T(8,128)} %constant.2.clone.table_ref) | copy-start | bytes 15364
  28.4 5.6 %collective-permute-start.6 = (bf16[2,160,128]{2,1,0:T(8,128)(2,1)S(1)}, bf16[2,160,128]{2,1,0:T(8,128)(2,1)S(1)}, u32[]{:S(2)}, u32[]{:S(2)}) collective-permute-start(bf16[2,160,128]{2,1,0:T(8,128)(2,1)S(1)} %get-tuple-element.31.own), channel_id=1, source_target_pairs={{0,64},{32,96},{64,0},{96,32},{1,65},{33,97},{65,1},{97,33},{2,66}... | collective-permute-start | bytes 245768 | tf_op jit(solution)/shard_map/ppermute | solution.py:354
  31.2 3.3 %collective-permute-start.7 = (bf16[2,160,128]{2,1,0:T(8,128)(2,1)S(1)}, bf16[2,160,128]{2,1,0:T(8,128)(2,1)S(1)}, u32[]{:S(2)}, u32[]{:S(2)}) collective-permute-start(bf16[2,160,128]{2,1,0:T(8,128)(2,1)S(1)} %get-tuple-element.31.own), channel_id=1, source_target_pairs={{0,32},{32,0},{64,96},{96,64},{1,33},{33,1},{65,97},{97,65},{2,34}... | collective-permute-start | bytes 245768 | tf_op jit(solution)/shard_map/ppermute | solution.py:354
  31.6 4.5 %collective-permute-start.8 = (bf16[2,160,128]{2,1,0:T(8,128)(2,1)S(1)}, bf16[2,160,128]{2,1,0:T(8,128)(2,1)S(1)}, u32[]{:S(2)}, u32[]{:S(2)}) collective-permute-start(bf16[2,160,128]{2,1,0:T(8,128)(2,1)S(1)} %get-tuple-element.31.own), channel_id=1, source_target_pairs={{0,96},{32,64},{64,32},{96,0},{1,97},{33,65},{65,33},{97,1},{2,98}... | collective-permute-start | bytes 245768 | tf_op jit(solution)/shard_map/ppermute | solution.py:354
  36.3 4.5 %collective-permute-start.9 = (bf16[2,160,128]{2,1,0:T(8,128)(2,1)S(1)}, bf16[2,160,128]{2,1,0:T(8,128)(2,1)S(1)}, u32[]{:S(2)}, u32[]{:S(2)}) collective-permute-start(bf16[2,160,128]{2,1,0:T(8,128)(2,1)S(1)} %get-tuple-element.33), channel_id=1, source_target_pairs={{0,2},{2,0},{4,6},{6,4},{1,3},{3,1},{5,7},{7,5},{8,10},{10,8},{12,... | collective-permute-start | bytes 245768 | tf_op jit(solution)/shard_map/ppermute | solution.py:354
  37.3 4.5 %collective-permute-start.10 = (bf16[2,160,128]{2,1,0:T(8,128)(2,1)S(1)}, bf16[2,160,128]{2,1,0:T(8,128)(2,1)S(1)}, u32[]{:S(2)}, u32[]{:S(2)}) collective-permute-start(bf16[2,160,128]{2,1,0:T(8,128)(2,1)S(1)} %get-tuple-element.34), channel_id=1, source_target_pairs={{0,6},{2,4},{4,2},{6,0},{1,7},{3,5},{5,3},{7,1},{8,14},{10,12},{12... | collective-permute-start | bytes 245768 | tf_op jit(solution)/shard_map/ppermute | solution.py:354
  42.6 17.7 %collective-permute-start.11 = (bf16[1024,512]{1,0:T(8,128)(2,1)S(1)}, bf16[1024,512]{1,0:T(8,128)(2,1)S(1)}, u32[]{:S(2)}, u32[]{:S(2)}) collective-permute-start(bf16[1024,512]{1,0:T(8,128)(2,1)S(1)} %outer_stage.3.refs_0_), channel_id=1, source_target_pairs={{0,1},{1,0},{2,3},{3,2},{4,5},{5,4},{6,7},{7,6},{8,9},{9,8},{10,11... | collective-permute-start | bytes 3145736 | tf_op jit(solution)/shard_map/ppermute | solution.py:445
  50.2 5.6 %collective-permute-start.12 = (bf16[2,160,128]{2,1,0:T(8,128)(2,1)S(1)}, bf16[2,160,128]{2,1,0:T(8,128)(2,1)S(1)}, u32[]{:S(2)}, u32[]{:S(2)}) collective-permute-start(bf16[2,160,128]{2,1,0:T(8,128)(2,1)S(1)} %get-tuple-element.43), channel_id=1, source_target_pairs={{0,4},{2,6},{4,0},{6,2},{1,5},{3,7},{5,1},{7,3},{8,12},{10,14},{12... | collective-permute-start | bytes 245768 | tf_op jit(solution)/shard_map/ppermute | solution.py:354
  51.4 6.5 %collective-permute-start.14 = (bf16[1024,256]{1,0:T(8,128)(2,1)S(1)}, bf16[1024,256]{1,0:T(8,128)(2,1)S(1)}, u32[]{:S(2)}, u32[]{:S(2)}) collective-permute-start(bf16[1024,256]{1,0:T(8,128)(2,1)S(1)} %outer_stage.5.refs_0_), channel_id=1, source_target_pairs={{0,1},{1,0},{2,3},{3,2},{4,5},{5,4},{6,7},{7,6},{8,9},{9,8},{10,11... | collective-permute-start | bytes 1572872 | tf_op jit(solution)/shard_map/ppermute | solution.py:445
  56.3 4.0 %collective-permute-start.13 = (bf16[1024,256]{1,0:T(8,128)(2,1)S(1)}, bf16[1024,256]{1,0:T(8,128)(2,1)S(1)}, u32[]{:S(2)}, u32[]{:S(2)}) collective-permute-start(bf16[1024,256]{1,0:T(8,128)(2,1)S(1)} %outer_stage.4.refs_1_), channel_id=1, source_target_pairs={{0,1},{1,0},{2,3},{3,2},{4,5},{5,4},{6,7},{7,6},{8,9},{9,8},{10,11... | collective-permute-start | bytes 1572872 | tf_op jit(solution)/shard_map/ppermute | solution.py:445

commit v2 on v1

--- a/solution.py
+++ b/solution.py
@@ -17,8 +17,8 @@
 MIB = 2**20
 HEAD_LIMIT, FETCH_LIMIT, OUT_LIMIT = (48 * MIB, 44 * MIB, 20 * MIB)
 SLOTS = (0, 2, 1, 3)
-OUT_STEPS = (0, 1, 3, 2)
-GROUPS = ((0,), (1, 3), (2,))
+OUT_STEPS = (0, 2, 1, 3)
+GROUPS = ((0,), (2, 1), (3,))
 F32, BF16 = (jnp.float32, jnp.bfloat16)
 VMEM = pl.BlockSpec(memory_space=pltpu.VMEM)
 SMEM = pl.BlockSpec(memory_space=pltpu.SMEM)
@@ -175,7 +175,7 @@
     )(tokens, w_key, w_query, w_value)
 
 
-def inner_kernel(slot, q_ref, kt_ref, val_ref, local_ref, table_ref, feat_out, part_out):
+def inner_kernel(slot, h, q_ref, kt_ref, val_ref, local_ref, table_ref, feat_out, part_out):
     tok = q_ref.shape[0]
     ones = jnp.ones((CHUNK, 128), BF16)
     below = lax.broadcasted_iota(jnp.int32, (CHUNK, CHUNK), 0) >= lax.broadcasted_iota(
@@ -185,58 +185,44 @@
     add_first, add_second = (table_ref[3:4], table_ref[4:5])
     entry = lax.broadcasted_iota(jnp.int32, (128, ROWS), 0).astype(F32)
     lane = lax.broadcasted_iota(jnp.int32, (CHUNK, 128), 1)
-    for h in range(2):
-        at = (quarter_of(SLOTS[slot]) * 2 + h) * 16
-        base = at.astype(F32)
-        pick_first = jnp.where((entry == first + base) & (first >= 0), 1.0, 0.0).astype(BF16)
-        pick_second = jnp.where((entry == second + base) & (second >= 0), scale, 0.0).astype(BF16)
-        mine = (lane >= at) & (lane < at + 16)
-        for c in range(tok // CHUNK):
-            rows = slice(c * CHUNK, (c + 1) * CHUNK)
-            q = q_ref[rows]
-            feat = (mm(q, pick_first) + add_first) * (mm(q, pick_second) + add_second)
-            feat = feat.astype(BF16)
-            feat_out[h, rows] = feat
-            own = jnp.where(mine, q.astype(F32) * 0.25, 0.0).astype(BF16)
-            s = mm(own, kt_ref[:, rows])
-            taylor = jnp.where(below, (0.5 * s + 1.0) * s + 1.0, 0.0).astype(BF16)
-            right = jnp.concatenate([val_ref[0, rows, h * 128 : (h + 1) * 128], ones], axis=1)
-            part = mm(taylor, right)
-            if c > 0:
-                part = part + mm(feat, local_ref[0, h, c - 1])
-            part_out[h, rows] = part
-
-
-def inner_stage(slot, q, kt, val, local, table):
-    tok = q.shape[0]
+    at = (quarter_of(SLOTS[slot]) * 2 + h) * 16
+    base = at.astype(F32)
+    pick_first = jnp.where((entry == first + base) & (first >= 0), 1.0, 0.0).astype(BF16)
+    pick_second = jnp.where((entry == second + base) & (second >= 0), scale, 0.0).astype(BF16)
+    mine = (lane >= at) & (lane < at + 16)
+    for c in range(tok // CHUNK):
+        rows = slice(c * CHUNK, (c + 1) * CHUNK)
+        q = q_ref[rows]
+        feat = (mm(q, pick_first) + add_first) * (mm(q, pick_second) + add_second)
+        feat = feat.astype(BF16)
+        feat_out[rows] = feat
+        own = jnp.where(mine, q.astype(F32) * 0.25, 0.0).astype(BF16)
+        s = mm(own, kt_ref[:, rows])
+        taylor = jnp.where(below, (0.5 * s + 1.0) * s + 1.0, 0.0).astype(BF16)
+        right = jnp.concatenate([val_ref[slot, rows, h * 128 : (h + 1) * 128], ones], axis=1)
+        part = mm(taylor, right)
+        if c > 0:
+            part = part + mm(feat, local_ref[slot, h, c - 1])
+        part_out[rows] = part
+
+
+def inner_stage(slot, h, *args):
+    tok = args[0].shape[0]
     shape = jax.ShapeDtypeStruct
     return pl.pallas_call(
-        functools.partial(inner_kernel, slot),
-        grid=(1,),
-        out_shape=[shape((2, tok, ROWS), BF16), shape((2, tok, 256), F32)],
-        in_specs=[
-            pl.BlockSpec(q.shape, lambda i: (0, 0)),
-            pl.BlockSpec(kt.shape, lambda i: (0, 0)),
-            pl.BlockSpec((1,) + val.shape[1:], lambda i: (slot, 0, 0)),
-            pl.BlockSpec((1,) + local.shape[1:], lambda i: (slot, 0, 0, 0, 0)),
-            pl.BlockSpec(table.shape, lambda i: (0, 0)),
-        ],
-        out_specs=[
-            pl.BlockSpec((2, tok, ROWS), lambda i: (0, 0, 0)),
-            pl.BlockSpec((2, tok, 256), lambda i: (0, 0, 0)),
-        ],
-        compiler_params=pltpu.CompilerParams(vmem_limit_bytes=16 * 2**20),
-        cost_estimate=pl.CostEstimate(
-            flops=2 * 10**9, bytes_accessed=4 * 2**20, transcendentals=0
-        ),
+        functools.partial(inner_kernel, slot, h),
+        out_shape=[shape((tok, ROWS), BF16), shape((tok, 256), F32)],
+        in_specs=[VMEM] * 5,
+        out_specs=[VMEM] * 2,
+        compiler_params=pltpu.CompilerParams(vmem_limit_bytes=16 * MIB),
+        cost_estimate=pl.CostEstimate(flops=10**9, bytes_accessed=2 * MIB, transcendentals=0),
         name="inner_stage",
-    )(q, kt, val, local, table)
+    )(*args)
 
 
 def outer_kernel(count, *refs):
-    prefixes, feats, parts, out = (
-        refs[:count], refs[count : 2 * count], refs[2 * count : 3 * count], refs[3 * count]
-    )
+    prefixes, (*inner, out) = (refs[:count], refs[count:])
+    feats, parts = (inner[: 2 * count], inner[2 * count :])
     for i in range(count):
         for h in range(2):
             low = prefixes[i][h]
@@ -245,18 +231,18 @@
             rest = jnp.transpose(jnp.broadcast_to(wide[2:3], (128, 128)))[:32]
             norm = jnp.concatenate([top, rest], axis=0).astype(BF16)
             right = jnp.concatenate([low, norm], axis=1)
-            both = mm(feats[i][h], right) + parts[i][h]
+            both = mm(feats[2 * i + h][...], right) + parts[2 * i + h][...]
             cols = slice(i * 256 + h * 128, i * 256 + (h + 1) * 128)
             out[:, cols] = (both[:, :128] / both[:, 128:]).astype(BF16)
 
 
 def outer_stage(prefixes, feats, parts):
     count = len(prefixes)
-    tok = feats[0].shape[1]
+    tok = feats[0].shape[0]
     return pl.pallas_call(
         functools.partial(outer_kernel, count),
         out_shape=jax.ShapeDtypeStruct((tok, 256 * count), BF16),
-        in_specs=[VMEM] * (3 * count),
+        in_specs=[VMEM] * (5 * count),
         out_specs=VMEM,
         compiler_params=pltpu.CompilerParams(vmem_limit_bytes=24 * 2**20),
         cost_estimate=pl.CostEstimate(
@@ -426,13 +412,14 @@
     back = exclusive_prefix(states, columns)
     inner = {}
     for slot, step in enumerate(SLOTS):
-        inner[step] = inner_stage(slot, q, kt, val, local, table)
+        for h in range(2):
+            inner[step, h] = inner_stage(slot, h, q, kt, val, local, table)
 
     def outer(steps):
         return outer_stage(
             [back[step] for step in steps],
-            [inner[step][0] for step in steps],
-            [inner[step][1] for step in steps],
+            [inner[step, h][0] for step in steps for h in range(2)],
+            [inner[step, h][1] for step in steps for h in range(2)],
         )
 
     places, start = ([], 0)

time: 63.2 us -> 65.1 us (1.030)
  Pallas kernels: 27.5 us -> 28.9 us
  starting transfers between devices: 23.1 us -> 24.3 us
  waiting for transfers between devices: 12.3 us -> 11.5 us
    pallas_call x4 -> x8, Pallas kernels: 7.43 us -> 8.8 us  [inner_stage(): pl.pallas_call(functools.partial(inner_kernel, slot, h), out_shape=[shape...]
    ppermute x12, starting transfers between devices: 16 us -> 16.9 us  [partner(): return lax.ppermute(x, axis, pairs)]
    ppermute x12, waiting for transfers between devices: 12.2 us -> 11.5 us  [partner(): return lax.ppermute(x, axis, pairs)]
  transfers between devices with their start and end apart: 15 -> 15, of which waited for: 9 -> 10; matrix products, arithmetic and copies ran while one was open for 0% -> 0% of each run, Pallas kernels for 22% -> 23%
where the time goes in v2:
time: 65.1 us; the launch traced here: 65 us
  Pallas kernels  28.9 us (44%)
  starting transfers between devices  24.3 us (37%)
  waiting for transfers between devices  11.5 us (18%)
    ppermute x12, starting transfers between devices, partner(): return lax.ppermute(x, axis, pairs)  16.9 us
    ppermute x12, waiting for transfers between devices, partner(): return lax.ppermute(x, axis, pairs)  11.5 us
    pallas_call x1, Pallas kernels, head_stage(): pl.pallas_call(head_kernel, out_shape=[shape((tok, kd), BF16), shape((kd,...  9.94 us
    pallas_call x8, Pallas kernels, inner_stage(): pl.pallas_call(functools.partial(inner_kernel, slot, h), out_shape=[shape...  8.8 us
    ppermute x3, starting transfers between devices, per_device(): other.append(lax.ppermute(own[-1], 'head', [(0, 1), (1, 0)]))  7.4 us
    pallas_call x3, Pallas kernels, out_stage(): pl.pallas_call(functools.partial(out_kernel, places, last), out_shape=jax...  5.67 us
    pallas_call x1, Pallas kernels, fetch_stage(): pl.pallas_call(fetch_kernel, out_shape=jax.ShapeDtypeStruct((2, 1024, 102...  2.21 us
    pallas_call x3, Pallas kernels, outer_stage(): pl.pallas_call(functools.partial(outer_kernel, count), out_shape=jax.Shap...  1.86 us
  transfers between devices with their start and end apart: 15, of which 10 were waited for; matrix products, arithmetic and copies ran while one was open for 0% of the time, Pallas kernels for 23%

profile of v2, /device:TPU:1, one launch (start us, length us, event | category | flops | bytes accessed | tf_op | source)
XLA Modules:
  0.0 65.0 jit_solution(4850269641790962707)
XLA Ops:
  0.0 0.0 copy-start
  0.0 9.9 %head_stage.1 = (bf16[1024,128]{1,0:T(8,128)(2,1)S(1)}, bf16[128,1024]{1,0:T(8,128)(2,1)S(1)}, bf16[4,1024,256]{2,1,0:T(8,128)(2,1)S(1)}, bf16[4,2,3,160,256]{4,...) custom-call(bf16[1024,2048]{1,0:T(8,128)(2,1)} %x_hbm.1, ...), custom_call_target="tpu_custom_call" | custom-call | flops 6000000000 | bytes 12582912 | tf_op jit(solution)/shard_map/head_stage/pallas_call | solution.py:149
  10.0 4.5 %collective-permute-start = (bf16[2,160,128]{2,1,0:T(8,128)(2,1)S(1)}, bf16[2,160,128]{2,1,0:T(8,128)(2,1)S(1)}, u32[]{:S(2)}, u32[]{:S(2)}) collective-permute-start(bf16[2,160,128]{2,1,0:T(8,128)(2,1)S(1)} %get-tuple-element.36), channel_id=1, source_target_pairs={{0,4},{2,6},{4,0},{6,2},{1,5},{3,7},{5,1},{7,3},{8,12},{10,14},{12... | collective-permute-start | bytes 245768 | tf_op jit(solution)/shard_map/ppermute | solution.py:340
  14.5 0.7 %collective-permute-start.1 = (bf16[2,160,128]{2,1,0:T(8,128)(2,1)S(1)}, bf16[2,160,128]{2,1,0:T(8,128)(2,1)S(1)}, u32[]{:S(2)}, u32[]{:S(2)}) collective-permute-start(bf16[2,160,128]{2,1,0:T(8,128)(2,1)S(1)} %get-tuple-element.37), channel_id=1, source_target_pairs={{0,2},{2,0},{4,6},{6,4},{1,3},{3,1},{5,7},{7,5},{8,10},{10,8},{12,... | collective-permute-start | bytes 245768 | tf_op jit(solution)/shard_map/ppermute | solution.py:340
  15.2 0.0 collective-permute-start.2
  15.2 0.0 copy-done
  15.2 1.1 %inner_stage.8 = (bf16[1024,160]{1,0:T(8,128)(2,1)S(1)}, f32[1024,256]{1,0:T(8,128)S(1)}) custom-call(bf16[1024,128]{1,0:T(8,128)(2,1)S(1)} %get-tuple-element.43.q_ref, bf16[128,1024]{1,0:T(8,128)(2,1)S(1)} %get-tuple-element.44.kt_ref, bf16[4,1024,256]{2,1,0:T(8,128)(2,1)S(1)} %get-tuple-element.45.val_ref, ...), custom_call_target="tpu_custom_call" | custom-call | flops 1000000000 | bytes 2097152 | tf_op jit(solution)/shard_map/inner_stage/pallas_call | solution.py:212
  16.3 1.1 %inner_stage.9 = (bf16[1024,160]{1,0:T(8,128)(2,1)S(1)}, f32[1024,256]{1,0:T(8,128)S(1)}) custom-call(bf16[1024,128]{1,0:T(8,128)(2,1)S(1)} %get-tuple-element.43.q_ref, bf16[128,1024]{1,0:T(8,128)(2,1)S(1)} %get-tuple-element.44.kt_ref, bf16[4,1024,256]{2,1,0:T(8,128)(2,1)S(1)} %get-tuple-element.45.val_ref, ...), custom_call_target="tpu_custom_call" | custom-call | flops 1000000000 | bytes 2097152 | tf_op jit(solution)/shard_map/inner_stage/pallas_call | solution.py:212
  17.4 0.0 collective-permute-done.p1
  17.4 1.1 %collective-permute-done.1.p2 = bf16[2,160,128]{2,1,0:T(8,128)(2,1)S(1)} collective-permute-done((bf16[2,160,128]{2,1,0:T(8,128)(2,1)S(1)}, bf16[2,160,128]{2,1,0:T(8,128)(2,1)S(1)}, u32[]{:S(2)}, u32[]{:S(2)}) %collective-permute-start.1) | collective-permute-done | bytes 81952 | tf_op jit(solution)/shard_map/ppermute | solution.py:340
  18.5 1.2 %collective-permute-done.2.p3 = bf16[2,160,128]{2,1,0:T(8,128)(2,1)S(1)} collective-permute-done((bf16[2,160,128]{2,1,0:T(8,128)(2,1)S(1)}, bf16[2,160,128]{2,1,0:T(8,128)(2,1)S(1)}, u32[]{:S(2)}, u32[]{:S(2)}) %collective-permute-start.2) | collective-permute-done | bytes 81952 | tf_op jit(solution)/shard_map/ppermute | solution.py:340
  19.7 3.0 %collective-permute-start.3 = (bf16[2,160,128]{2,1,0:T(8,128)(2,1)S(1)}, bf16[2,160,128]{2,1,0:T(8,128)(2,1)S(1)}, u32[]{:S(2)}, u32[]{:S(2)}) collective-permute-start(bf16[2,160,128]{2,1,0:T(8,128)(2,1)S(1)} %shard_map.64.own), channel_id=1, source_target_pairs={{0,16},{8,24},{16,0},{24,8},{1,17},{9,25},{17,1},{25,9},{2,18},{10... | collective-permute-start | bytes 245768 | tf_op jit(solution)/shard_map/ppermute | solution.py:340
  22.7 0.4 collective-permute-start.4
  23.1 0.4 collective-permute-start.5
  23.5 2.2 %fetch_stage.1.columns.refs_1_.refs_3_.refs_2_ = bf16[2,1024,1024]{2,1,0:T(8,128)(2,1)S(1)} custom-call(bf16[2048,2048]{1,0:T(8,128)(2,1)} %w_hbm.1), custom_call_target="tpu_custom_call" | custom-call | flops 1000000000 | bytes 8388608 | tf_op jit(solution)/shard_map/fetch_stage/pallas_call | solution.py:275
  25.7 0.0 collective-permute-done.3.g0
  25.7 0.3 collective-permute-done.4.g1
  26.0 2.3 %collective-permute-done.5.g2 = bf16[2,160,128]{2,1,0:T(8,128)(2,1)S(1)} collective-permute-done((bf16[2,160,128]{2,1,0:T(8,128)(2,1)S(1)}, bf16[2,160,128]{2,1,0:T(8,128)(2,1)S(1)}, u32[]{:S(2)}, u32[]{:S(2)}) %collective-permute-start.5) | collective-permute-done | bytes 81952 | tf_op jit(solution)/shard_map/ppermute | solution.py:340
  28.3 0.1 shard_map.65
  28.4 2.8 %collective-permute-start.6 = (bf16[2,160,128]{2,1,0:T(8,128)(2,1)S(1)}, bf16[2,160,128]{2,1,0:T(8,128)(2,1)S(1)}, u32[]{:S(2)}, u32[]{:S(2)}) collective-permute-start(bf16[2,160,128]{2,1,0:T(8,128)(2,1)S(1)} %get-tuple-element.39.own), channel_id=1, source_target_pairs={{0,64},{32,96},{64,0},{96,32},{1,65},{33,97},{65,1},{97,33},{2,66}... | collective-permute-start | bytes 245768 | tf_op jit(solution)/shard_map/ppermute | solution.py:340
  31.3 0.3 collective-permute-start.7
  31.6 0.6 collective-permute-start.8
  32.1 1.1 %inner_stage.10 = (bf16[1024,160]{1,0:T(8,128)(2,1)S(1)}, f32[1024,256]{1,0:T(8,128)S(1)}) custom-call(bf16[1024,128]{1,0:T(8,128)(2,1)S(1)} %get-tuple-element.43.q_ref, bf16[128,1024]{1,0:T(8,128)(2,1)S(1)} %get-tuple-element.44.kt_ref, bf16[4,1024,256]{2,1,0:T(8,128)(2,1)S(1)} %get-tuple-element.45.val_ref, ...), custom_call_target="tpu_custom_call" | custom-call | flops 1000000000 | bytes 2097152 | tf_op jit(solution)/shard_map/inner_stage/pallas_call | solution.py:212
  33.2 0.1 collective-permute-done.6.g0
  33.3 1.2 %collective-permute-done.7.g1 = bf16[2,160,128]{2,1,0:T(8,128)(2,1)S(1)} collective-permute-done((bf16[2,160,128]{2,1,0:T(8,128)(2,1)S(1)}, bf16[2,160,128]{2,1,0:T(8,128)(2,1)S(1)}, u32[]{:S(2)}, u32[]{:S(2)}) %collective-permute-start.7) | collective-permute-done | bytes 81952 | tf_op jit(solution)/shard_map/ppermute | solution.py:340
  34.6 1.5 %collective-permute-done.8.g2 = bf16[2,160,128]{2,1,0:T(8,128)(2,1)S(1)} collective-permute-done((bf16[2,160,128]{2,1,0:T(8,128)(2,1)S(1)}, bf16[2,160,128]{2,1,0:T(8,128)(2,1)S(1)}, u32[]{:S(2)}, u32[]{:S(2)}) %collective-permute-start.8) | collective-permute-done | bytes 81952 | tf_op jit(solution)/shard_map/ppermute | solution.py:340
  36.1 0.3 shard_map.66
  36.3 2.1 %collective-permute-start.9 = (bf16[2,160,128]{2,1,0:T(8,128)(2,1)S(1)}, bf16[2,160,128]{2,1,0:T(8,128)(2,1)S(1)}, u32[]{:S(2)}, u32[]{:S(2)}) collective-permute-start(bf16[2,160,128]{2,1,0:T(8,128)(2,1)S(1)} %get-tuple-element.41), channel_id=1, source_target_pairs={{0,4},{2,6},{4,0},{6,2},{1,5},{3,7},{5,1},{7,3},{8,12},{10,14},{12... | collective-permute-start | bytes 245768 | tf_op jit(solution)/shard_map/ppermute | solution.py:340
  38.5 0.8 %collective-permute-start.10 = (bf16[2,160,128]{2,1,0:T(8,128)(2,1)S(1)}, bf16[2,160,128]{2,1,0:T(8,128)(2,1)S(1)}, u32[]{:S(2)}, u32[]{:S(2)}) collective-permute-start(bf16[2,160,128]{2,1,0:T(8,128)(2,1)S(1)} %get-tuple-element.42), channel_id=1, source_target_pairs={{0,2},{2,0},{4,6},{6,4},{1,3},{3,1},{5,7},{7,5},{8,10},{10,8},{12,... | collective-permute-start | bytes 245768 | tf_op jit(solution)/shard_map/ppermute | solution.py:340
  39.3 1.1 %inner_stage.11 = (bf16[1024,160]{1,0:T(8,128)(2,1)S(1)}, f32[1024,256]{1,0:T(8,128)S(1)}) custom-call(bf16[1024,128]{1,0:T(8,128)(2,1)S(1)} %get-tuple-element.43.q_ref, bf16[128,1024]{1,0:T(8,128)(2,1)S(1)} %get-tuple-element.44.kt_ref, bf16[4,1024,256]{2,1,0:T(8,128)(2,1)S(1)} %get-tuple-element.45.val_ref, ...), custom_call_target="tpu_custom_call" | custom-call | flops 1000000000 | bytes 2097152 | tf_op jit(solution)/shard_map/inner_stage/pallas_call | solution.py:212
  40.4 0.8 %collective-permute-done.9.refs_0_ = bf16[2,160,128]{2,1,0:T(8,128)(2,1)S(1)} collective-permute-done((bf16[2,160,128]{2,1,0:T(8,128)(2,1)S(1)}, bf16[2,160,128]{2,1,0:T(8,128)(2,1)S(1)}, u32[]{:S(2)}, u32[]{:S(2)}) %collective-permute-start.9) | collective-permute-done | bytes 81952 | tf_op jit(solution)/shard_map/ppermute | solution.py:340
  41.2 0.7 %collective-permute-done.10.refs_1_ = bf16[2,160,128]{2,1,0:T(8,128)(2,1)S(1)} collective-permute-done((bf16[2,160,128]{2,1,0:T(8,128)(2,1)S(1)}, bf16[2,160,128]{2,1,0:T(8,128)(2,1)S(1)}, u32[]{:S(2)}, u32[]{:S(2)}) %collective-permute-start.10) | collective-permute-done | bytes 81952 | tf_op jit(solution)/shard_map/ppermute | solution.py:340
  42.0 0.8 %outer_stage.3.refs_0_ = bf16[1024,512]{1,0:T(8,128)(2,1)S(1)} custom-call(bf16[2,160,128]{2,1,0:T(8,128)(2,1)S(1)} %collective-permute-done.9.refs_0_, bf16[2,160,128]{2,1,0:T(8,128)(2,1)S(1)} %collective-permute-done.10.refs_1_, bf16[1024,160]{1,0:T(8,128)(2,1)S(1)} %get-tuple-element.47.refs_2_, bf16[1024,160]{1,0:T(8,128)(2,1)S(1)} %get-tuple-element.48.refs_3_, ...), custom_call_target="tpu_custom_call" | custom-call | flops 600000000 | bytes 2097152 | tf_op jit(solution)/shard_map/outer_stage/pallas_call | solution.py:242
  42.8 5.6 %collective-permute-start.11 = (bf16[1024,512]{1,0:T(8,128)(2,1)S(1)}, bf16[1024,512]{1,0:T(8,128)(2,1)S(1)}, u32[]{:S(2)}, u32[]{:S(2)}) collective-permute-start(bf16[1024,512]{1,0:T(8,128)(2,1)S(1)} %outer_stage.3.refs_0_), channel_id=1, source_target_pairs={{0,1},{1,0},{2,3},{3,2},{4,5},{5,4},{6,7},{7,6},{8,9},{9,8},{10,11... | collective-permute-start | bytes 3145736 | tf_op jit(solution)/shard_map/ppermute | solution.py:432
  48.4 1.1 %inner_stage.14 = (bf16[1024,160]{1,0:T(8,128)(2,1)S(1)}, f32[1024,256]{1,0:T(8,128)S(1)}) custom-call(bf16[1024,128]{1,0:T(8,128)(2,1)S(1)} %get-tuple-element.43.q_ref, bf16[128,1024]{1,0:T(8,128)(2,1)S(1)} %get-tuple-element.44.kt_ref, bf16[4,1024,256]{2,1,0:T(8,128)(2,1)S(1)} %get-tuple-element.45.val_ref, ...), custom_call_target="tpu_custom_call" | custom-call | flops 1000000000 | bytes 2097152 | tf_op jit(solution)/shard_map/inner_stage/pallas_call | solution.py:212
  49.5 1.1 %inner_stage.15 = (bf16[1024,160]{1,0:T(8,128)(2,1)S(1)}, f32[1024,256]{1,0:T(8,128)S(1)}) custom-call(bf16[1024,128]{1,0:T(8,128)(2,1)S(1)} %get-tuple-element.43.q_ref, bf16[128,1024]{1,0:T(8,128)(2,1)S(1)} %get-tuple-element.44.kt_ref, bf16[4,1024,256]{2,1,0:T(8,128)(2,1)S(1)} %get-tuple-element.45.val_ref, ...), custom_call_target="tpu_custom_call" | custom-call | flops 1000000000 | bytes 2097152 | tf_op jit(solution)/shard_map/inner_stage/pallas_call | solution.py:212
  50.6 0.5 outer_stage.5.refs_0_
  51.1 0.1 collective-permute-start.14
  51.2 1.1 %inner_stage.12 = (bf16[1024,160]{1,0:T(8,128)(2,1)S(1)}, f32[1024,256]{1,0:T(8,128)S(1)}) custom-call(bf16[1024,128]{1,0:T(8,128)(2,1)S(1)} %get-tuple-element.43.q_ref, bf16[128,1024]{1,0:T(8,128)(2,1)S(1)} %get-tuple-element.44.kt_ref, bf16[4,1024,256]{2,1,0:T(8,128)(2,1)S(1)} %get-tuple-element.45.val_ref, ...), custom_call_target="tpu_custom_call" | custom-call | flops 1000000000 | bytes 2097152 | tf_op jit(solution)/shard_map/inner_stage/pallas_call | solution.py:212
  52.3 1.2 %collective-permute-start.12 = (bf16[2,160,128]{2,1,0:T(8,128)(2,1)S(1)}, bf16[2,160,128]{2,1,0:T(8,128)(2,1)S(1)}, u32[]{:S(2)}, u32[]{:S(2)}) collective-permute-start(bf16[2,160,128]{2,1,0:T(8,128)(2,1)S(1)} %get-tuple-element.55), channel_id=1, source_target_pairs={{0,6},{2,4},{4,2},{6,0},{1,7},{3,5},{5,3},{7,1},{8,14},{10,12},{12... | collective-permute-start | bytes 245768 | tf_op jit(solution)/shard_map/ppermute | solution.py:340
  53.6 1.1 %inner_stage.13 = (bf16[1024,160]{1,0:T(8,128)(2,1)S(1)}, f32[1024,256]{1,0:T(8,128)S(1)}) custom-call(bf16[1024,128]{1,0:T(8,128)(2,1)S(1)} %get-tuple-element.43.q_ref, bf16[128,1024]{1,0:T(8,128)(2,1)S(1)} %get-tuple-element.44.kt_ref, bf16[4,1024,256]{2,1,0:T(8,128)(2,1)S(1)} %get-tuple-element.45.val_ref, ...), custom_call_target="tpu_custom_call" | custom-call | flops 1000000000 | bytes 2097152 | tf_op jit(solution)/shard_map/inner_stage/pallas_call | solution.py:212
  54.7 2.2 %collective-permute-done.12.refs_0_ = bf16[2,160,128]{2,1,0:T(8,128)(2,1)S(1)} collective-permute-done((bf16[2,160,128]{2,1,0:T(8,128)(2,1)S(1)}, bf16[2,160,128]{2,1,0:T(8,128)(2,1)S(1)}, u32[]{:S(2)}, u32[]{:S(2)}) %collective-permute-start.12) | collective-permute-done | bytes 81952 | tf_op jit(solution)/shard_map/ppermute | solution.py:340
  56.9 0.5 outer_stage.4.refs_1_
  57.4 1.7 %collective-permute-start.13 = (bf16[1024,256]{1,0:T(8,128)(2,1)S(1)}, bf16[1024,256]{1,0:T(8,128)(2,1)S(1)}, u32[]{:S(2)}, u32[]{:S(2)}) collective-permute-start(bf16[1024,256]{1,0:T(8,128)(2,1)S(1)} %outer_stage.4.refs_1_), channel_id=1, source_target_pairs={{0,1},{1,0},{2,3},{3,2},{4,5},{5,4},{6,7},{7,6},{8,9},{9,8},{10,11... | collective-permute-start | bytes 1572872 | tf_op jit(solution)/shard_map/ppermute | solution.py:432
  59.1 0.7 %out_stage.3.refs_4_ = f32[1024,1024]{1,0:T(8,128)S(1)} custom-call(bf16[1024,256]{1,0:T(8,128)(2,1)S(1)} %outer_stage.5.refs_0_, bf16[2,1024,1024]{2,1,0:T(8,128)(2,1)S(1)} %fetch_stage.1.columns.refs_1_.refs_3_.refs_2_), custom_call_target="tpu_custom_call" | custom-call | flops 536870912 | bytes 1048576 | tf_op jit(solution)/shard_map/out_stage/pallas_call | solution.py:322
  59.9 0.0 collective-permute-done.14.refs_2_
  59.9 2.3 %out_stage.4.refs_3_ = f32[1024,1024]{1,0:T(8,128)S(1)} custom-call(bf16[1024,512]{1,0:T(8,128)(2,1)S(1)} %outer_stage.3.refs_0_, bf16[1024,256]{1,0:T(8,128)(2,1)S(1)} %outer_stage.4.refs_1_, bf16[1024,256]{1,0:T(8,128)(2,1)S(1)} %collective-permute-done.14.refs_2_, bf16[2,1024,1024]{2,1,0:T(8,128)(2,1)S(1)} %fetch_stage.1.columns.refs_1_.refs_3_.refs_2_, ...), custom_call_target="tpu_custom_call" | custom-call | flops 2147483648 | bytes 1048576 | tf_op jit(solution)/shard_map/out_stage/pallas_call | solution.py:322
  62.2 0.0 collective-permute-done.13.refs_1_
  62.2 0.0 collective-permute-done.11.refs_0_
  62.2 2.6 %out_stage.5 = bf16[1024,1024]{1,0:T(8,128)(2,1)} custom-call(bf16[1024,512]{1,0:T(8,128)(2,1)S(1)} %collective-permute-done.11.refs_0_, bf16[1024,256]{1,0:T(8,128)(2,1)S(1)} %collective-permute-done.13.refs_1_, bf16[2,1024,1024]{2,1,0:T(8,128)(2,1)S(1)} %fetch_stage.1.columns.refs_1_.refs_3_.refs_2_, f32[1024,1024]{1,0:T(8,128)S(1)} %out_stage.4.refs_3_), custom_call_target="tpu_custom_call" | custom-call | flops 1610612736 | bytes 1048576 | tf_op jit(solution)/shard_map/out_stage/pallas_call | solution.py:322
  (1 shorter events, 0.0 us)
Async XLA Ops:
  0.0 15.2 %copy-start = (f32[8,160]{1,0:T(8,128)S(1)}, f32[8,160]{1,0:T(8,128)}, u32[]{:S(2)}) copy-start(f32[8,160]{1,0:T(8,128)} %constant.2.clone.table_ref) | copy-start | bytes 15364
  10.0 7.5 %collective-permute-start = (bf16[2,160,128]{2,1,0:T(8,128)(2,1)S(1)}, bf16[2,160,128]{2,1,0:T(8,128)(2,1)S(1)}, u32[]{:S(2)}, u32[]{:S(2)}) collective-permute-start(bf16[2,160,128]{2,1,0:T(8,128)(2,1)S(1)} %get-tuple-element.36), channel_id=1, source_target_pairs={{0,4},{2,6},{4,0},{6,2},{1,5},{3,7},{5,1},{7,3},{8,12},{10,14},{12... | collective-permute-start | bytes 245768 | tf_op jit(solution)/shard_map/ppermute | solution.py:340
  14.5 4.1 %collective-permute-start.1 = (bf16[2,160,128]{2,1,0:T(8,128)(2,1)S(1)}, bf16[2,160,128]{2,1,0:T(8,128)(2,1)S(1)}, u32[]{:S(2)}, u32[]{:S(2)}) collective-permute-start(bf16[2,160,128]{2,1,0:T(8,128)(2,1)S(1)} %get-tuple-element.37), channel_id=1, source_target_pairs={{0,2},{2,0},{4,6},{6,4},{1,3},{3,1},{5,7},{7,5},{8,10},{10,8},{12,... | collective-permute-start | bytes 245768 | tf_op jit(solution)/shard_map/ppermute | solution.py:340
  15.2 4.5 %collective-permute-start.2 = (bf16[2,160,128]{2,1,0:T(8,128)(2,1)S(1)}, bf16[2,160,128]{2,1,0:T(8,128)(2,1)S(1)}, u32[]{:S(2)}, u32[]{:S(2)}) collective-permute-start(bf16[2,160,128]{2,1,0:T(8,128)(2,1)S(1)} %get-tuple-element.38), channel_id=1, source_target_pairs={{0,6},{2,4},{4,2},{6,0},{1,7},{3,5},{5,3},{7,1},{8,14},{10,12},{12... | collective-permute-start | bytes 245768 | tf_op jit(solution)/shard_map/ppermute | solution.py:340
  19.7 6.0 %collective-permute-start.3 = (bf16[2,160,128]{2,1,0:T(8,128)(2,1)S(1)}, bf16[2,160,128]{2,1,0:T(8,128)(2,1)S(1)}, u32[]{:S(2)}, u32[]{:S(2)}) collective-permute-start(bf16[2,160,128]{2,1,0:T(8,128)(2,1)S(1)} %shard_map.64.own), channel_id=1, source_target_pairs={{0,16},{8,24},{16,0},{24,8},{1,17},{9,25},{17,1},{25,9},{2,18},{10... | collective-permute-start | bytes 245768 | tf_op jit(solution)/shard_map/ppermute | solution.py:340
  22.7 3.3 %collective-permute-start.4 = (bf16[2,160,128]{2,1,0:T(8,128)(2,1)S(1)}, bf16[2,160,128]{2,1,0:T(8,128)(2,1)S(1)}, u32[]{:S(2)}, u32[]{:S(2)}) collective-permute-start(bf16[2,160,128]{2,1,0:T(8,128)(2,1)S(1)} %shard_map.64.own), channel_id=1, source_target_pairs={{0,8},{8,0},{16,24},{24,16},{1,9},{9,1},{17,25},{25,17},{2,10},{10... | collective-permute-start | bytes 245768 | tf_op jit(solution)/shard_map/ppermute | solution.py:340
  23.1 5.2 %collective-permute-start.5 = (bf16[2,160,128]{2,1,0:T(8,128)(2,1)S(1)}, bf16[2,160,128]{2,1,0:T(8,128)(2,1)S(1)}, u32[]{:S(2)}, u32[]{:S(2)}) collective-permute-start(bf16[2,160,128]{2,1,0:T(8,128)(2,1)S(1)} %shard_map.64.own), channel_id=1, source_target_pairs={{0,24},{8,16},{16,8},{24,0},{1,25},{9,17},{17,9},{25,1},{2,26},{10... | collective-permute-start | bytes 245768 | tf_op jit(solution)/shard_map/ppermute | solution.py:340
  28.4 4.9 %collective-permute-start.6 = (bf16[2,160,128]{2,1,0:T(8,128)(2,1)S(1)}, bf16[2,160,128]{2,1,0:T(8,128)(2,1)S(1)}, u32[]{:S(2)}, u32[]{:S(2)}) collective-permute-start(bf16[2,160,128]{2,1,0:T(8,128)(2,1)S(1)} %get-tuple-element.39.own), channel_id=1, source_target_pairs={{0,64},{32,96},{64,0},{96,32},{1,65},{33,97},{65,1},{97,33},{2,66}... | collective-permute-start | bytes 245768 | tf_op jit(solution)/shard_map/ppermute | solution.py:340
  31.3 3.3 %collective-permute-start.7 = (bf16[2,160,128]{2,1,0:T(8,128)(2,1)S(1)}, bf16[2,160,128]{2,1,0:T(8,128)(2,1)S(1)}, u32[]{:S(2)}, u32[]{:S(2)}) collective-permute-start(bf16[2,160,128]{2,1,0:T(8,128)(2,1)S(1)} %get-tuple-element.39.own), channel_id=1, source_target_pairs={{0,32},{32,0},{64,96},{96,64},{1,33},{33,1},{65,97},{97,65},{2,34}... | collective-permute-start | bytes 245768 | tf_op jit(solution)/shard_map/ppermute | solution.py:340
  31.6 4.5 %collective-permute-start.8 = (bf16[2,160,128]{2,1,0:T(8,128)(2,1)S(1)}, bf16[2,160,128]{2,1,0:T(8,128)(2,1)S(1)}, u32[]{:S(2)}, u32[]{:S(2)}) collective-permute-start(bf16[2,160,128]{2,1,0:T(8,128)(2,1)S(1)} %get-tuple-element.39.own), channel_id=1, source_target_pairs={{0,96},{32,64},{64,32},{96,0},{1,97},{33,65},{65,33},{97,1},{2,98}... | collective-permute-start | bytes 245768 | tf_op jit(solution)/shard_map/ppermute | solution.py:340
  36.3 4.9 %collective-permute-start.9 = (bf16[2,160,128]{2,1,0:T(8,128)(2,1)S(1)}, bf16[2,160,128]{2,1,0:T(8,128)(2,1)S(1)}, u32[]{:S(2)}, u32[]{:S(2)}) collective-permute-start(bf16[2,160,128]{2,1,0:T(8,128)(2,1)S(1)} %get-tuple-element.41), channel_id=1, source_target_pairs={{0,4},{2,6},{4,0},{6,2},{1,5},{3,7},{5,1},{7,3},{8,12},{10,14},{12... | collective-permute-start | bytes 245768 | tf_op jit(solution)/shard_map/ppermute | solution.py:340
  38.5 3.5 %collective-permute-start.10 = (bf16[2,160,128]{2,1,0:T(8,128)(2,1)S(1)}, bf16[2,160,128]{2,1,0:T(8,128)(2,1)S(1)}, u32[]{:S(2)}, u32[]{:S(2)}) collective-permute-start(bf16[2,160,128]{2,1,0:T(8,128)(2,1)S(1)} %get-tuple-element.42), channel_id=1, source_target_pairs={{0,2},{2,0},{4,6},{6,4},{1,3},{3,1},{5,7},{7,5},{8,10},{10,8},{12,... | collective-permute-start | bytes 245768 | tf_op jit(solution)/shard_map/ppermute | solution.py:340
  42.8 19.4 %collective-permute-start.11 = (bf16[1024,512]{1,0:T(8,128)(2,1)S(1)}, bf16[1024,512]{1,0:T(8,128)(2,1)S(1)}, u32[]{:S(2)}, u32[]{:S(2)}) collective-permute-start(bf16[1024,512]{1,0:T(8,128)(2,1)S(1)} %outer_stage.3.refs_0_), channel_id=1, source_target_pairs={{0,1},{1,0},{2,3},{3,2},{4,5},{5,4},{6,7},{7,6},{8,9},{9,8},{10,11... | collective-permute-start | bytes 3145736 | tf_op jit(solution)/shard_map/ppermute | solution.py:432
  51.1 8.7 %collective-permute-start.14 = (bf16[1024,256]{1,0:T(8,128)(2,1)S(1)}, bf16[1024,256]{1,0:T(8,128)(2,1)S(1)}, u32[]{:S(2)}, u32[]{:S(2)}) collective-permute-start(bf16[1024,256]{1,0:T(8,128)(2,1)S(1)} %outer_stage.5.refs_0_), channel_id=1, source_target_pairs={{0,1},{1,0},{2,3},{3,2},{4,5},{5,4},{6,7},{7,6},{8,9},{9,8},{10,11... | collective-permute-start | bytes 1572872 | tf_op jit(solution)/shard_map/ppermute | solution.py:432
  52.3 4.6 %collective-permute-start.12 = (bf16[2,160,128]{2,1,0:T(8,128)(2,1)S(1)}, bf16[2,160,128]{2,1,0:T(8,128)(2,1)S(1)}, u32[]{:S(2)}, u32[]{:S(2)}) collective-permute-start(bf16[2,160,128]{2,1,0:T(8,128)(2,1)S(1)} %get-tuple-element.55), channel_id=1, source_target_pairs={{0,6},{2,4},{4,2},{6,0},{1,7},{3,5},{5,3},{7,1},{8,14},{10,12},{12... | collective-permute-start | bytes 245768 | tf_op jit(solution)/shard_map/ppermute | solution.py:340
  57.4 4.8 %collective-permute-start.13 = (bf16[1024,256]{1,0:T(8,128)(2,1)S(1)}, bf16[1024,256]{1,0:T(8,128)(2,1)S(1)}, u32[]{:S(2)}, u32[]{:S(2)}) collective-permute-start(bf16[1024,256]{1,0:T(8,128)(2,1)S(1)} %outer_stage.4.refs_1_), channel_id=1, source_target_pairs={{0,1},{1,0},{2,3},{3,2},{4,5},{5,4},{6,7},{7,6},{8,9},{9,8},{10,11... | collective-permute-start | bytes 1572872 | tf_op jit(solution)/shard_map/ppermute | solution.py:432

commit v3 on v2

--- a/solution.py
+++ b/solution.py
@@ -15,10 +15,11 @@
 SEQ = ("seq_0", "seq_1", "seq_2")
 STEPS = (2, 1, 3)
 MIB = 2**20
-HEAD_LIMIT, FETCH_LIMIT, OUT_LIMIT = (48 * MIB, 44 * MIB, 20 * MIB)
+HEAD_LIMIT, OUT_LIMIT = (48 * MIB, 20 * MIB)
 SLOTS = (0, 2, 1, 3)
 OUT_STEPS = (0, 2, 1, 3)
 GROUPS = ((0,), (2, 1), (3,))
+FETCH_STEP = 2
 F32, BF16 = (jnp.float32, jnp.bfloat16)
 VMEM = pl.BlockSpec(memory_space=pltpu.VMEM)
 SMEM = pl.BlockSpec(memory_space=pltpu.SMEM)
@@ -83,7 +84,7 @@
     def wcopy(j, src, half):
         rows = pl.ds(j * cut, cut)
         return pltpu.make_async_copy(
-            src.at[rows], wkq.at[rows, pl.ds(half * kd, kd)], w_sem.at[2 * j + half]
+            src.at[rows], wkq.at[half, rows], w_sem.at[2 * j + half]
         )
 
     def xcopy(j):
@@ -102,15 +103,15 @@
         wcopy(j, wk_hbm, 0).start()
         wcopy(j, wq_hbm, 1).start()
         xcopy(j).start()
-    for s in range(4):
-        vcopy(s).start()
     for j in range(cuts):
         wcopy(j, wk_hbm, 0).wait()
         wcopy(j, wq_hbm, 1).wait()
         xcopy(j).wait()
+        vcopy(j).start()
         cols = slice(j * cut, (j + 1) * cut)
+        both = jnp.concatenate([wkq[0, cols], wkq[1, cols]], axis=1)
         for rows in (slice(0, tok // 2), slice(tok // 2, tok)):
-            part = mm(x[rows, cols], wkq[cols])
+            part = mm(x[rows, cols], both)
             acc[rows] = part if j == 0 else acc[rows] + part
     q_out[...] = acc[:, kd:].astype(BF16)
     keys = jnp.transpose(acc[:, :kd].astype(BF16).astype(F32))
@@ -159,7 +160,7 @@
         out_specs=[VMEM] * 8,
         scratch_shapes=[
             pltpu.VMEM((tok, width), BF16),
-            pltpu.VMEM((width, 2 * kd), BF16),
+            pltpu.VMEM((2, width, kd), BF16),
             pltpu.VMEM((2, width, 512), BF16),
             pltpu.VMEM((tok, 2 * kd), F32),
             pltpu.VMEM((kd, tok), F32),
@@ -252,38 +253,47 @@
     )(*prefixes, *feats, *parts)
 
 
-def fetch_kernel(w_hbm, out, sem):
+def fetch_copies(w_hbm, out, sem):
     own = lax.axis_index("head")
     cols = pl.ds(pl.multiple_of(own * 1024, 1024), 1024)
-
-    def copy(half, s):
-        start = pl.multiple_of((own ^ half) * 1024 + quarter_of(OUT_STEPS[s]) * 256, 256)
-        return pltpu.make_async_copy(
-            w_hbm.at[pl.ds(start, 256), cols],
-            out.at[half, pl.ds(s * 256, 256)],
-            sem.at[half * 4 + s],
-        )
-
-    pieces = [copy(half, s) for half in range(2) for s in range(4)]
-    for piece in pieces:
-        piece.start()
-    for piece in pieces:
-        piece.wait()
-
-
-def fetch_stage(w_out):
-    return pl.pallas_call(
-        fetch_kernel,
-        out_shape=jax.ShapeDtypeStruct((2, 1024, 1024), BF16),
-        in_specs=[ANY],
-        out_specs=VMEM,
+    copies = []
+    for half in range(2):
+        for s in range(4):
+            row = (own ^ half) * 1024 + quarter_of(OUT_STEPS[s]) * 256
+            source = w_hbm.at[pl.ds(pl.multiple_of(row, 256), 256), cols]
+            target = out.at[half, pl.ds(s * 256, 256)]
+            copies.append(pltpu.make_async_copy(source, target, sem.at[half * 4 + s]))
+    return copies
+
+
+def fetch_kernel(slot, q, kt, val, local, table, w_hbm, *rest):
+    *outs, columns, sem = rest
+    copies = fetch_copies(w_hbm, columns, sem)
+    for copy in copies:
+        copy.start()
+    for h in range(2):
+        inner_kernel(slot, h, q, kt, val, local, table, *outs[2 * h : 2 * h + 2])
+    for copy in copies:
+        copy.wait()
+
+
+def fetch_stage(slot, *args):
+    tok = args[0].shape[0]
+    shape = jax.ShapeDtypeStruct
+    *outs, columns = pl.pallas_call(
+        functools.partial(fetch_kernel, slot),
+        out_shape=[shape((tok, ROWS), BF16), shape((tok, 256), F32)] * 2
+        + [shape((2, 1024, 1024), BF16)],
+        in_specs=[VMEM] * 5 + [ANY],
+        out_specs=[VMEM] * 5,
         scratch_shapes=[pltpu.SemaphoreType.DMA((8,))],
-        compiler_params=pltpu.CompilerParams(vmem_limit_bytes=FETCH_LIMIT),
+        compiler_params=pltpu.CompilerParams(vmem_limit_bytes=16 * MIB),
         cost_estimate=pl.CostEstimate(
-            flops=10**9, bytes_accessed=8 * 2**20, transcendentals=0
+            flops=2 * 10**9, bytes_accessed=4 * MIB, transcendentals=0
         ),
         name="fetch_stage",
-    )(w_out)
+    )(*args)
+    return outs[:2], outs[2:], columns
 
 
 def out_kernel(places, last, *refs):
@@ -408,12 +418,16 @@
     )
     table = jnp.asarray(feature_tables())
     q, kt, val, local, *states = head_stage(tokens, w_key, w_query, w_value)
-    columns = fetch_stage(w_out)
+    inner = {}
+    args = (q, kt, val, local, table)
+    for slot, step in enumerate(SLOTS):
+        if step == FETCH_STEP:
+            *pair, columns = fetch_stage(slot, *args, w_out)
+            inner[step, 0], inner[step, 1] = pair
+            continue
+        for h in range(2):
+            inner[step, h] = inner_stage(slot, h, *args)
     back = exclusive_prefix(states, columns)
-    inner = {}
-    for slot, step in enumerate(SLOTS):
-        for h in range(2):
-            inner[step, h] = inner_stage(slot, h, q, kt, val, local, table)
 
     def outer(steps):
         return outer_stage(

time: 65.1 us -> 64.4 us (0.989)
  Pallas kernels: 28.9 us -> 27.7 us
    pallas_call x8 -> x6, Pallas kernels: 8.8 us -> 6.6 us  [inner_stage(): pl.pallas_call(functools.partial(inner_kernel, slot, h), out_shape=[shape...]
    pallas_call x1, Pallas kernels: 2.21 us -> 3.91 us  [fetch_stage(): pl.pallas_call(functools.partial(fetch_kernel, slot), out_shape=[shape((t...]
    pallas_call x1, Pallas kernels: 9.94 us -> 9.26 us  [head_stage(): pl.pallas_call(head_kernel, out_shape=[shape((tok, kd), BF16), shape((kd,...]
where the time goes in v3:
time: 64.4 us; the launch traced here: 64.3 us
  Pallas kernels  27.7 us (43%)
  starting transfers between devices  24.3 us (38%)
  waiting for transfers between devices  12.1 us (19%)
    ppermute x12, starting transfers between devices, partner(): return lax.ppermute(x, axis, pairs)  16.9 us
    ppermute x12, waiting for transfers between devices, partner(): return lax.ppermute(x, axis, pairs)  12.1 us
    pallas_call x1, Pallas kernels, head_stage(): pl.pallas_call(head_kernel, out_shape=[shape((tok, kd), BF16), shape((kd,...  9.26 us
    ppermute x3, starting transfers between devices, per_device(): other.append(lax.ppermute(own[-1], 'head', [(0, 1), (1, 0)]))  7.4 us
    pallas_call x6, Pallas kernels, inner_stage(): pl.pallas_call(functools.partial(inner_kernel, slot, h), out_shape=[shape...  6.6 us
    pallas_call x3, Pallas kernels, out_stage(): pl.pallas_call(functools.partial(out_kernel, places, last), out_shape=jax...  5.67 us
    pallas_call x1, Pallas kernels, fetch_stage(): pl.pallas_call(functools.partial(fetch_kernel, slot), out_shape=[shape((t...  3.91 us
    pallas_call x3, Pallas kernels, outer_stage(): pl.pallas_call(functools.partial(outer_kernel, count), out_shape=jax.Shap...  1.83 us
  transfers between devices with their start and end apart: 15, of which 10 were waited for; matrix products, arithmetic and copies ran while one was open for 0% of the time, Pallas kernels for 23%

profile of v3, /device:TPU:1, one launch (start us, length us, event | category | flops | bytes accessed | tf_op | source)
XLA Modules:
  0.0 64.3 jit_solution(3260032981241560117)
XLA Ops:
  0.0 0.0 copy-start
  0.0 9.3 %head_stage.1 = (bf16[1024,128]{1,0:T(8,128)(2,1)S(1)}, bf16[128,1024]{1,0:T(8,128)(2,1)S(1)}, bf16[4,1024,256]{2,1,0:T(8,128)(2,1)S(1)}, bf16[4,2,3,160,256]{4,...) custom-call(bf16[1024,2048]{1,0:T(8,128)(2,1)} %x_hbm.1, ...), custom_call_target="tpu_custom_call" | custom-call | flops 6000000000 | bytes 12582912 | tf_op jit(solution)/shard_map/head_stage/pallas_call | solution.py:150
  9.3 4.5 %collective-permute-start = (bf16[2,160,128]{2,1,0:T(8,128)(2,1)S(1)}, bf16[2,160,128]{2,1,0:T(8,128)(2,1)S(1)}, u32[]{:S(2)}, u32[]{:S(2)}) collective-permute-start(bf16[2,160,128]{2,1,0:T(8,128)(2,1)S(1)} %get-tuple-element.37), channel_id=1, source_target_pairs={{0,4},{2,6},{4,0},{6,2},{1,5},{3,7},{5,1},{7,3},{8,12},{10,14},{12... | collective-permute-start | bytes 245768 | tf_op jit(solution)/shard_map/ppermute | solution.py:350
  13.8 0.7 %collective-permute-start.1 = (bf16[2,160,128]{2,1,0:T(8,128)(2,1)S(1)}, bf16[2,160,128]{2,1,0:T(8,128)(2,1)S(1)}, u32[]{:S(2)}, u32[]{:S(2)}) collective-permute-start(bf16[2,160,128]{2,1,0:T(8,128)(2,1)S(1)} %get-tuple-element.38), channel_id=1, source_target_pairs={{0,2},{2,0},{4,6},{6,4},{1,3},{3,1},{5,7},{7,5},{8,10},{10,8},{12,... | collective-permute-start | bytes 245768 | tf_op jit(solution)/shard_map/ppermute | solution.py:350
  14.5 0.0 collective-permute-start.2
  14.5 1.4 %collective-permute-done.p1 = bf16[2,160,128]{2,1,0:T(8,128)(2,1)S(1)} collective-permute-done((bf16[2,160,128]{2,1,0:T(8,128)(2,1)S(1)}, bf16[2,160,128]{2,1,0:T(8,128)(2,1)S(1)}, u32[]{:S(2)}, u32[]{:S(2)}) %collective-permute-start) | collective-permute-done | bytes 81952 | tf_op jit(solution)/shard_map/ppermute | solution.py:350
  15.9 1.9 %collective-permute-done.1.p2 = bf16[2,160,128]{2,1,0:T(8,128)(2,1)S(1)} collective-permute-done((bf16[2,160,128]{2,1,0:T(8,128)(2,1)S(1)}, bf16[2,160,128]{2,1,0:T(8,128)(2,1)S(1)}, u32[]{:S(2)}, u32[]{:S(2)}) %collective-permute-start.1) | collective-permute-done | bytes 81952 | tf_op jit(solution)/shard_map/ppermute | solution.py:350
  17.8 1.2 %collective-permute-done.2.p3 = bf16[2,160,128]{2,1,0:T(8,128)(2,1)S(1)} collective-permute-done((bf16[2,160,128]{2,1,0:T(8,128)(2,1)S(1)}, bf16[2,160,128]{2,1,0:T(8,128)(2,1)S(1)}, u32[]{:S(2)}, u32[]{:S(2)}) %collective-permute-start.2) | collective-permute-done | bytes 81952 | tf_op jit(solution)/shard_map/ppermute | solution.py:350
  19.0 3.0 %collective-permute-start.3 = (bf16[2,160,128]{2,1,0:T(8,128)(2,1)S(1)}, bf16[2,160,128]{2,1,0:T(8,128)(2,1)S(1)}, u32[]{:S(2)}, u32[]{:S(2)}) collective-permute-start(bf16[2,160,128]{2,1,0:T(8,128)(2,1)S(1)} %shard_map.64.own), channel_id=1, source_target_pairs={{0,16},{8,24},{16,0},{24,8},{1,17},{9,25},{17,1},{25,9},{2,18},{10... | collective-permute-start | bytes 245768 | tf_op jit(solution)/shard_map/ppermute | solution.py:350
  22.0 0.4 collective-permute-start.4
  22.4 0.4 collective-permute-start.5
  22.8 0.0 copy-done
  22.8 3.9 %fetch_stage.1 = (bf16[1024,160]{1,0:T(8,128)(2,1)S(1)}, f32[1024,256]{1,0:T(8,128)S(1)}, bf16[1024,160]{1,0:T(8,128)(2,1)S(1)}, f32[1024,256]{1,0:T(8,128)S(1)}, bf16[2,1024,1024]{2,1,0:T(8,128)(2,1)S(1)}) custom-call(bf16[1024,128]{1,0:T(8,128)(2,1)S(1)} %get-tuple-element.40.q.q_ref, bf16[128,1024]{1,0:T(8,128)(2,1)S(1)} %get-tuple-element.41.kt.kt_ref, ...), custom_call_target="tpu_custom_call" | custom-call | flops 2000000000 | bytes 4194304 | tf_op jit(solution)/shard_map/fetch_stage/pallas_call | solution.py:283
  26.7 0.0 collective-permute-done.3.g0
  26.7 0.0 collective-permute-done.4.g1
  26.8 0.9 %collective-permute-done.5.g2 = bf16[2,160,128]{2,1,0:T(8,128)(2,1)S(1)} collective-permute-done((bf16[2,160,128]{2,1,0:T(8,128)(2,1)S(1)}, bf16[2,160,128]{2,1,0:T(8,128)(2,1)S(1)}, u32[]{:S(2)}, u32[]{:S(2)}) %collective-permute-start.5) | collective-permute-done | bytes 81952 | tf_op jit(solution)/shard_map/ppermute | solution.py:350
  27.6 0.1 shard_map.65
  27.7 2.8 %collective-permute-start.6 = (bf16[2,160,128]{2,1,0:T(8,128)(2,1)S(1)}, bf16[2,160,128]{2,1,0:T(8,128)(2,1)S(1)}, u32[]{:S(2)}, u32[]{:S(2)}) collective-permute-start(bf16[2,160,128]{2,1,0:T(8,128)(2,1)S(1)} %get-tuple-element.45.own), channel_id=1, source_target_pairs={{0,64},{32,96},{64,0},{96,32},{1,65},{33,97},{65,1},{97,33},{2,66}... | collective-permute-start | bytes 245768 | tf_op jit(solution)/shard_map/ppermute | solution.py:350
  30.6 0.3 collective-permute-start.7
  30.9 0.6 collective-permute-start.8
  31.4 1.1 %inner_stage.6 = (bf16[1024,160]{1,0:T(8,128)(2,1)S(1)}, f32[1024,256]{1,0:T(8,128)S(1)}) custom-call(bf16[1024,128]{1,0:T(8,128)(2,1)S(1)} %get-tuple-element.40.q.q_ref, bf16[128,1024]{1,0:T(8,128)(2,1)S(1)} %get-tuple-element.41.kt.kt_ref, bf16[4,1024,256]{2,1,0:T(8,128)(2,1)S(1)} %get-tuple-element.42.val.val_ref, ...), custom_call_target="tpu_custom_call" | custom-call | flops 1000000000 | bytes 2097152 | tf_op jit(solution)/shard_map/inner_stage/pallas_call | solution.py:213
  32.5 0.1 collective-permute-done.6.g0
  32.6 1.3 %collective-permute-done.7.g1 = bf16[2,160,128]{2,1,0:T(8,128)(2,1)S(1)} collective-permute-done((bf16[2,160,128]{2,1,0:T(8,128)(2,1)S(1)}, bf16[2,160,128]{2,1,0:T(8,128)(2,1)S(1)}, u32[]{:S(2)}, u32[]{:S(2)}) %collective-permute-start.7) | collective-permute-done | bytes 81952 | tf_op jit(solution)/shard_map/ppermute | solution.py:350
  33.9 1.5 %collective-permute-done.8.g2 = bf16[2,160,128]{2,1,0:T(8,128)(2,1)S(1)} collective-permute-done((bf16[2,160,128]{2,1,0:T(8,128)(2,1)S(1)}, bf16[2,160,128]{2,1,0:T(8,128)(2,1)S(1)}, u32[]{:S(2)}, u32[]{:S(2)}) %collective-permute-start.8) | collective-permute-done | bytes 81952 | tf_op jit(solution)/shard_map/ppermute | solution.py:350
  35.4 0.3 shard_map.66
  35.6 2.1 %collective-permute-start.9 = (bf16[2,160,128]{2,1,0:T(8,128)(2,1)S(1)}, bf16[2,160,128]{2,1,0:T(8,128)(2,1)S(1)}, u32[]{:S(2)}, u32[]{:S(2)}) collective-permute-start(bf16[2,160,128]{2,1,0:T(8,128)(2,1)S(1)} %get-tuple-element.47), channel_id=1, source_target_pairs={{0,4},{2,6},{4,0},{6,2},{1,5},{3,7},{5,1},{7,3},{8,12},{10,14},{12... | collective-permute-start | bytes 245768 | tf_op jit(solution)/shard_map/ppermute | solution.py:350
  37.8 0.8 %collective-permute-start.10 = (bf16[2,160,128]{2,1,0:T(8,128)(2,1)S(1)}, bf16[2,160,128]{2,1,0:T(8,128)(2,1)S(1)}, u32[]{:S(2)}, u32[]{:S(2)}) collective-permute-start(bf16[2,160,128]{2,1,0:T(8,128)(2,1)S(1)} %get-tuple-element.48), channel_id=1, source_target_pairs={{0,2},{2,0},{4,6},{6,4},{1,3},{3,1},{5,7},{7,5},{8,10},{10,8},{12,... | collective-permute-start | bytes 245768 | tf_op jit(solution)/shard_map/ppermute | solution.py:350
  38.6 1.1 %inner_stage.7 = (bf16[1024,160]{1,0:T(8,128)(2,1)S(1)}, f32[1024,256]{1,0:T(8,128)S(1)}) custom-call(bf16[1024,128]{1,0:T(8,128)(2,1)S(1)} %get-tuple-element.40.q.q_ref, bf16[128,1024]{1,0:T(8,128)(2,1)S(1)} %get-tuple-element.41.kt.kt_ref, bf16[4,1024,256]{2,1,0:T(8,128)(2,1)S(1)} %get-tuple-element.42.val.val_ref, ...), custom_call_target="tpu_custom_call" | custom-call | flops 1000000000 | bytes 2097152 | tf_op jit(solution)/shard_map/inner_stage/pallas_call | solution.py:213
  39.7 0.8 %collective-permute-done.9.refs_0_ = bf16[2,160,128]{2,1,0:T(8,128)(2,1)S(1)} collective-permute-done((bf16[2,160,128]{2,1,0:T(8,128)(2,1)S(1)}, bf16[2,160,128]{2,1,0:T(8,128)(2,1)S(1)}, u32[]{:S(2)}, u32[]{:S(2)}) %collective-permute-start.9) | collective-permute-done | bytes 81952 | tf_op jit(solution)/shard_map/ppermute | solution.py:350
  40.5 0.8 %collective-permute-done.10.refs_1_ = bf16[2,160,128]{2,1,0:T(8,128)(2,1)S(1)} collective-permute-done((bf16[2,160,128]{2,1,0:T(8,128)(2,1)S(1)}, bf16[2,160,128]{2,1,0:T(8,128)(2,1)S(1)}, u32[]{:S(2)}, u32[]{:S(2)}) %collective-permute-start.10) | collective-permute-done | bytes 81952 | tf_op jit(solution)/shard_map/ppermute | solution.py:350
  41.3 0.8 %outer_stage.3.refs_0_ = bf16[1024,512]{1,0:T(8,128)(2,1)S(1)} custom-call(bf16[2,160,128]{2,1,0:T(8,128)(2,1)S(1)} %collective-permute-done.9.refs_0_, bf16[2,160,128]{2,1,0:T(8,128)(2,1)S(1)} %collective-permute-done.10.refs_1_, bf16[1024,160]{1,0:T(8,128)(2,1)S(1)} %get-tuple-element.49.refs_2_, bf16[1024,160]{1,0:T(8,128)(2,1)S(1)} %get-tuple-element.50.refs_3_, ...), custom_call_target="tpu_custom_call" | custom-call | flops 600000000 | bytes 2097152 | tf_op jit(solution)/shard_map/outer_stage/pallas_call | solution.py:243
  42.1 5.6 %collective-permute-start.11 = (bf16[1024,512]{1,0:T(8,128)(2,1)S(1)}, bf16[1024,512]{1,0:T(8,128)(2,1)S(1)}, u32[]{:S(2)}, u32[]{:S(2)}) collective-permute-start(bf16[1024,512]{1,0:T(8,128)(2,1)S(1)} %outer_stage.3.refs_0_), channel_id=1, source_target_pairs={{0,1},{1,0},{2,3},{3,2},{4,5},{5,4},{6,7},{7,6},{8,9},{9,8},{10,11... | collective-permute-start | bytes 3145736 | tf_op jit(solution)/shard_map/ppermute | solution.py:446
  47.7 1.1 %inner_stage.10 = (bf16[1024,160]{1,0:T(8,128)(2,1)S(1)}, f32[1024,256]{1,0:T(8,128)S(1)}) custom-call(bf16[1024,128]{1,0:T(8,128)(2,1)S(1)} %get-tuple-element.40.q.q_ref, bf16[128,1024]{1,0:T(8,128)(2,1)S(1)} %get-tuple-element.41.kt.kt_ref, bf16[4,1024,256]{2,1,0:T(8,128)(2,1)S(1)} %get-tuple-element.42.val.val_ref, ...), custom_call_target="tpu_custom_call" | custom-call | flops 1000000000 | bytes 2097152 | tf_op jit(solution)/shard_map/inner_stage/pallas_call | solution.py:213
  48.8 1.1 %inner_stage.11 = (bf16[1024,160]{1,0:T(8,128)(2,1)S(1)}, f32[1024,256]{1,0:T(8,128)S(1)}) custom-call(bf16[1024,128]{1,0:T(8,128)(2,1)S(1)} %get-tuple-element.40.q.q_ref, bf16[128,1024]{1,0:T(8,128)(2,1)S(1)} %get-tuple-element.41.kt.kt_ref, bf16[4,1024,256]{2,1,0:T(8,128)(2,1)S(1)} %get-tuple-element.42.val.val_ref, ...), custom_call_target="tpu_custom_call" | custom-call | flops 1000000000 | bytes 2097152 | tf_op jit(solution)/shard_map/inner_stage/pallas_call | solution.py:213
  49.9 0.5 outer_stage.5.refs_0_
  50.4 0.1 collective-permute-start.14
  50.5 1.1 %inner_stage.8 = (bf16[1024,160]{1,0:T(8,128)(2,1)S(1)}, f32[1024,256]{1,0:T(8,128)S(1)}) custom-call(bf16[1024,128]{1,0:T(8,128)(2,1)S(1)} %get-tuple-element.40.q.q_ref, bf16[128,1024]{1,0:T(8,128)(2,1)S(1)} %get-tuple-element.41.kt.kt_ref, bf16[4,1024,256]{2,1,0:T(8,128)(2,1)S(1)} %get-tuple-element.42.val.val_ref, ...), custom_call_target="tpu_custom_call" | custom-call | flops 1000000000 | bytes 2097152 | tf_op jit(solution)/shard_map/inner_stage/pallas_call | solution.py:213
  51.6 1.2 %collective-permute-start.12 = (bf16[2,160,128]{2,1,0:T(8,128)(2,1)S(1)}, bf16[2,160,128]{2,1,0:T(8,128)(2,1)S(1)}, u32[]{:S(2)}, u32[]{:S(2)}) collective-permute-start(bf16[2,160,128]{2,1,0:T(8,128)(2,1)S(1)} %get-tuple-element.57), channel_id=1, source_target_pairs={{0,6},{2,4},{4,2},{6,0},{1,7},{3,5},{5,3},{7,1},{8,14},{10,12},{12... | collective-permute-start | bytes 245768 | tf_op jit(solution)/shard_map/ppermute | solution.py:350
  52.8 1.1 %inner_stage.9 = (bf16[1024,160]{1,0:T(8,128)(2,1)S(1)}, f32[1024,256]{1,0:T(8,128)S(1)}) custom-call(bf16[1024,128]{1,0:T(8,128)(2,1)S(1)} %get-tuple-element.40.q.q_ref, bf16[128,1024]{1,0:T(8,128)(2,1)S(1)} %get-tuple-element.41.kt.kt_ref, bf16[4,1024,256]{2,1,0:T(8,128)(2,1)S(1)} %get-tuple-element.42.val.val_ref, ...), custom_call_target="tpu_custom_call" | custom-call | flops 1000000000 | bytes 2097152 | tf_op jit(solution)/shard_map/inner_stage/pallas_call | solution.py:213
  53.9 2.3 %collective-permute-done.12.refs_0_ = bf16[2,160,128]{2,1,0:T(8,128)(2,1)S(1)} collective-permute-done((bf16[2,160,128]{2,1,0:T(8,128)(2,1)S(1)}, bf16[2,160,128]{2,1,0:T(8,128)(2,1)S(1)}, u32[]{:S(2)}, u32[]{:S(2)}) %collective-permute-start.12) | collective-permute-done | bytes 81952 | tf_op jit(solution)/shard_map/ppermute | solution.py:350
  56.2 0.5 outer_stage.4.refs_1_
  56.7 1.7 %collective-permute-start.13 = (bf16[1024,256]{1,0:T(8,128)(2,1)S(1)}, bf16[1024,256]{1,0:T(8,128)(2,1)S(1)}, u32[]{:S(2)}, u32[]{:S(2)}) collective-permute-start(bf16[1024,256]{1,0:T(8,128)(2,1)S(1)} %outer_stage.4.refs_1_), channel_id=1, source_target_pairs={{0,1},{1,0},{2,3},{3,2},{4,5},{5,4},{6,7},{7,6},{8,9},{9,8},{10,11... | collective-permute-start | bytes 1572872 | tf_op jit(solution)/shard_map/ppermute | solution.py:446
  58.4 0.7 %out_stage.3.refs_4_ = f32[1024,1024]{1,0:T(8,128)S(1)} custom-call(bf16[1024,256]{1,0:T(8,128)(2,1)S(1)} %outer_stage.5.refs_0_, bf16[2,1024,1024]{2,1,0:T(8,128)(2,1)S(1)} %get-tuple-element.44.columns.refs_1_.refs_3_.refs_2_), custom_call_target="tpu_custom_call" | custom-call | flops 536870912 | bytes 1048576 | tf_op jit(solution)/shard_map/out_stage/pallas_call | solution.py:332
  59.2 0.0 collective-permute-done.14.refs_2_
  59.2 2.3 %out_stage.4.refs_3_ = f32[1024,1024]{1,0:T(8,128)S(1)} custom-call(bf16[1024,512]{1,0:T(8,128)(2,1)S(1)} %outer_stage.3.refs_0_, bf16[1024,256]{1,0:T(8,128)(2,1)S(1)} %outer_stage.4.refs_1_, bf16[1024,256]{1,0:T(8,128)(2,1)S(1)} %collective-permute-done.14.refs_2_, bf16[2,1024,1024]{2,1,0:T(8,128)(2,1)S(1)} %get-tuple-element.44.columns.refs_1_.refs_3_.refs_2_, ...), custom_call_target="tpu_custom_call" | custom-call | flops 2147483648 | bytes 1048576 | tf_op jit(solution)/shard_map/out_stage/pallas_call | solution.py:332
  61.5 0.0 collective-permute-done.13.refs_1_
  61.5 0.0 collective-permute-done.11.refs_0_
  61.5 2.6 %out_stage.5 = bf16[1024,1024]{1,0:T(8,128)(2,1)} custom-call(bf16[1024,512]{1,0:T(8,128)(2,1)S(1)} %collective-permute-done.11.refs_0_, bf16[1024,256]{1,0:T(8,128)(2,1)S(1)} %collective-permute-done.13.refs_1_, bf16[2,1024,1024]{2,1,0:T(8,128)(2,1)S(1)} %get-tuple-element.44.columns.refs_1_.refs_3_.refs_2_, f32[1024,1024]{1,0:T(8,128)S(1)} %out_stage.4.refs_3_), custom_call_target="tpu_custom_call" | custom-call | flops 1610612736 | bytes 1048576 | tf_op jit(solution)/shard_map/out_stage/pallas_call | solution.py:332
  (1 shorter events, 0.0 us)
Async XLA Ops:
  0.0 22.8 %copy-start = (f32[8,160]{1,0:T(8,128)S(1)}, f32[8,160]{1,0:T(8,128)}, u32[]{:S(2)}) copy-start(f32[8,160]{1,0:T(8,128)} %constant.2.clone.table.table_ref) | copy-start | bytes 15364
  9.3 6.6 %collective-permute-start = (bf16[2,160,128]{2,1,0:T(8,128)(2,1)S(1)}, bf16[2,160,128]{2,1,0:T(8,128)(2,1)S(1)}, u32[]{:S(2)}, u32[]{:S(2)}) collective-permute-start(bf16[2,160,128]{2,1,0:T(8,128)(2,1)S(1)} %get-tuple-element.37), channel_id=1, source_target_pairs={{0,4},{2,6},{4,0},{6,2},{1,5},{3,7},{5,1},{7,3},{8,12},{10,14},{12... | collective-permute-start | bytes 245768 | tf_op jit(solution)/shard_map/ppermute | solution.py:350
  13.8 4.1 %collective-permute-start.1 = (bf16[2,160,128]{2,1,0:T(8,128)(2,1)S(1)}, bf16[2,160,128]{2,1,0:T(8,128)(2,1)S(1)}, u32[]{:S(2)}, u32[]{:S(2)}) collective-permute-start(bf16[2,160,128]{2,1,0:T(8,128)(2,1)S(1)} %get-tuple-element.38), channel_id=1, source_target_pairs={{0,2},{2,0},{4,6},{6,4},{1,3},{3,1},{5,7},{7,5},{8,10},{10,8},{12,... | collective-permute-start | bytes 245768 | tf_op jit(solution)/shard_map/ppermute | solution.py:350
  14.5 4.5 %collective-permute-start.2 = (bf16[2,160,128]{2,1,0:T(8,128)(2,1)S(1)}, bf16[2,160,128]{2,1,0:T(8,128)(2,1)S(1)}, u32[]{:S(2)}, u32[]{:S(2)}) collective-permute-start(bf16[2,160,128]{2,1,0:T(8,128)(2,1)S(1)} %get-tuple-element.39), channel_id=1, source_target_pairs={{0,6},{2,4},{4,2},{6,0},{1,7},{3,5},{5,3},{7,1},{8,14},{10,12},{12... | collective-permute-start | bytes 245768 | tf_op jit(solution)/shard_map/ppermute | solution.py:350
  19.0 7.7 %collective-permute-start.3 = (bf16[2,160,128]{2,1,0:T(8,128)(2,1)S(1)}, bf16[2,160,128]{2,1,0:T(8,128)(2,1)S(1)}, u32[]{:S(2)}, u32[]{:S(2)}) collective-permute-start(bf16[2,160,128]{2,1,0:T(8,128)(2,1)S(1)} %shard_map.64.own), channel_id=1, source_target_pairs={{0,16},{8,24},{16,0},{24,8},{1,17},{9,25},{17,1},{25,9},{2,18},{10... | collective-permute-start | bytes 245768 | tf_op jit(solution)/shard_map/ppermute | solution.py:350
  22.0 4.7 %collective-permute-start.4 = (bf16[2,160,128]{2,1,0:T(8,128)(2,1)S(1)}, bf16[2,160,128]{2,1,0:T(8,128)(2,1)S(1)}, u32[]{:S(2)}, u32[]{:S(2)}) collective-permute-start(bf16[2,160,128]{2,1,0:T(8,128)(2,1)S(1)} %shard_map.64.own), channel_id=1, source_target_pairs={{0,8},{8,0},{16,24},{24,16},{1,9},{9,1},{17,25},{25,17},{2,10},{10... | collective-permute-start | bytes 245768 | tf_op jit(solution)/shard_map/ppermute | solution.py:350
  22.4 5.2 %collective-permute-start.5 = (bf16[2,160,128]{2,1,0:T(8,128)(2,1)S(1)}, bf16[2,160,128]{2,1,0:T(8,128)(2,1)S(1)}, u32[]{:S(2)}, u32[]{:S(2)}) collective-permute-start(bf16[2,160,128]{2,1,0:T(8,128)(2,1)S(1)} %shard_map.64.own), channel_id=1, source_target_pairs={{0,24},{8,16},{16,8},{24,0},{1,25},{9,17},{17,9},{25,1},{2,26},{10... | collective-permute-start | bytes 245768 | tf_op jit(solution)/shard_map/ppermute | solution.py:350
  27.7 4.9 %collective-permute-start.6 = (bf16[2,160,128]{2,1,0:T(8,128)(2,1)S(1)}, bf16[2,160,128]{2,1,0:T(8,128)(2,1)S(1)}, u32[]{:S(2)}, u32[]{:S(2)}) collective-permute-start(bf16[2,160,128]{2,1,0:T(8,128)(2,1)S(1)} %get-tuple-element.45.own), channel_id=1, source_target_pairs={{0,64},{32,96},{64,0},{96,32},{1,65},{33,97},{65,1},{97,33},{2,66}... | collective-permute-start | bytes 245768 | tf_op jit(solution)/shard_map/ppermute | solution.py:350
  30.6 3.3 %collective-permute-start.7 = (bf16[2,160,128]{2,1,0:T(8,128)(2,1)S(1)}, bf16[2,160,128]{2,1,0:T(8,128)(2,1)S(1)}, u32[]{:S(2)}, u32[]{:S(2)}) collective-permute-start(bf16[2,160,128]{2,1,0:T(8,128)(2,1)S(1)} %get-tuple-element.45.own), channel_id=1, source_target_pairs={{0,32},{32,0},{64,96},{96,64},{1,33},{33,1},{65,97},{97,65},{2,34}... | collective-permute-start | bytes 245768 | tf_op jit(solution)/shard_map/ppermute | solution.py:350
  30.9 4.5 %collective-permute-start.8 = (bf16[2,160,128]{2,1,0:T(8,128)(2,1)S(1)}, bf16[2,160,128]{2,1,0:T(8,128)(2,1)S(1)}, u32[]{:S(2)}, u32[]{:S(2)}) collective-permute-start(bf16[2,160,128]{2,1,0:T(8,128)(2,1)S(1)} %get-tuple-element.45.own), channel_id=1, source_target_pairs={{0,96},{32,64},{64,32},{96,0},{1,97},{33,65},{65,33},{97,1},{2,98}... | collective-permute-start | bytes 245768 | tf_op jit(solution)/shard_map/ppermute | solution.py:350
  35.6 4.9 %collective-permute-start.9 = (bf16[2,160,128]{2,1,0:T(8,128)(2,1)S(1)}, bf16[2,160,128]{2,1,0:T(8,128)(2,1)S(1)}, u32[]{:S(2)}, u32[]{:S(2)}) collective-permute-start(bf16[2,160,128]{2,1,0:T(8,128)(2,1)S(1)} %get-tuple-element.47), channel_id=1, source_target_pairs={{0,4},{2,6},{4,0},{6,2},{1,5},{3,7},{5,1},{7,3},{8,12},{10,14},{12... | collective-permute-start | bytes 245768 | tf_op jit(solution)/shard_map/ppermute | solution.py:350
  37.8 3.5 %collective-permute-start.10 = (bf16[2,160,128]{2,1,0:T(8,128)(2,1)S(1)}, bf16[2,160,128]{2,1,0:T(8,128)(2,1)S(1)}, u32[]{:S(2)}, u32[]{:S(2)}) collective-permute-start(bf16[2,160,128]{2,1,0:T(8,128)(2,1)S(1)} %get-tuple-element.48), channel_id=1, source_target_pairs={{0,2},{2,0},{4,6},{6,4},{1,3},{3,1},{5,7},{7,5},{8,10},{10,8},{12,... | collective-permute-start | bytes 245768 | tf_op jit(solution)/shard_map/ppermute | solution.py:350
  42.1 19.4 %collective-permute-start.11 = (bf16[1024,512]{1,0:T(8,128)(2,1)S(1)}, bf16[1024,512]{1,0:T(8,128)(2,1)S(1)}, u32[]{:S(2)}, u32[]{:S(2)}) collective-permute-start(bf16[1024,512]{1,0:T(8,128)(2,1)S(1)} %outer_stage.3.refs_0_), channel_id=1, source_target_pairs={{0,1},{1,0},{2,3},{3,2},{4,5},{5,4},{6,7},{7,6},{8,9},{9,8},{10,11... | collective-permute-start | bytes 3145736 | tf_op jit(solution)/shard_map/ppermute | solution.py:446
  50.4 8.8 %collective-permute-start.14 = (bf16[1024,256]{1,0:T(8,128)(2,1)S(1)}, bf16[1024,256]{1,0:T(8,128)(2,1)S(1)}, u32[]{:S(2)}, u32[]{:S(2)}) collective-permute-start(bf16[1024,256]{1,0:T(8,128)(2,1)S(1)} %outer_stage.5.refs_0_), channel_id=1, source_target_pairs={{0,1},{1,0},{2,3},{3,2},{4,5},{5,4},{6,7},{7,6},{8,9},{9,8},{10,11... | collective-permute-start | bytes 1572872 | tf_op jit(solution)/shard_map/ppermute | solution.py:446
  51.6 4.6 %collective-permute-start.12 = (bf16[2,160,128]{2,1,0:T(8,128)(2,1)S(1)}, bf16[2,160,128]{2,1,0:T(8,128)(2,1)S(1)}, u32[]{:S(2)}, u32[]{:S(2)}) collective-permute-start(bf16[2,160,128]{2,1,0:T(8,128)(2,1)S(1)} %get-tuple-element.57), channel_id=1, source_target_pairs={{0,6},{2,4},{4,2},{6,0},{1,7},{3,5},{5,3},{7,1},{8,14},{10,12},{12... | collective-permute-start | bytes 245768 | tf_op jit(solution)/shard_map/ppermute | solution.py:350
  56.7 4.8 %collective-permute-start.13 = (bf16[1024,256]{1,0:T(8,128)(2,1)S(1)}, bf16[1024,256]{1,0:T(8,128)(2,1)S(1)}, u32[]{:S(2)}, u32[]{:S(2)}) collective-permute-start(bf16[1024,256]{1,0:T(8,128)(2,1)S(1)} %outer_stage.4.refs_1_), channel_id=1, source_target_pairs={{0,1},{1,0},{2,3},{3,2},{4,5},{5,4},{6,7},{7,6},{8,9},{9,8},{10,11... | collective-permute-start | bytes 1572872 | tf_op jit(solution)/shard_map/ppermute | solution.py:446

commit v4 on v3

--- a/solution.py
+++ b/solution.py
@@ -15,11 +15,10 @@
 SEQ = ("seq_0", "seq_1", "seq_2")
 STEPS = (2, 1, 3)
 MIB = 2**20
-HEAD_LIMIT, OUT_LIMIT = (48 * MIB, 20 * MIB)
+HEAD_LIMIT, OUT_LIMIT = (40 * MIB, 20 * MIB)
 SLOTS = (0, 2, 1, 3)
 OUT_STEPS = (0, 2, 1, 3)
 GROUPS = ((0,), (2, 1), (3,))
-FETCH_STEP = 2
 F32, BF16 = (jnp.float32, jnp.bfloat16)
 VMEM = pl.BlockSpec(memory_space=pltpu.VMEM)
 SMEM = pl.BlockSpec(memory_space=pltpu.SMEM)
@@ -71,10 +70,23 @@
     return jnp.where(row == 1, top, jnp.where(row == 2, low, 0.0))
 
 
+def fetch_copies(w_hbm, out, sem):
+    own = lax.axis_index("head")
+    cols = pl.ds(pl.multiple_of(own * 1024, 1024), 1024)
+    copies = []
+    for half in range(2):
+        for s in range(4):
+            row = (own ^ half) * 1024 + quarter_of(OUT_STEPS[s]) * 256
+            source = w_hbm.at[pl.ds(pl.multiple_of(row, 256), 256), cols]
+            target = out.at[half, pl.ds(s * 256, 256)]
+            copies.append(pltpu.make_async_copy(source, target, sem.at[half * 4 + s]))
+    return copies
+
+
 def head_kernel(
-    x_hbm, wk_hbm, wq_hbm, wv_hbm,
-    q_out, kt_out, val_out, local_out, s0, s1, s2, s3,
-    x, wkq, wv, acc, kt, x_sem, w_sem, v_sem,
+    x_hbm, wk_hbm, wq_hbm, wv_hbm, out_hbm,
+    q_out, kt_out, val_out, local_out, s0, s1, s2, s3, columns,
+    x, wkq, wv, acc, kt, x_sem, w_sem, v_sem, c_sem,
 ):
     tok, width = x.shape
     cuts = 4
@@ -113,6 +125,9 @@
         for rows in (slice(0, tok // 2), slice(tok // 2, tok)):
             part = mm(x[rows, cols], both)
             acc[rows] = part if j == 0 else acc[rows] + part
+    fetches = fetch_copies(out_hbm, columns, c_sem)
+    for fetch in fetches:
+        fetch.start()
     q_out[...] = acc[:, kd:].astype(BF16)
     keys = jnp.transpose(acc[:, :kd].astype(BF16).astype(F32))
     kt[...] = keys
@@ -140,9 +155,11 @@
             extra = norm_rows(run[:, 128:])
             row = lax.broadcasted_iota(jnp.int32, (8, 128), 0)
             state[h, 152:] = jnp.where(row == 0, run[152:, :128], extra).astype(BF16)
-
-
-def head_stage(tokens, w_key, w_query, w_value):
+    for fetch in fetches:
+        fetch.wait()
+
+
+def head_stage(tokens, w_key, w_query, w_value, w_out):
     tok, width = tokens.shape
     kd = w_key.shape[1]
     chunks = tok // CHUNK
@@ -155,9 +172,10 @@
             shape((4, tok, 256), BF16),
             shape((4, 2, chunks - 1, ROWS, 256), BF16),
         ]
-        + [shape((2, ROWS, 128), BF16)] * 4,
-        in_specs=[ANY] * 4,
-        out_specs=[VMEM] * 8,
+        + [shape((2, ROWS, 128), BF16)] * 4
+        + [shape((2, 1024, 1024), BF16)],
+        in_specs=[ANY] * 5,
+        out_specs=[VMEM] * 9,
         scratch_shapes=[
             pltpu.VMEM((tok, width), BF16),
             pltpu.VMEM((2, width, kd), BF16),
@@ -167,13 +185,14 @@
             pltpu.SemaphoreType.DMA((4,)),
             pltpu.SemaphoreType.DMA((8,)),
             pltpu.SemaphoreType.DMA((4,)),
+            pltpu.SemaphoreType.DMA((8,)),
         ],
         compiler_params=pltpu.CompilerParams(vmem_limit_bytes=HEAD_LIMIT),
         cost_estimate=pl.CostEstimate(
             flops=6 * 10**9, bytes_accessed=12 * 2**20, transcendentals=0
         ),
         name="head_stage",
-    )(tokens, w_key, w_query, w_value)
+    )(tokens, w_key, w_query, w_value, w_out)
 
 
 def inner_kernel(slot, h, q_ref, kt_ref, val_ref, local_ref, table_ref, feat_out, part_out):
@@ -253,49 +272,6 @@
     )(*prefixes, *feats, *parts)
 
 
-def fetch_copies(w_hbm, out, sem):
-    own = lax.axis_index("head")
-    cols = pl.ds(pl.multiple_of(own * 1024, 1024), 1024)
-    copies = []
-    for half in range(2):
-        for s in range(4):
-            row = (own ^ half) * 1024 + quarter_of(OUT_STEPS[s]) * 256
-            source = w_hbm.at[pl.ds(pl.multiple_of(row, 256), 256), cols]
-            target = out.at[half, pl.ds(s * 256, 256)]
-            copies.append(pltpu.make_async_copy(source, target, sem.at[half * 4 + s]))
-    return copies
-
-
-def fetch_kernel(slot, q, kt, val, local, table, w_hbm, *rest):
-    *outs, columns, sem = rest
-    copies = fetch_copies(w_hbm, columns, sem)
-    for copy in copies:
-        copy.start()
-    for h in range(2):
-        inner_kernel(slot, h, q, kt, val, local, table, *outs[2 * h : 2 * h + 2])
-    for copy in copies:
-        copy.wait()
-
-
-def fetch_stage(slot, *args):
-    tok = args[0].shape[0]
-    shape = jax.ShapeDtypeStruct
-    *outs, columns = pl.pallas_call(
-        functools.partial(fetch_kernel, slot),
-        out_shape=[shape((tok, ROWS), BF16), shape((tok, 256), F32)] * 2
-        + [shape((2, 1024, 1024), BF16)],
-        in_specs=[VMEM] * 5 + [ANY],
-        out_specs=[VMEM] * 5,
-        scratch_shapes=[pltpu.SemaphoreType.DMA((8,))],
-        compiler_params=pltpu.CompilerParams(vmem_limit_bytes=16 * MIB),
-        cost_estimate=pl.CostEstimate(
-            flops=2 * 10**9, bytes_accessed=4 * MIB, transcendentals=0
-        ),
-        name="fetch_stage",
-    )(*args)
-    return outs[:2], outs[2:], columns
-
-
 def out_kernel(places, last, *refs):
     count = len(places)
     groups, (w_ref, *rest) = (refs[:count], refs[count:])
@@ -380,28 +356,28 @@
         out[...] = run.astype(BF16)
 
 
-def small_call(kernel, outs, *args, scratch=(), after=()):
+def small_call(kernel, outs, *args, scratch=()):
     shape = args[0].shape
     return pl.pallas_call(
         kernel,
         out_shape=[jax.ShapeDtypeStruct(shape, kind) for kind in outs],
-        in_specs=[VMEM] * len(args) + [ANY] * len(after),
+        in_specs=[VMEM] * len(args),
         out_specs=[VMEM] * len(outs),
         scratch_shapes=list(scratch),
         compiler_params=pltpu.CompilerParams(vmem_limit_bytes=4 * 2**20),
         cost_estimate=pl.CostEstimate(flops=10**6, bytes_accessed=2**20, transcendentals=0),
-    )(*args, *after)
-
-
-def middle_kernel(own, g0, g1, g2, columns, total, base):
+    )(*args)
+
+
+def middle_kernel(own, g0, g1, g2, total, base):
     level_kernel(SEQ[1], own, g0, g1, g2, None, total, base)
 
 
-def exclusive_prefix(states, columns):
+def exclusive_prefix(states):
     parts = [states[0]] + [partner(state, SEQ[2], step) for step, state in zip(STEPS, states[1:])]
     (low,) = small_call(total_kernel, [BF16], *parts)
     got = [partner(low, SEQ[1], step) for step in STEPS]
-    total, base = small_call(middle_kernel, [BF16, F32], low, *got, after=[columns])
+    total, base = small_call(middle_kernel, [BF16, F32], low, *got)
     got = [partner(total, SEQ[0], step) for step in STEPS]
     scratch = [pltpu.VMEM(low.shape, F32)]
     outs = small_call(spread_kernel, [BF16] * 4, total, *got, base, *parts, scratch=scratch)
@@ -417,17 +393,15 @@
         for x in (tokens, w_query, w_key, w_value, w_out)
     )
     table = jnp.asarray(feature_tables())
-    q, kt, val, local, *states = head_stage(tokens, w_key, w_query, w_value)
+    q, kt, val, local, *states, columns = head_stage(
+        tokens, w_key, w_query, w_value, w_out
+    )
     inner = {}
     args = (q, kt, val, local, table)
     for slot, step in enumerate(SLOTS):
-        if step == FETCH_STEP:
-            *pair, columns = fetch_stage(slot, *args, w_out)
-            inner[step, 0], inner[step, 1] = pair
-            continue
         for h in range(2):
             inner[step, h] = inner_stage(slot, h, *args)
-    back = exclusive_prefix(states, columns)
+    back = exclusive_prefix(states)
 
     def outer(steps):
         return outer_stage(

time: 64.4 us -> 64.5 us (level)
  waiting for transfers between devices: 12.1 us -> 13.8 us
  Pallas kernels: 27.7 us -> 26 us
    pallas_call x1 -> x0, Pallas kernels: 3.91 us -> none  [fetch_stage(): pl.pallas_call(functools.partial(fetch_kernel, slot), out_shape=[shape((t...]
    pallas_call x6 -> x8, Pallas kernels: 6.6 us -> 8.8 us  [inner_stage(): pl.pallas_call(functools.partial(inner_kernel, slot, h), out_shape=[shape...]
    ppermute x12, waiting for transfers between devices: 12.1 us -> 13.8 us  [partner(): return lax.ppermute(x, axis, pairs)]
  transfers between devices with their start and end apart: 15 -> 15, of which waited for: 10 -> 11; matrix products, arithmetic and copies ran while one was open for 0% -> 0% of each run, Pallas kernels for 23% -> 20%
where the time goes in v4:
time: 64.5 us; the launch traced here: 64.4 us
  Pallas kernels  26 us (40%)
  starting transfers between devices  24.3 us (38%)
  waiting for transfers between devices  13.8 us (21%)
    ppermute x12, starting transfers between devices, partner(): return lax.ppermute(x, axis, pairs)  16.9 us
    ppermute x12, waiting for transfers between devices, partner(): return lax.ppermute(x, axis, pairs)  13.8 us
    pallas_call x1, Pallas kernels, head_stage(): pl.pallas_call(head_kernel, out_shape=[shape((tok, kd), BF16), shape((kd,...  9.34 us
    pallas_call x8, Pallas kernels, inner_stage(): pl.pallas_call(functools.partial(inner_kernel, slot, h), out_shape=[shape...  8.8 us
    ppermute x3, starting transfers between devices, per_device(): other.append(lax.ppermute(own[-1], 'head', [(0, 1), (1, 0)]))  7.4 us
    pallas_call x3, Pallas kernels, out_stage(): pl.pallas_call(functools.partial(out_kernel, places, last), out_shape=jax...  5.67 us
    pallas_call x3, Pallas kernels, outer_stage(): pl.pallas_call(functools.partial(outer_kernel, count), out_shape=jax.Shap...  1.83 us
  transfers between devices with their start and end apart: 15, of which 11 were waited for; matrix products, arithmetic and copies ran while one was open for 0% of the time, Pallas kernels for 20%

profile of v4, /device:TPU:1, one launch (start us, length us, event | category | flops | bytes accessed | tf_op | source)
XLA Modules:
  0.0 64.4 jit_solution(1194515566445354478)
XLA Ops:
  0.0 0.0 copy-start
  0.0 9.3 %head_stage.1 = (bf16[1024,128]{1,0:T(8,128)(2,1)S(1)}, bf16[128,1024]{1,0:T(8,128)(2,1)S(1)}, bf16[4,1024,256]{2,1,0:T(8,128)(2,1)S(1)}, bf16[4,2,3,160,256]{4,...) custom-call(bf16[1024,2048]{1,0:T(8,128)(2,1)} %x_hbm.1, ...), custom_call_target="tpu_custom_call" | custom-call | flops 6000000000 | bytes 12582912 | tf_op jit(solution)/shard_map/head_stage/pallas_call | solution.py:167
  9.4 4.5 %collective-permute-start = (bf16[2,160,128]{2,1,0:T(8,128)(2,1)S(1)}, bf16[2,160,128]{2,1,0:T(8,128)(2,1)S(1)}, u32[]{:S(2)}, u32[]{:S(2)}) collective-permute-start(bf16[2,160,128]{2,1,0:T(8,128)(2,1)S(1)} %get-tuple-element.37), channel_id=1, source_target_pairs={{0,4},{2,6},{4,0},{6,2},{1,5},{3,7},{5,1},{7,3},{8,12},{10,14},{12... | collective-permute-start | bytes 245768 | tf_op jit(solution)/shard_map/ppermute | solution.py:326
  13.8 0.7 %collective-permute-start.1 = (bf16[2,160,128]{2,1,0:T(8,128)(2,1)S(1)}, bf16[2,160,128]{2,1,0:T(8,128)(2,1)S(1)}, u32[]{:S(2)}, u32[]{:S(2)}) collective-permute-start(bf16[2,160,128]{2,1,0:T(8,128)(2,1)S(1)} %get-tuple-element.38), channel_id=1, source_target_pairs={{0,2},{2,0},{4,6},{6,4},{1,3},{3,1},{5,7},{7,5},{8,10},{10,8},{12,... | collective-permute-start | bytes 245768 | tf_op jit(solution)/shard_map/ppermute | solution.py:326
  14.6 0.0 collective-permute-start.2
  14.6 0.0 copy-done
  14.6 1.1 %inner_stage.8 = (bf16[1024,160]{1,0:T(8,128)(2,1)S(1)}, f32[1024,256]{1,0:T(8,128)S(1)}) custom-call(bf16[1024,128]{1,0:T(8,128)(2,1)S(1)} %get-tuple-element.44.q_ref, bf16[128,1024]{1,0:T(8,128)(2,1)S(1)} %get-tuple-element.45.kt_ref, bf16[4,1024,256]{2,1,0:T(8,128)(2,1)S(1)} %get-tuple-element.46.val_ref, ...), custom_call_target="tpu_custom_call" | custom-call | flops 1000000000 | bytes 2097152 | tf_op jit(solution)/shard_map/inner_stage/pallas_call | solution.py:232
  15.7 0.3 collective-permute-done.p1
  16.0 1.9 %collective-permute-done.1.p2 = bf16[2,160,128]{2,1,0:T(8,128)(2,1)S(1)} collective-permute-done((bf16[2,160,128]{2,1,0:T(8,128)(2,1)S(1)}, bf16[2,160,128]{2,1,0:T(8,128)(2,1)S(1)}, u32[]{:S(2)}, u32[]{:S(2)}) %collective-permute-start.1) | collective-permute-done | bytes 81952 | tf_op jit(solution)/shard_map/ppermute | solution.py:326
  17.9 1.2 %collective-permute-done.2.p3 = bf16[2,160,128]{2,1,0:T(8,128)(2,1)S(1)} collective-permute-done((bf16[2,160,128]{2,1,0:T(8,128)(2,1)S(1)}, bf16[2,160,128]{2,1,0:T(8,128)(2,1)S(1)}, u32[]{:S(2)}, u32[]{:S(2)}) %collective-permute-start.2) | collective-permute-done | bytes 81952 | tf_op jit(solution)/shard_map/ppermute | solution.py:326
  19.1 3.0 %collective-permute-start.3 = (bf16[2,160,128]{2,1,0:T(8,128)(2,1)S(1)}, bf16[2,160,128]{2,1,0:T(8,128)(2,1)S(1)}, u32[]{:S(2)}, u32[]{:S(2)}) collective-permute-start(bf16[2,160,128]{2,1,0:T(8,128)(2,1)S(1)} %shard_map.64.own), channel_id=1, source_target_pairs={{0,16},{8,24},{16,0},{24,8},{1,17},{9,25},{17,1},{25,9},{2,18},{10... | collective-permute-start | bytes 245768 | tf_op jit(solution)/shard_map/ppermute | solution.py:326
  22.1 0.4 collective-permute-start.4
  22.5 0.4 collective-permute-start.5
  22.9 1.1 %inner_stage.9 = (bf16[1024,160]{1,0:T(8,128)(2,1)S(1)}, f32[1024,256]{1,0:T(8,128)S(1)}) custom-call(bf16[1024,128]{1,0:T(8,128)(2,1)S(1)} %get-tuple-element.44.q_ref, bf16[128,1024]{1,0:T(8,128)(2,1)S(1)} %get-tuple-element.45.kt_ref, bf16[4,1024,256]{2,1,0:T(8,128)(2,1)S(1)} %get-tuple-element.46.val_ref, ...), custom_call_target="tpu_custom_call" | custom-call | flops 1000000000 | bytes 2097152 | tf_op jit(solution)/shard_map/inner_stage/pallas_call | solution.py:232
  24.0 0.0 collective-permute-done.3.g0
  24.0 1.4 %collective-permute-done.4.g1 = bf16[2,160,128]{2,1,0:T(8,128)(2,1)S(1)} collective-permute-done((bf16[2,160,128]{2,1,0:T(8,128)(2,1)S(1)}, bf16[2,160,128]{2,1,0:T(8,128)(2,1)S(1)}, u32[]{:S(2)}, u32[]{:S(2)}) %collective-permute-start.4) | collective-permute-done | bytes 81952 | tf_op jit(solution)/shard_map/ppermute | solution.py:326
  25.4 2.3 %collective-permute-done.5.g2 = bf16[2,160,128]{2,1,0:T(8,128)(2,1)S(1)} collective-permute-done((bf16[2,160,128]{2,1,0:T(8,128)(2,1)S(1)}, bf16[2,160,128]{2,1,0:T(8,128)(2,1)S(1)}, u32[]{:S(2)}, u32[]{:S(2)}) %collective-permute-start.5) | collective-permute-done | bytes 81952 | tf_op jit(solution)/shard_map/ppermute | solution.py:326
  27.7 0.1 shard_map.65
  27.8 2.8 %collective-permute-start.6 = (bf16[2,160,128]{2,1,0:T(8,128)(2,1)S(1)}, bf16[2,160,128]{2,1,0:T(8,128)(2,1)S(1)}, u32[]{:S(2)}, u32[]{:S(2)}) collective-permute-start(bf16[2,160,128]{2,1,0:T(8,128)(2,1)S(1)} %get-tuple-element.40.own), channel_id=1, source_target_pairs={{0,64},{32,96},{64,0},{96,32},{1,65},{33,97},{65,1},{97,33},{2,66}... | collective-permute-start | bytes 245768 | tf_op jit(solution)/shard_map/ppermute | solution.py:326
  30.6 0.3 collective-permute-start.7
  30.9 0.6 collective-permute-start.8
  31.5 1.1 %inner_stage.10 = (bf16[1024,160]{1,0:T(8,128)(2,1)S(1)}, f32[1024,256]{1,0:T(8,128)S(1)}) custom-call(bf16[1024,128]{1,0:T(8,128)(2,1)S(1)} %get-tuple-element.44.q_ref, bf16[128,1024]{1,0:T(8,128)(2,1)S(1)} %get-tuple-element.45.kt_ref, bf16[4,1024,256]{2,1,0:T(8,128)(2,1)S(1)} %get-tuple-element.46.val_ref, ...), custom_call_target="tpu_custom_call" | custom-call | flops 1000000000 | bytes 2097152 | tf_op jit(solution)/shard_map/inner_stage/pallas_call | solution.py:232
  32.6 0.1 collective-permute-done.6.g0
  32.7 1.3 %collective-permute-done.7.g1 = bf16[2,160,128]{2,1,0:T(8,128)(2,1)S(1)} collective-permute-done((bf16[2,160,128]{2,1,0:T(8,128)(2,1)S(1)}, bf16[2,160,128]{2,1,0:T(8,128)(2,1)S(1)}, u32[]{:S(2)}, u32[]{:S(2)}) %collective-permute-start.7) | collective-permute-done | bytes 81952 | tf_op jit(solution)/shard_map/ppermute | solution.py:326
  33.9 1.5 %collective-permute-done.8.g2 = bf16[2,160,128]{2,1,0:T(8,128)(2,1)S(1)} collective-permute-done((bf16[2,160,128]{2,1,0:T(8,128)(2,1)S(1)}, bf16[2,160,128]{2,1,0:T(8,128)(2,1)S(1)}, u32[]{:S(2)}, u32[]{:S(2)}) %collective-permute-start.8) | collective-permute-done | bytes 81952 | tf_op jit(solution)/shard_map/ppermute | solution.py:326
  35.4 0.3 shard_map.66
  35.7 2.1 %collective-permute-start.9 = (bf16[2,160,128]{2,1,0:T(8,128)(2,1)S(1)}, bf16[2,160,128]{2,1,0:T(8,128)(2,1)S(1)}, u32[]{:S(2)}, u32[]{:S(2)}) collective-permute-start(bf16[2,160,128]{2,1,0:T(8,128)(2,1)S(1)} %get-tuple-element.42), channel_id=1, source_target_pairs={{0,4},{2,6},{4,0},{6,2},{1,5},{3,7},{5,1},{7,3},{8,12},{10,14},{12... | collective-permute-start | bytes 245768 | tf_op jit(solution)/shard_map/ppermute | solution.py:326
  37.9 0.8 %collective-permute-start.10 = (bf16[2,160,128]{2,1,0:T(8,128)(2,1)S(1)}, bf16[2,160,128]{2,1,0:T(8,128)(2,1)S(1)}, u32[]{:S(2)}, u32[]{:S(2)}) collective-permute-start(bf16[2,160,128]{2,1,0:T(8,128)(2,1)S(1)} %get-tuple-element.43), channel_id=1, source_target_pairs={{0,2},{2,0},{4,6},{6,4},{1,3},{3,1},{5,7},{7,5},{8,10},{10,8},{12,... | collective-permute-start | bytes 245768 | tf_op jit(solution)/shard_map/ppermute | solution.py:326
  38.7 1.1 %inner_stage.11 = (bf16[1024,160]{1,0:T(8,128)(2,1)S(1)}, f32[1024,256]{1,0:T(8,128)S(1)}) custom-call(bf16[1024,128]{1,0:T(8,128)(2,1)S(1)} %get-tuple-element.44.q_ref, bf16[128,1024]{1,0:T(8,128)(2,1)S(1)} %get-tuple-element.45.kt_ref, bf16[4,1024,256]{2,1,0:T(8,128)(2,1)S(1)} %get-tuple-element.46.val_ref, ...), custom_call_target="tpu_custom_call" | custom-call | flops 1000000000 | bytes 2097152 | tf_op jit(solution)/shard_map/inner_stage/pallas_call | solution.py:232
  39.8 0.8 %collective-permute-done.9.refs_0_ = bf16[2,160,128]{2,1,0:T(8,128)(2,1)S(1)} collective-permute-done((bf16[2,160,128]{2,1,0:T(8,128)(2,1)S(1)}, bf16[2,160,128]{2,1,0:T(8,128)(2,1)S(1)}, u32[]{:S(2)}, u32[]{:S(2)}) %collective-permute-start.9) | collective-permute-done | bytes 81952 | tf_op jit(solution)/shard_map/ppermute | solution.py:326
  40.6 0.8 %collective-permute-done.10.refs_1_ = bf16[2,160,128]{2,1,0:T(8,128)(2,1)S(1)} collective-permute-done((bf16[2,160,128]{2,1,0:T(8,128)(2,1)S(1)}, bf16[2,160,128]{2,1,0:T(8,128)(2,1)S(1)}, u32[]{:S(2)}, u32[]{:S(2)}) %collective-permute-start.10) | collective-permute-done | bytes 81952 | tf_op jit(solution)/shard_map/ppermute | solution.py:326
  41.4 0.8 %outer_stage.3.refs_0_ = bf16[1024,512]{1,0:T(8,128)(2,1)S(1)} custom-call(bf16[2,160,128]{2,1,0:T(8,128)(2,1)S(1)} %collective-permute-done.9.refs_0_, bf16[2,160,128]{2,1,0:T(8,128)(2,1)S(1)} %collective-permute-done.10.refs_1_, bf16[1024,160]{1,0:T(8,128)(2,1)S(1)} %get-tuple-element.48.refs_2_, bf16[1024,160]{1,0:T(8,128)(2,1)S(1)} %get-tuple-element.49.refs_3_, ...), custom_call_target="tpu_custom_call" | custom-call | flops 600000000 | bytes 2097152 | tf_op jit(solution)/shard_map/outer_stage/pallas_call | solution.py:262
  42.2 5.6 %collective-permute-start.11 = (bf16[1024,512]{1,0:T(8,128)(2,1)S(1)}, bf16[1024,512]{1,0:T(8,128)(2,1)S(1)}, u32[]{:S(2)}, u32[]{:S(2)}) collective-permute-start(bf16[1024,512]{1,0:T(8,128)(2,1)S(1)} %outer_stage.3.refs_0_), channel_id=1, source_target_pairs={{0,1},{1,0},{2,3},{3,2},{4,5},{5,4},{6,7},{7,6},{8,9},{9,8},{10,11... | collective-permute-start | bytes 3145736 | tf_op jit(solution)/shard_map/ppermute | solution.py:420
  47.7 1.1 %inner_stage.14 = (bf16[1024,160]{1,0:T(8,128)(2,1)S(1)}, f32[1024,256]{1,0:T(8,128)S(1)}) custom-call(bf16[1024,128]{1,0:T(8,128)(2,1)S(1)} %get-tuple-element.44.q_ref, bf16[128,1024]{1,0:T(8,128)(2,1)S(1)} %get-tuple-element.45.kt_ref, bf16[4,1024,256]{2,1,0:T(8,128)(2,1)S(1)} %get-tuple-element.46.val_ref, ...), custom_call_target="tpu_custom_call" | custom-call | flops 1000000000 | bytes 2097152 | tf_op jit(solution)/shard_map/inner_stage/pallas_call | solution.py:232
  48.8 1.1 %inner_stage.15 = (bf16[1024,160]{1,0:T(8,128)(2,1)S(1)}, f32[1024,256]{1,0:T(8,128)S(1)}) custom-call(bf16[1024,128]{1,0:T(8,128)(2,1)S(1)} %get-tuple-element.44.q_ref, bf16[128,1024]{1,0:T(8,128)(2,1)S(1)} %get-tuple-element.45.kt_ref, bf16[4,1024,256]{2,1,0:T(8,128)(2,1)S(1)} %get-tuple-element.46.val_ref, ...), custom_call_target="tpu_custom_call" | custom-call | flops 1000000000 | bytes 2097152 | tf_op jit(solution)/shard_map/inner_stage/pallas_call | solution.py:232
  50.0 0.5 outer_stage.5.refs_0_
  50.5 0.1 collective-permute-start.14
  50.6 1.1 %inner_stage.12 = (bf16[1024,160]{1,0:T(8,128)(2,1)S(1)}, f32[1024,256]{1,0:T(8,128)S(1)}) custom-call(bf16[1024,128]{1,0:T(8,128)(2,1)S(1)} %get-tuple-element.44.q_ref, bf16[128,1024]{1,0:T(8,128)(2,1)S(1)} %get-tuple-element.45.kt_ref, bf16[4,1024,256]{2,1,0:T(8,128)(2,1)S(1)} %get-tuple-element.46.val_ref, ...), custom_call_target="tpu_custom_call" | custom-call | flops 1000000000 | bytes 2097152 | tf_op jit(solution)/shard_map/inner_stage/pallas_call | solution.py:232
  51.7 1.2 %collective-permute-start.12 = (bf16[2,160,128]{2,1,0:T(8,128)(2,1)S(1)}, bf16[2,160,128]{2,1,0:T(8,128)(2,1)S(1)}, u32[]{:S(2)}, u32[]{:S(2)}) collective-permute-start(bf16[2,160,128]{2,1,0:T(8,128)(2,1)S(1)} %get-tuple-element.56), channel_id=1, source_target_pairs={{0,6},{2,4},{4,2},{6,0},{1,7},{3,5},{5,3},{7,1},{8,14},{10,12},{12... | collective-permute-start | bytes 245768 | tf_op jit(solution)/shard_map/ppermute | solution.py:326
  52.9 1.1 %inner_stage.13 = (bf16[1024,160]{1,0:T(8,128)(2,1)S(1)}, f32[1024,256]{1,0:T(8,128)S(1)}) custom-call(bf16[1024,128]{1,0:T(8,128)(2,1)S(1)} %get-tuple-element.44.q_ref, bf16[128,1024]{1,0:T(8,128)(2,1)S(1)} %get-tuple-element.45.kt_ref, bf16[4,1024,256]{2,1,0:T(8,128)(2,1)S(1)} %get-tuple-element.46.val_ref, ...), custom_call_target="tpu_custom_call" | custom-call | flops 1000000000 | bytes 2097152 | tf_op jit(solution)/shard_map/inner_stage/pallas_call | solution.py:232
  54.0 2.3 %collective-permute-done.12.refs_0_ = bf16[2,160,128]{2,1,0:T(8,128)(2,1)S(1)} collective-permute-done((bf16[2,160,128]{2,1,0:T(8,128)(2,1)S(1)}, bf16[2,160,128]{2,1,0:T(8,128)(2,1)S(1)}, u32[]{:S(2)}, u32[]{:S(2)}) %collective-permute-start.12) | collective-permute-done | bytes 81952 | tf_op jit(solution)/shard_map/ppermute | solution.py:326
  56.3 0.5 outer_stage.4.refs_1_
  56.8 1.7 %collective-permute-start.13 = (bf16[1024,256]{1,0:T(8,128)(2,1)S(1)}, bf16[1024,256]{1,0:T(8,128)(2,1)S(1)}, u32[]{:S(2)}, u32[]{:S(2)}) collective-permute-start(bf16[1024,256]{1,0:T(8,128)(2,1)S(1)} %outer_stage.4.refs_1_), channel_id=1, source_target_pairs={{0,1},{1,0},{2,3},{3,2},{4,5},{5,4},{6,7},{7,6},{8,9},{9,8},{10,11... | collective-permute-start | bytes 1572872 | tf_op jit(solution)/shard_map/ppermute | solution.py:420
  58.5 0.7 %out_stage.3.refs_4_ = f32[1024,1024]{1,0:T(8,128)S(1)} custom-call(bf16[1024,256]{1,0:T(8,128)(2,1)S(1)} %outer_stage.5.refs_0_, bf16[2,1024,1024]{2,1,0:T(8,128)(2,1)S(1)} %get-tuple-element.61.refs_1_.refs_3_.refs_2_), custom_call_target="tpu_custom_call" | custom-call | flops 536870912 | bytes 1048576 | tf_op jit(solution)/shard_map/out_stage/pallas_call | solution.py:308
  59.2 0.0 collective-permute-done.14.refs_2_
  59.2 2.3 %out_stage.4.refs_3_ = f32[1024,1024]{1,0:T(8,128)S(1)} custom-call(bf16[1024,512]{1,0:T(8,128)(2,1)S(1)} %outer_stage.3.refs_0_, bf16[1024,256]{1,0:T(8,128)(2,1)S(1)} %outer_stage.4.refs_1_, bf16[1024,256]{1,0:T(8,128)(2,1)S(1)} %collective-permute-done.14.refs_2_, bf16[2,1024,1024]{2,1,0:T(8,128)(2,1)S(1)} %get-tuple-element.61.refs_1_.refs_3_.refs_2_, ...), custom_call_target="tpu_custom_call" | custom-call | flops 2147483648 | bytes 1048576 | tf_op jit(solution)/shard_map/out_stage/pallas_call | solution.py:308
  61.6 0.0 collective-permute-done.13.refs_1_
  61.6 0.0 collective-permute-done.11.refs_0_
  61.6 2.6 %out_stage.5 = bf16[1024,1024]{1,0:T(8,128)(2,1)} custom-call(bf16[1024,512]{1,0:T(8,128)(2,1)S(1)} %collective-permute-done.11.refs_0_, bf16[1024,256]{1,0:T(8,128)(2,1)S(1)} %collective-permute-done.13.refs_1_, bf16[2,1024,1024]{2,1,0:T(8,128)(2,1)S(1)} %get-tuple-element.61.refs_1_.refs_3_.refs_2_, f32[1024,1024]{1,0:T(8,128)S(1)} %out_stage.4.refs_3_), custom_call_target="tpu_custom_call" | custom-call | flops 1610612736 | bytes 1048576 | tf_op jit(solution)/shard_map/out_stage/pallas_call | solution.py:308
  (1 shorter events, 0.0 us)
Async XLA Ops:
  0.0 14.6 %copy-start = (f32[8,160]{1,0:T(8,128)S(1)}, f32[8,160]{1,0:T(8,128)}, u32[]{:S(2)}) copy-start(f32[8,160]{1,0:T(8,128)} %constant.2.clone.table_ref) | copy-start | bytes 15364
  9.4 6.6 %collective-permute-start = (bf16[2,160,128]{2,1,0:T(8,128)(2,1)S(1)}, bf16[2,160,128]{2,1,0:T(8,128)(2,1)S(1)}, u32[]{:S(2)}, u32[]{:S(2)}) collective-permute-start(bf16[2,160,128]{2,1,0:T(8,128)(2,1)S(1)} %get-tuple-element.37), channel_id=1, source_target_pairs={{0,4},{2,6},{4,0},{6,2},{1,5},{3,7},{5,1},{7,3},{8,12},{10,14},{12... | collective-permute-start | bytes 245768 | tf_op jit(solution)/shard_map/ppermute | solution.py:326
  13.8 4.1 %collective-permute-start.1 = (bf16[2,160,128]{2,1,0:T(8,128)(2,1)S(1)}, bf16[2,160,128]{2,1,0:T(8,128)(2,1)S(1)}, u32[]{:S(2)}, u32[]{:S(2)}) collective-permute-start(bf16[2,160,128]{2,1,0:T(8,128)(2,1)S(1)} %get-tuple-element.38), channel_id=1, source_target_pairs={{0,2},{2,0},{4,6},{6,4},{1,3},{3,1},{5,7},{7,5},{8,10},{10,8},{12,... | collective-permute-start | bytes 245768 | tf_op jit(solution)/shard_map/ppermute | solution.py:326
  14.6 4.5 %collective-permute-start.2 = (bf16[2,160,128]{2,1,0:T(8,128)(2,1)S(1)}, bf16[2,160,128]{2,1,0:T(8,128)(2,1)S(1)}, u32[]{:S(2)}, u32[]{:S(2)}) collective-permute-start(bf16[2,160,128]{2,1,0:T(8,128)(2,1)S(1)} %get-tuple-element.39), channel_id=1, source_target_pairs={{0,6},{2,4},{4,2},{6,0},{1,7},{3,5},{5,3},{7,1},{8,14},{10,12},{12... | collective-permute-start | bytes 245768 | tf_op jit(solution)/shard_map/ppermute | solution.py:326
  19.1 4.9 %collective-permute-start.3 = (bf16[2,160,128]{2,1,0:T(8,128)(2,1)S(1)}, bf16[2,160,128]{2,1,0:T(8,128)(2,1)S(1)}, u32[]{:S(2)}, u32[]{:S(2)}) collective-permute-start(bf16[2,160,128]{2,1,0:T(8,128)(2,1)S(1)} %shard_map.64.own), channel_id=1, source_target_pairs={{0,16},{8,24},{16,0},{24,8},{1,17},{9,25},{17,1},{25,9},{2,18},{10... | collective-permute-start | bytes 245768 | tf_op jit(solution)/shard_map/ppermute | solution.py:326
  22.1 3.3 %collective-permute-start.4 = (bf16[2,160,128]{2,1,0:T(8,128)(2,1)S(1)}, bf16[2,160,128]{2,1,0:T(8,128)(2,1)S(1)}, u32[]{:S(2)}, u32[]{:S(2)}) collective-permute-start(bf16[2,160,128]{2,1,0:T(8,128)(2,1)S(1)} %shard_map.64.own), channel_id=1, source_target_pairs={{0,8},{8,0},{16,24},{24,16},{1,9},{9,1},{17,25},{25,17},{2,10},{10... | collective-permute-start | bytes 245768 | tf_op jit(solution)/shard_map/ppermute | solution.py:326
  22.5 5.2 %collective-permute-start.5 = (bf16[2,160,128]{2,1,0:T(8,128)(2,1)S(1)}, bf16[2,160,128]{2,1,0:T(8,128)(2,1)S(1)}, u32[]{:S(2)}, u32[]{:S(2)}) collective-permute-start(bf16[2,160,128]{2,1,0:T(8,128)(2,1)S(1)} %shard_map.64.own), channel_id=1, source_target_pairs={{0,24},{8,16},{16,8},{24,0},{1,25},{9,17},{17,9},{25,1},{2,26},{10... | collective-permute-start | bytes 245768 | tf_op jit(solution)/shard_map/ppermute | solution.py:326
  27.8 4.9 %collective-permute-start.6 = (bf16[2,160,128]{2,1,0:T(8,128)(2,1)S(1)}, bf16[2,160,128]{2,1,0:T(8,128)(2,1)S(1)}, u32[]{:S(2)}, u32[]{:S(2)}) collective-permute-start(bf16[2,160,128]{2,1,0:T(8,128)(2,1)S(1)} %get-tuple-element.40.own), channel_id=1, source_target_pairs={{0,64},{32,96},{64,0},{96,32},{1,65},{33,97},{65,1},{97,33},{2,66}... | collective-permute-start | bytes 245768 | tf_op jit(solution)/shard_map/ppermute | solution.py:326
  30.6 3.3 %collective-permute-start.7 = (bf16[2,160,128]{2,1,0:T(8,128)(2,1)S(1)}, bf16[2,160,128]{2,1,0:T(8,128)(2,1)S(1)}, u32[]{:S(2)}, u32[]{:S(2)}) collective-permute-start(bf16[2,160,128]{2,1,0:T(8,128)(2,1)S(1)} %get-tuple-element.40.own), channel_id=1, source_target_pairs={{0,32},{32,0},{64,96},{96,64},{1,33},{33,1},{65,97},{97,65},{2,34}... | collective-permute-start | bytes 245768 | tf_op jit(solution)/shard_map/ppermute | solution.py:326
  30.9 4.5 %collective-permute-start.8 = (bf16[2,160,128]{2,1,0:T(8,128)(2,1)S(1)}, bf16[2,160,128]{2,1,0:T(8,128)(2,1)S(1)}, u32[]{:S(2)}, u32[]{:S(2)}) collective-permute-start(bf16[2,160,128]{2,1,0:T(8,128)(2,1)S(1)} %get-tuple-element.40.own), channel_id=1, source_target_pairs={{0,96},{32,64},{64,32},{96,0},{1,97},{33,65},{65,33},{97,1},{2,98}... | collective-permute-start | bytes 245768 | tf_op jit(solution)/shard_map/ppermute | solution.py:326
  35.7 4.9 %collective-permute-start.9 = (bf16[2,160,128]{2,1,0:T(8,128)(2,1)S(1)}, bf16[2,160,128]{2,1,0:T(8,128)(2,1)S(1)}, u32[]{:S(2)}, u32[]{:S(2)}) collective-permute-start(bf16[2,160,128]{2,1,0:T(8,128)(2,1)S(1)} %get-tuple-element.42), channel_id=1, source_target_pairs={{0,4},{2,6},{4,0},{6,2},{1,5},{3,7},{5,1},{7,3},{8,12},{10,14},{12... | collective-permute-start | bytes 245768 | tf_op jit(solution)/shard_map/ppermute | solution.py:326
  37.9 3.5 %collective-permute-start.10 = (bf16[2,160,128]{2,1,0:T(8,128)(2,1)S(1)}, bf16[2,160,128]{2,1,0:T(8,128)(2,1)S(1)}, u32[]{:S(2)}, u32[]{:S(2)}) collective-permute-start(bf16[2,160,128]{2,1,0:T(8,128)(2,1)S(1)} %get-tuple-element.43), channel_id=1, source_target_pairs={{0,2},{2,0},{4,6},{6,4},{1,3},{3,1},{5,7},{7,5},{8,10},{10,8},{12,... | collective-permute-start | bytes 245768 | tf_op jit(solution)/shard_map/ppermute | solution.py:326
  42.2 19.4 %collective-permute-start.11 = (bf16[1024,512]{1,0:T(8,128)(2,1)S(1)}, bf16[1024,512]{1,0:T(8,128)(2,1)S(1)}, u32[]{:S(2)}, u32[]{:S(2)}) collective-permute-start(bf16[1024,512]{1,0:T(8,128)(2,1)S(1)} %outer_stage.3.refs_0_), channel_id=1, source_target_pairs={{0,1},{1,0},{2,3},{3,2},{4,5},{5,4},{6,7},{7,6},{8,9},{9,8},{10,11... | collective-permute-start | bytes 3145736 | tf_op jit(solution)/shard_map/ppermute | solution.py:420
  50.5 8.8 %collective-permute-start.14 = (bf16[1024,256]{1,0:T(8,128)(2,1)S(1)}, bf16[1024,256]{1,0:T(8,128)(2,1)S(1)}, u32[]{:S(2)}, u32[]{:S(2)}) collective-permute-start(bf16[1024,256]{1,0:T(8,128)(2,1)S(1)} %outer_stage.5.refs_0_), channel_id=1, source_target_pairs={{0,1},{1,0},{2,3},{3,2},{4,5},{5,4},{6,7},{7,6},{8,9},{9,8},{10,11... | collective-permute-start | bytes 1572872 | tf_op jit(solution)/shard_map/ppermute | solution.py:420
  51.7 4.6 %collective-permute-start.12 = (bf16[2,160,128]{2,1,0:T(8,128)(2,1)S(1)}, bf16[2,160,128]{2,1,0:T(8,128)(2,1)S(1)}, u32[]{:S(2)}, u32[]{:S(2)}) collective-permute-start(bf16[2,160,128]{2,1,0:T(8,128)(2,1)S(1)} %get-tuple-element.56), channel_id=1, source_target_pairs={{0,6},{2,4},{4,2},{6,0},{1,7},{3,5},{5,3},{7,1},{8,14},{10,12},{12... | collective-permute-start | bytes 245768 | tf_op jit(solution)/shard_map/ppermute | solution.py:326
  56.8 4.8 %collective-permute-start.13 = (bf16[1024,256]{1,0:T(8,128)(2,1)S(1)}, bf16[1024,256]{1,0:T(8,128)(2,1)S(1)}, u32[]{:S(2)}, u32[]{:S(2)}) collective-permute-start(bf16[1024,256]{1,0:T(8,128)(2,1)S(1)} %outer_stage.4.refs_1_), channel_id=1, source_target_pairs={{0,1},{1,0},{2,3},{3,2},{4,5},{5,4},{6,7},{7,6},{8,9},{9,8},{10,11... | collective-permute-start | bytes 1572872 | tf_op jit(solution)/shard_map/ppermute | solution.py:420

commit v5 on v4

--- a/solution.py
+++ b/solution.py
@@ -13,12 +13,12 @@
 ROWS = 160
 CHUNK = 256
 SEQ = ("seq_0", "seq_1", "seq_2")
-STEPS = (2, 1, 3)
+STEPS = (1, 3, 2)
 MIB = 2**20
 HEAD_LIMIT, OUT_LIMIT = (40 * MIB, 20 * MIB)
-SLOTS = (0, 2, 1, 3)
-OUT_STEPS = (0, 2, 1, 3)
-GROUPS = ((0,), (2, 1), (3,))
+SLOTS = (0, 1, 3, 2)
+OUT_STEPS = (0, 1, 3, 2)
+GROUPS = ((0,), (1, 3), (2,))
 F32, BF16 = (jnp.float32, jnp.bfloat16)
 VMEM = pl.BlockSpec(memory_space=pltpu.VMEM)
 SMEM = pl.BlockSpec(memory_space=pltpu.SMEM)

time: 64.5 us -> 65.8 us (1.020)
  waiting for transfers between devices: 13.8 us -> 15.3 us
    ppermute x12, starting transfers between devices: 16.9 us -> 15.1 us  [partner(): return lax.ppermute(x, axis, pairs)]
    ppermute x12, waiting for transfers between devices: 13.8 us -> 15.3 us  [partner(): return lax.ppermute(x, axis, pairs)]
    ppermute x3, starting transfers between devices: 7.4 us -> 8.88 us  [per_device(): other.append(lax.ppermute(own[-1], 'head', [(0, 1), (1, 0)]))]
  transfers between devices with their start and end apart: 15 -> 15, of which waited for: 11 -> 9; matrix products, arithmetic and copies ran while one was open for 0% -> 0% of each run, Pallas kernels for 20% -> 20%
where the time goes in v5:
time: 65.8 us; the launch traced here: 65.7 us
  Pallas kernels  26 us (40%)
  starting transfers between devices  24 us (36%)
  waiting for transfers between devices  15.3 us (23%)
    ppermute x12, waiting for transfers between devices, partner(): return lax.ppermute(x, axis, pairs)  15.3 us
    ppermute x12, starting transfers between devices, partner(): return lax.ppermute(x, axis, pairs)  15.1 us
    pallas_call x1, Pallas kernels, head_stage(): pl.pallas_call(head_kernel, out_shape=[shape((tok, kd), BF16), shape((kd,...  9.34 us
    ppermute x3, starting transfers between devices, per_device(): other.append(lax.ppermute(own[-1], 'head', [(0, 1), (1, 0)]))  8.88 us
    pallas_call x8, Pallas kernels, inner_stage(): pl.pallas_call(functools.partial(inner_kernel, slot, h), out_shape=[shape...  8.8 us
    pallas_call x3, Pallas kernels, out_stage(): pl.pallas_call(functools.partial(out_kernel, places, last), out_shape=jax...  5.67 us
    pallas_call x3, Pallas kernels, outer_stage(): pl.pallas_call(functools.partial(outer_kernel, count), out_shape=jax.Shap...  1.83 us
  transfers between devices with their start and end apart: 15, of which 9 were waited for; matrix products, arithmetic and copies ran while one was open for 0% of the time, Pallas kernels for 20%

profile of v5, /device:TPU:1, one launch (start us, length us, event | category | flops | bytes accessed | tf_op | source)
XLA Modules:
  0.0 65.7 jit_solution(10065193338982639471)
XLA Ops:
  0.0 0.0 copy-start
  0.0 9.3 %head_stage.1 = (bf16[1024,128]{1,0:T(8,128)(2,1)S(1)}, bf16[128,1024]{1,0:T(8,128)(2,1)S(1)}, bf16[4,1024,256]{2,1,0:T(8,128)(2,1)S(1)}, bf16[4,2,3,160,256]{4,...) custom-call(bf16[1024,2048]{1,0:T(8,128)(2,1)} %x_hbm.1, ...), custom_call_target="tpu_custom_call" | custom-call | flops 6000000000 | bytes 12582912 | tf_op jit(solution)/shard_map/head_stage/pallas_call | solution.py:167
  9.4 2.5 %collective-permute-start = (bf16[2,160,128]{2,1,0:T(8,128)(2,1)S(1)}, bf16[2,160,128]{2,1,0:T(8,128)(2,1)S(1)}, u32[]{:S(2)}, u32[]{:S(2)}) collective-permute-start(bf16[2,160,128]{2,1,0:T(8,128)(2,1)S(1)} %get-tuple-element.37), channel_id=1, source_target_pairs={{0,2},{2,0},{4,6},{6,4},{1,3},{3,1},{5,7},{7,5},{8,10},{10,8},{12,... | collective-permute-start | bytes 245768 | tf_op jit(solution)/shard_map/ppermute | solution.py:326
  11.9 2.3 %collective-permute-start.1 = (bf16[2,160,128]{2,1,0:T(8,128)(2,1)S(1)}, bf16[2,160,128]{2,1,0:T(8,128)(2,1)S(1)}, u32[]{:S(2)}, u32[]{:S(2)}) collective-permute-start(bf16[2,160,128]{2,1,0:T(8,128)(2,1)S(1)} %get-tuple-element.38), channel_id=1, source_target_pairs={{0,6},{2,4},{4,2},{6,0},{1,7},{3,5},{5,3},{7,1},{8,14},{10,12},{12... | collective-permute-start | bytes 245768 | tf_op jit(solution)/shard_map/ppermute | solution.py:326
  14.1 1.1 %collective-permute-start.2 = (bf16[2,160,128]{2,1,0:T(8,128)(2,1)S(1)}, bf16[2,160,128]{2,1,0:T(8,128)(2,1)S(1)}, u32[]{:S(2)}, u32[]{:S(2)}) collective-permute-start(bf16[2,160,128]{2,1,0:T(8,128)(2,1)S(1)} %get-tuple-element.39), channel_id=1, source_target_pairs={{0,4},{2,6},{4,0},{6,2},{1,5},{3,7},{5,1},{7,3},{8,12},{10,14},{12... | collective-permute-start | bytes 245768 | tf_op jit(solution)/shard_map/ppermute | solution.py:326
  15.2 0.0 copy-done
  15.2 1.1 %inner_stage.8 = (bf16[1024,160]{1,0:T(8,128)(2,1)S(1)}, f32[1024,256]{1,0:T(8,128)S(1)}) custom-call(bf16[1024,128]{1,0:T(8,128)(2,1)S(1)} %get-tuple-element.44.q_ref, bf16[128,1024]{1,0:T(8,128)(2,1)S(1)} %get-tuple-element.45.kt_ref, bf16[4,1024,256]{2,1,0:T(8,128)(2,1)S(1)} %get-tuple-element.46.val_ref, ...), custom_call_target="tpu_custom_call" | custom-call | flops 1000000000 | bytes 2097152 | tf_op jit(solution)/shard_map/inner_stage/pallas_call | solution.py:232
  16.3 0.0 collective-permute-done.p1
  16.3 0.1 collective-permute-done.1.p2
  16.4 2.6 %collective-permute-done.2.p3 = bf16[2,160,128]{2,1,0:T(8,128)(2,1)S(1)} collective-permute-done((bf16[2,160,128]{2,1,0:T(8,128)(2,1)S(1)}, bf16[2,160,128]{2,1,0:T(8,128)(2,1)S(1)}, u32[]{:S(2)}, u32[]{:S(2)}) %collective-permute-start.2) | collective-permute-done | bytes 81952 | tf_op jit(solution)/shard_map/ppermute | solution.py:326
  19.1 1.4 %collective-permute-start.3 = (bf16[2,160,128]{2,1,0:T(8,128)(2,1)S(1)}, bf16[2,160,128]{2,1,0:T(8,128)(2,1)S(1)}, u32[]{:S(2)}, u32[]{:S(2)}) collective-permute-start(bf16[2,160,128]{2,1,0:T(8,128)(2,1)S(1)} %shard_map.64.own), channel_id=1, source_target_pairs={{0,8},{8,0},{16,24},{24,16},{1,9},{9,1},{17,25},{25,17},{2,10},{10... | collective-permute-start | bytes 245768 | tf_op jit(solution)/shard_map/ppermute | solution.py:326
  20.4 1.9 %collective-permute-start.4 = (bf16[2,160,128]{2,1,0:T(8,128)(2,1)S(1)}, bf16[2,160,128]{2,1,0:T(8,128)(2,1)S(1)}, u32[]{:S(2)}, u32[]{:S(2)}) collective-permute-start(bf16[2,160,128]{2,1,0:T(8,128)(2,1)S(1)} %shard_map.64.own), channel_id=1, source_target_pairs={{0,24},{8,16},{16,8},{24,0},{1,25},{9,17},{17,9},{25,1},{2,26},{10... | collective-permute-start | bytes 245768 | tf_op jit(solution)/shard_map/ppermute | solution.py:326
  22.3 0.7 %collective-permute-start.5 = (bf16[2,160,128]{2,1,0:T(8,128)(2,1)S(1)}, bf16[2,160,128]{2,1,0:T(8,128)(2,1)S(1)}, u32[]{:S(2)}, u32[]{:S(2)}) collective-permute-start(bf16[2,160,128]{2,1,0:T(8,128)(2,1)S(1)} %shard_map.64.own), channel_id=1, source_target_pairs={{0,16},{8,24},{16,0},{24,8},{1,17},{9,25},{17,1},{25,9},{2,18},{10... | collective-permute-start | bytes 245768 | tf_op jit(solution)/shard_map/ppermute | solution.py:326
  23.1 1.1 %inner_stage.9 = (bf16[1024,160]{1,0:T(8,128)(2,1)S(1)}, f32[1024,256]{1,0:T(8,128)S(1)}) custom-call(bf16[1024,128]{1,0:T(8,128)(2,1)S(1)} %get-tuple-element.44.q_ref, bf16[128,1024]{1,0:T(8,128)(2,1)S(1)} %get-tuple-element.45.kt_ref, bf16[4,1024,256]{2,1,0:T(8,128)(2,1)S(1)} %get-tuple-element.46.val_ref, ...), custom_call_target="tpu_custom_call" | custom-call | flops 1000000000 | bytes 2097152 | tf_op jit(solution)/shard_map/inner_stage/pallas_call | solution.py:232
  24.2 0.0 collective-permute-done.3.g0
  24.2 0.8 %collective-permute-done.4.g1 = bf16[2,160,128]{2,1,0:T(8,128)(2,1)S(1)} collective-permute-done((bf16[2,160,128]{2,1,0:T(8,128)(2,1)S(1)}, bf16[2,160,128]{2,1,0:T(8,128)(2,1)S(1)}, u32[]{:S(2)}, u32[]{:S(2)}) %collective-permute-start.4) | collective-permute-done | bytes 81952 | tf_op jit(solution)/shard_map/ppermute | solution.py:326
  24.9 2.6 %collective-permute-done.5.g2 = bf16[2,160,128]{2,1,0:T(8,128)(2,1)S(1)} collective-permute-done((bf16[2,160,128]{2,1,0:T(8,128)(2,1)S(1)}, bf16[2,160,128]{2,1,0:T(8,128)(2,1)S(1)}, u32[]{:S(2)}, u32[]{:S(2)}) %collective-permute-start.5) | collective-permute-done | bytes 81952 | tf_op jit(solution)/shard_map/ppermute | solution.py:326
  27.5 0.1 shard_map.65
  27.6 1.3 %collective-permute-start.6 = (bf16[2,160,128]{2,1,0:T(8,128)(2,1)S(1)}, bf16[2,160,128]{2,1,0:T(8,128)(2,1)S(1)}, u32[]{:S(2)}, u32[]{:S(2)}) collective-permute-start(bf16[2,160,128]{2,1,0:T(8,128)(2,1)S(1)} %get-tuple-element.40.own), channel_id=1, source_target_pairs={{0,32},{32,0},{64,96},{96,64},{1,33},{33,1},{65,97},{97,65},{2,34}... | collective-permute-start | bytes 245768 | tf_op jit(solution)/shard_map/ppermute | solution.py:326
  28.9 1.8 %collective-permute-start.7 = (bf16[2,160,128]{2,1,0:T(8,128)(2,1)S(1)}, bf16[2,160,128]{2,1,0:T(8,128)(2,1)S(1)}, u32[]{:S(2)}, u32[]{:S(2)}) collective-permute-start(bf16[2,160,128]{2,1,0:T(8,128)(2,1)S(1)} %get-tuple-element.40.own), channel_id=1, source_target_pairs={{0,96},{32,64},{64,32},{96,0},{1,97},{33,65},{65,33},{97,1},{2,98}... | collective-permute-start | bytes 245768 | tf_op jit(solution)/shard_map/ppermute | solution.py:326
  30.7 0.7 %collective-permute-start.8 = (bf16[2,160,128]{2,1,0:T(8,128)(2,1)S(1)}, bf16[2,160,128]{2,1,0:T(8,128)(2,1)S(1)}, u32[]{:S(2)}, u32[]{:S(2)}) collective-permute-start(bf16[2,160,128]{2,1,0:T(8,128)(2,1)S(1)} %get-tuple-element.40.own), channel_id=1, source_target_pairs={{0,64},{32,96},{64,0},{96,32},{1,65},{33,97},{65,1},{97,33},{2,66}... | collective-permute-start | bytes 245768 | tf_op jit(solution)/shard_map/ppermute | solution.py:326
  31.4 1.1 %inner_stage.10 = (bf16[1024,160]{1,0:T(8,128)(2,1)S(1)}, f32[1024,256]{1,0:T(8,128)S(1)}) custom-call(bf16[1024,128]{1,0:T(8,128)(2,1)S(1)} %get-tuple-element.44.q_ref, bf16[128,1024]{1,0:T(8,128)(2,1)S(1)} %get-tuple-element.45.kt_ref, bf16[4,1024,256]{2,1,0:T(8,128)(2,1)S(1)} %get-tuple-element.46.val_ref, ...), custom_call_target="tpu_custom_call" | custom-call | flops 1000000000 | bytes 2097152 | tf_op jit(solution)/shard_map/inner_stage/pallas_call | solution.py:232
  32.5 0.0 collective-permute-done.6.g0
  32.5 0.9 %collective-permute-done.7.g1 = bf16[2,160,128]{2,1,0:T(8,128)(2,1)S(1)} collective-permute-done((bf16[2,160,128]{2,1,0:T(8,128)(2,1)S(1)}, bf16[2,160,128]{2,1,0:T(8,128)(2,1)S(1)}, u32[]{:S(2)}, u32[]{:S(2)}) %collective-permute-start.7) | collective-permute-done | bytes 81952 | tf_op jit(solution)/shard_map/ppermute | solution.py:326
  33.4 2.1 %collective-permute-done.8.g2 = bf16[2,160,128]{2,1,0:T(8,128)(2,1)S(1)} collective-permute-done((bf16[2,160,128]{2,1,0:T(8,128)(2,1)S(1)}, bf16[2,160,128]{2,1,0:T(8,128)(2,1)S(1)}, u32[]{:S(2)}, u32[]{:S(2)}) %collective-permute-start.8) | collective-permute-done | bytes 81952 | tf_op jit(solution)/shard_map/ppermute | solution.py:326
  35.5 0.3 shard_map.66
  35.8 0.6 collective-permute-start.9
  36.4 0.8 %collective-permute-start.10 = (bf16[2,160,128]{2,1,0:T(8,128)(2,1)S(1)}, bf16[2,160,128]{2,1,0:T(8,128)(2,1)S(1)}, u32[]{:S(2)}, u32[]{:S(2)}) collective-permute-start(bf16[2,160,128]{2,1,0:T(8,128)(2,1)S(1)} %get-tuple-element.43), channel_id=1, source_target_pairs={{0,6},{2,4},{4,2},{6,0},{1,7},{3,5},{5,3},{7,1},{8,14},{10,12},{12... | collective-permute-start | bytes 245768 | tf_op jit(solution)/shard_map/ppermute | solution.py:326
  37.2 1.1 %inner_stage.11 = (bf16[1024,160]{1,0:T(8,128)(2,1)S(1)}, f32[1024,256]{1,0:T(8,128)S(1)}) custom-call(bf16[1024,128]{1,0:T(8,128)(2,1)S(1)} %get-tuple-element.44.q_ref, bf16[128,1024]{1,0:T(8,128)(2,1)S(1)} %get-tuple-element.45.kt_ref, bf16[4,1024,256]{2,1,0:T(8,128)(2,1)S(1)} %get-tuple-element.46.val_ref, ...), custom_call_target="tpu_custom_call" | custom-call | flops 1000000000 | bytes 2097152 | tf_op jit(solution)/shard_map/inner_stage/pallas_call | solution.py:232
  38.3 1.1 %collective-permute-done.9.refs_0_ = bf16[2,160,128]{2,1,0:T(8,128)(2,1)S(1)} collective-permute-done((bf16[2,160,128]{2,1,0:T(8,128)(2,1)S(1)}, bf16[2,160,128]{2,1,0:T(8,128)(2,1)S(1)}, u32[]{:S(2)}, u32[]{:S(2)}) %collective-permute-start.9) | collective-permute-done | bytes 81952 | tf_op jit(solution)/shard_map/ppermute | solution.py:326
  39.5 1.4 %collective-permute-done.10.refs_1_ = bf16[2,160,128]{2,1,0:T(8,128)(2,1)S(1)} collective-permute-done((bf16[2,160,128]{2,1,0:T(8,128)(2,1)S(1)}, bf16[2,160,128]{2,1,0:T(8,128)(2,1)S(1)}, u32[]{:S(2)}, u32[]{:S(2)}) %collective-permute-start.10) | collective-permute-done | bytes 81952 | tf_op jit(solution)/shard_map/ppermute | solution.py:326
  40.9 0.8 %outer_stage.3.refs_0_ = bf16[1024,512]{1,0:T(8,128)(2,1)S(1)} custom-call(bf16[2,160,128]{2,1,0:T(8,128)(2,1)S(1)} %collective-permute-done.9.refs_0_, bf16[2,160,128]{2,1,0:T(8,128)(2,1)S(1)} %collective-permute-done.10.refs_1_, bf16[1024,160]{1,0:T(8,128)(2,1)S(1)} %get-tuple-element.48.refs_2_, bf16[1024,160]{1,0:T(8,128)(2,1)S(1)} %get-tuple-element.49.refs_3_, ...), custom_call_target="tpu_custom_call" | custom-call | flops 600000000 | bytes 2097152 | tf_op jit(solution)/shard_map/outer_stage/pallas_call | solution.py:262
  41.7 7.0 %collective-permute-start.11 = (bf16[1024,512]{1,0:T(8,128)(2,1)S(1)}, bf16[1024,512]{1,0:T(8,128)(2,1)S(1)}, u32[]{:S(2)}, u32[]{:S(2)}) collective-permute-start(bf16[1024,512]{1,0:T(8,128)(2,1)S(1)} %outer_stage.3.refs_0_), channel_id=1, source_target_pairs={{0,1},{1,0},{2,3},{3,2},{4,5},{5,4},{6,7},{7,6},{8,9},{9,8},{10,11... | collective-permute-start | bytes 3145736 | tf_op jit(solution)/shard_map/ppermute | solution.py:420
  48.7 1.1 %inner_stage.14 = (bf16[1024,160]{1,0:T(8,128)(2,1)S(1)}, f32[1024,256]{1,0:T(8,128)S(1)}) custom-call(bf16[1024,128]{1,0:T(8,128)(2,1)S(1)} %get-tuple-element.44.q_ref, bf16[128,1024]{1,0:T(8,128)(2,1)S(1)} %get-tuple-element.45.kt_ref, bf16[4,1024,256]{2,1,0:T(8,128)(2,1)S(1)} %get-tuple-element.46.val_ref, ...), custom_call_target="tpu_custom_call" | custom-call | flops 1000000000 | bytes 2097152 | tf_op jit(solution)/shard_map/inner_stage/pallas_call | solution.py:232
  49.8 1.1 %inner_stage.15 = (bf16[1024,160]{1,0:T(8,128)(2,1)S(1)}, f32[1024,256]{1,0:T(8,128)S(1)}) custom-call(bf16[1024,128]{1,0:T(8,128)(2,1)S(1)} %get-tuple-element.44.q_ref, bf16[128,1024]{1,0:T(8,128)(2,1)S(1)} %get-tuple-element.45.kt_ref, bf16[4,1024,256]{2,1,0:T(8,128)(2,1)S(1)} %get-tuple-element.46.val_ref, ...), custom_call_target="tpu_custom_call" | custom-call | flops 1000000000 | bytes 2097152 | tf_op jit(solution)/shard_map/inner_stage/pallas_call | solution.py:232
  50.9 0.5 outer_stage.5.refs_0_
  51.5 0.1 collective-permute-start.14
  51.6 1.1 %inner_stage.12 = (bf16[1024,160]{1,0:T(8,128)(2,1)S(1)}, f32[1024,256]{1,0:T(8,128)S(1)}) custom-call(bf16[1024,128]{1,0:T(8,128)(2,1)S(1)} %get-tuple-element.44.q_ref, bf16[128,1024]{1,0:T(8,128)(2,1)S(1)} %get-tuple-element.45.kt_ref, bf16[4,1024,256]{2,1,0:T(8,128)(2,1)S(1)} %get-tuple-element.46.val_ref, ...), custom_call_target="tpu_custom_call" | custom-call | flops 1000000000 | bytes 2097152 | tf_op jit(solution)/shard_map/inner_stage/pallas_call | solution.py:232
  52.7 0.1 collective-permute-start.12
  52.8 1.1 %inner_stage.13 = (bf16[1024,160]{1,0:T(8,128)(2,1)S(1)}, f32[1024,256]{1,0:T(8,128)S(1)}) custom-call(bf16[1024,128]{1,0:T(8,128)(2,1)S(1)} %get-tuple-element.44.q_ref, bf16[128,1024]{1,0:T(8,128)(2,1)S(1)} %get-tuple-element.45.kt_ref, bf16[4,1024,256]{2,1,0:T(8,128)(2,1)S(1)} %get-tuple-element.46.val_ref, ...), custom_call_target="tpu_custom_call" | custom-call | flops 1000000000 | bytes 2097152 | tf_op jit(solution)/shard_map/inner_stage/pallas_call | solution.py:232
  53.9 3.7 %collective-permute-done.12.refs_0_ = bf16[2,160,128]{2,1,0:T(8,128)(2,1)S(1)} collective-permute-done((bf16[2,160,128]{2,1,0:T(8,128)(2,1)S(1)}, bf16[2,160,128]{2,1,0:T(8,128)(2,1)S(1)}, u32[]{:S(2)}, u32[]{:S(2)}) %collective-permute-start.12) | collective-permute-done | bytes 81952 | tf_op jit(solution)/shard_map/ppermute | solution.py:326
  57.6 0.5 outer_stage.4.refs_1_
  58.1 1.7 %collective-permute-start.13 = (bf16[1024,256]{1,0:T(8,128)(2,1)S(1)}, bf16[1024,256]{1,0:T(8,128)(2,1)S(1)}, u32[]{:S(2)}, u32[]{:S(2)}) collective-permute-start(bf16[1024,256]{1,0:T(8,128)(2,1)S(1)} %outer_stage.4.refs_1_), channel_id=1, source_target_pairs={{0,1},{1,0},{2,3},{3,2},{4,5},{5,4},{6,7},{7,6},{8,9},{9,8},{10,11... | collective-permute-start | bytes 1572872 | tf_op jit(solution)/shard_map/ppermute | solution.py:420
  59.8 0.7 %out_stage.3.refs_4_ = f32[1024,1024]{1,0:T(8,128)S(1)} custom-call(bf16[1024,256]{1,0:T(8,128)(2,1)S(1)} %outer_stage.5.refs_0_, bf16[2,1024,1024]{2,1,0:T(8,128)(2,1)S(1)} %get-tuple-element.61.refs_1_.refs_3_.refs_2_), custom_call_target="tpu_custom_call" | custom-call | flops 536870912 | bytes 1048576 | tf_op jit(solution)/shard_map/out_stage/pallas_call | solution.py:308
  60.5 0.0 collective-permute-done.14.refs_2_
  60.5 2.3 %out_stage.4.refs_3_ = f32[1024,1024]{1,0:T(8,128)S(1)} custom-call(bf16[1024,512]{1,0:T(8,128)(2,1)S(1)} %outer_stage.3.refs_0_, bf16[1024,256]{1,0:T(8,128)(2,1)S(1)} %outer_stage.4.refs_1_, bf16[1024,256]{1,0:T(8,128)(2,1)S(1)} %collective-permute-done.14.refs_2_, bf16[2,1024,1024]{2,1,0:T(8,128)(2,1)S(1)} %get-tuple-element.61.refs_1_.refs_3_.refs_2_, ...), custom_call_target="tpu_custom_call" | custom-call | flops 2147483648 | bytes 1048576 | tf_op jit(solution)/shard_map/out_stage/pallas_call | solution.py:308
  62.9 0.0 collective-permute-done.13.refs_1_
  62.9 0.0 collective-permute-done.11.refs_0_
  62.9 2.6 %out_stage.5 = bf16[1024,1024]{1,0:T(8,128)(2,1)} custom-call(bf16[1024,512]{1,0:T(8,128)(2,1)S(1)} %collective-permute-done.11.refs_0_, bf16[1024,256]{1,0:T(8,128)(2,1)S(1)} %collective-permute-done.13.refs_1_, bf16[2,1024,1024]{2,1,0:T(8,128)(2,1)S(1)} %get-tuple-element.61.refs_1_.refs_3_.refs_2_, f32[1024,1024]{1,0:T(8,128)S(1)} %out_stage.4.refs_3_), custom_call_target="tpu_custom_call" | custom-call | flops 1610612736 | bytes 1048576 | tf_op jit(solution)/shard_map/out_stage/pallas_call | solution.py:308
  (1 shorter events, 0.0 us)
Async XLA Ops:
  0.0 15.2 %copy-start = (f32[8,160]{1,0:T(8,128)S(1)}, f32[8,160]{1,0:T(8,128)}, u32[]{:S(2)}) copy-start(f32[8,160]{1,0:T(8,128)} %constant.2.clone.table_ref) | copy-start | bytes 15364
  9.4 6.9 %collective-permute-start = (bf16[2,160,128]{2,1,0:T(8,128)(2,1)S(1)}, bf16[2,160,128]{2,1,0:T(8,128)(2,1)S(1)}, u32[]{:S(2)}, u32[]{:S(2)}) collective-permute-start(bf16[2,160,128]{2,1,0:T(8,128)(2,1)S(1)} %get-tuple-element.37), channel_id=1, source_target_pairs={{0,2},{2,0},{4,6},{6,4},{1,3},{3,1},{5,7},{7,5},{8,10},{10,8},{12,... | collective-permute-start | bytes 245768 | tf_op jit(solution)/shard_map/ppermute | solution.py:326
  11.9 4.5 %collective-permute-start.1 = (bf16[2,160,128]{2,1,0:T(8,128)(2,1)S(1)}, bf16[2,160,128]{2,1,0:T(8,128)(2,1)S(1)}, u32[]{:S(2)}, u32[]{:S(2)}) collective-permute-start(bf16[2,160,128]{2,1,0:T(8,128)(2,1)S(1)} %get-tuple-element.38), channel_id=1, source_target_pairs={{0,6},{2,4},{4,2},{6,0},{1,7},{3,5},{5,3},{7,1},{8,14},{10,12},{12... | collective-permute-start | bytes 245768 | tf_op jit(solution)/shard_map/ppermute | solution.py:326
  14.1 4.9 %collective-permute-start.2 = (bf16[2,160,128]{2,1,0:T(8,128)(2,1)S(1)}, bf16[2,160,128]{2,1,0:T(8,128)(2,1)S(1)}, u32[]{:S(2)}, u32[]{:S(2)}) collective-permute-start(bf16[2,160,128]{2,1,0:T(8,128)(2,1)S(1)} %get-tuple-element.39), channel_id=1, source_target_pairs={{0,4},{2,6},{4,0},{6,2},{1,5},{3,7},{5,1},{7,3},{8,12},{10,14},{12... | collective-permute-start | bytes 245768 | tf_op jit(solution)/shard_map/ppermute | solution.py:326
  19.1 5.1 %collective-permute-start.3 = (bf16[2,160,128]{2,1,0:T(8,128)(2,1)S(1)}, bf16[2,160,128]{2,1,0:T(8,128)(2,1)S(1)}, u32[]{:S(2)}, u32[]{:S(2)}) collective-permute-start(bf16[2,160,128]{2,1,0:T(8,128)(2,1)S(1)} %shard_map.64.own), channel_id=1, source_target_pairs={{0,8},{8,0},{16,24},{24,16},{1,9},{9,1},{17,25},{25,17},{2,10},{10... | collective-permute-start | bytes 245768 | tf_op jit(solution)/shard_map/ppermute | solution.py:326
  20.4 4.5 %collective-permute-start.4 = (bf16[2,160,128]{2,1,0:T(8,128)(2,1)S(1)}, bf16[2,160,128]{2,1,0:T(8,128)(2,1)S(1)}, u32[]{:S(2)}, u32[]{:S(2)}) collective-permute-start(bf16[2,160,128]{2,1,0:T(8,128)(2,1)S(1)} %shard_map.64.own), channel_id=1, source_target_pairs={{0,24},{8,16},{16,8},{24,0},{1,25},{9,17},{17,9},{25,1},{2,26},{10... | collective-permute-start | bytes 245768 | tf_op jit(solution)/shard_map/ppermute | solution.py:326
  22.3 5.2 %collective-permute-start.5 = (bf16[2,160,128]{2,1,0:T(8,128)(2,1)S(1)}, bf16[2,160,128]{2,1,0:T(8,128)(2,1)S(1)}, u32[]{:S(2)}, u32[]{:S(2)}) collective-permute-start(bf16[2,160,128]{2,1,0:T(8,128)(2,1)S(1)} %shard_map.64.own), channel_id=1, source_target_pairs={{0,16},{8,24},{16,0},{24,8},{1,17},{9,25},{17,1},{25,9},{2,18},{10... | collective-permute-start | bytes 245768 | tf_op jit(solution)/shard_map/ppermute | solution.py:326
  27.6 4.9 %collective-permute-start.6 = (bf16[2,160,128]{2,1,0:T(8,128)(2,1)S(1)}, bf16[2,160,128]{2,1,0:T(8,128)(2,1)S(1)}, u32[]{:S(2)}, u32[]{:S(2)}) collective-permute-start(bf16[2,160,128]{2,1,0:T(8,128)(2,1)S(1)} %get-tuple-element.40.own), channel_id=1, source_target_pairs={{0,32},{32,0},{64,96},{96,64},{1,33},{33,1},{65,97},{97,65},{2,34}... | collective-permute-start | bytes 245768 | tf_op jit(solution)/shard_map/ppermute | solution.py:326
  28.9 4.5 %collective-permute-start.7 = (bf16[2,160,128]{2,1,0:T(8,128)(2,1)S(1)}, bf16[2,160,128]{2,1,0:T(8,128)(2,1)S(1)}, u32[]{:S(2)}, u32[]{:S(2)}) collective-permute-start(bf16[2,160,128]{2,1,0:T(8,128)(2,1)S(1)} %get-tuple-element.40.own), channel_id=1, source_target_pairs={{0,96},{32,64},{64,32},{96,0},{1,97},{33,65},{65,33},{97,1},{2,98}... | collective-permute-start | bytes 245768 | tf_op jit(solution)/shard_map/ppermute | solution.py:326
  30.7 4.8 %collective-permute-start.8 = (bf16[2,160,128]{2,1,0:T(8,128)(2,1)S(1)}, bf16[2,160,128]{2,1,0:T(8,128)(2,1)S(1)}, u32[]{:S(2)}, u32[]{:S(2)}) collective-permute-start(bf16[2,160,128]{2,1,0:T(8,128)(2,1)S(1)} %get-tuple-element.40.own), channel_id=1, source_target_pairs={{0,64},{32,96},{64,0},{96,32},{1,65},{33,97},{65,1},{97,33},{2,66}... | collective-permute-start | bytes 245768 | tf_op jit(solution)/shard_map/ppermute | solution.py:326
  35.8 3.7 %collective-permute-start.9 = (bf16[2,160,128]{2,1,0:T(8,128)(2,1)S(1)}, bf16[2,160,128]{2,1,0:T(8,128)(2,1)S(1)}, u32[]{:S(2)}, u32[]{:S(2)}) collective-permute-start(bf16[2,160,128]{2,1,0:T(8,128)(2,1)S(1)} %get-tuple-element.42), channel_id=1, source_target_pairs={{0,2},{2,0},{4,6},{6,4},{1,3},{3,1},{5,7},{7,5},{8,10},{10,8},{12,... | collective-permute-start | bytes 245768 | tf_op jit(solution)/shard_map/ppermute | solution.py:326
  36.4 4.5 %collective-permute-start.10 = (bf16[2,160,128]{2,1,0:T(8,128)(2,1)S(1)}, bf16[2,160,128]{2,1,0:T(8,128)(2,1)S(1)}, u32[]{:S(2)}, u32[]{:S(2)}) collective-permute-start(bf16[2,160,128]{2,1,0:T(8,128)(2,1)S(1)} %get-tuple-element.43), channel_id=1, source_target_pairs={{0,6},{2,4},{4,2},{6,0},{1,7},{3,5},{5,3},{7,1},{8,14},{10,12},{12... | collective-permute-start | bytes 245768 | tf_op jit(solution)/shard_map/ppermute | solution.py:326
  41.7 21.2 %collective-permute-start.11 = (bf16[1024,512]{1,0:T(8,128)(2,1)S(1)}, bf16[1024,512]{1,0:T(8,128)(2,1)S(1)}, u32[]{:S(2)}, u32[]{:S(2)}) collective-permute-start(bf16[1024,512]{1,0:T(8,128)(2,1)S(1)} %outer_stage.3.refs_0_), channel_id=1, source_target_pairs={{0,1},{1,0},{2,3},{3,2},{4,5},{5,4},{6,7},{7,6},{8,9},{9,8},{10,11... | collective-permute-start | bytes 3145736 | tf_op jit(solution)/shard_map/ppermute | solution.py:420
  51.5 9.0 %collective-permute-start.14 = (bf16[1024,256]{1,0:T(8,128)(2,1)S(1)}, bf16[1024,256]{1,0:T(8,128)(2,1)S(1)}, u32[]{:S(2)}, u32[]{:S(2)}) collective-permute-start(bf16[1024,256]{1,0:T(8,128)(2,1)S(1)} %outer_stage.5.refs_0_), channel_id=1, source_target_pairs={{0,1},{1,0},{2,3},{3,2},{4,5},{5,4},{6,7},{7,6},{8,9},{9,8},{10,11... | collective-permute-start | bytes 1572872 | tf_op jit(solution)/shard_map/ppermute | solution.py:420
  52.7 4.9 %collective-permute-start.12 = (bf16[2,160,128]{2,1,0:T(8,128)(2,1)S(1)}, bf16[2,160,128]{2,1,0:T(8,128)(2,1)S(1)}, u32[]{:S(2)}, u32[]{:S(2)}) collective-permute-start(bf16[2,160,128]{2,1,0:T(8,128)(2,1)S(1)} %get-tuple-element.56), channel_id=1, source_target_pairs={{0,4},{2,6},{4,0},{6,2},{1,5},{3,7},{5,1},{7,3},{8,12},{10,14},{12... | collective-permute-start | bytes 245768 | tf_op jit(solution)/shard_map/ppermute | solution.py:326
  58.1 4.8 %collective-permute-start.13 = (bf16[1024,256]{1,0:T(8,128)(2,1)S(1)}, bf16[1024,256]{1,0:T(8,128)(2,1)S(1)}, u32[]{:S(2)}, u32[]{:S(2)}) collective-permute-start(bf16[1024,256]{1,0:T(8,128)(2,1)S(1)} %outer_stage.4.refs_1_), channel_id=1, source_target_pairs={{0,1},{1,0},{2,3},{3,2},{4,5},{5,4},{6,7},{7,6},{8,9},{9,8},{10,11... | collective-permute-start | bytes 1572872 | tf_op jit(solution)/shard_map/ppermute | solution.py:420

commit v6 on v4

--- a/solution.py
+++ b/solution.py
@@ -13,10 +13,10 @@
 ROWS = 160
 CHUNK = 256
 SEQ = ("seq_0", "seq_1", "seq_2")
-STEPS = (2, 1, 3)
+STEPS = (1, 2, 3)
 MIB = 2**20
 HEAD_LIMIT, OUT_LIMIT = (40 * MIB, 20 * MIB)
-SLOTS = (0, 2, 1, 3)
+SLOTS = (0, 1, 2, 3)
 OUT_STEPS = (0, 2, 1, 3)
 GROUPS = ((0,), (2, 1), (3,))
 F32, BF16 = (jnp.float32, jnp.bfloat16)
@@ -251,9 +251,12 @@
             rest = jnp.transpose(jnp.broadcast_to(wide[2:3], (128, 128)))[:32]
             norm = jnp.concatenate([top, rest], axis=0).astype(BF16)
             right = jnp.concatenate([low, norm], axis=1)
-            both = mm(feats[2 * i + h][...], right) + parts[2 * i + h][...]
             cols = slice(i * 256 + h * 128, i * 256 + (h + 1) * 128)
-            out[:, cols] = (both[:, :128] / both[:, 128:]).astype(BF16)
+            feat, part = (feats[2 * i + h], parts[2 * i + h])
+            half = feat.shape[0] // 2
+            for rows in (slice(0, half), slice(half, 2 * half)):
+                both = mm(feat[rows], right) + part[rows]
+                out[rows, cols] = (both[:, :128] / both[:, 128:]).astype(BF16)
 
 
 def outer_stage(prefixes, feats, parts):

time: 64.5 us -> 66.3 us (1.028)
  waiting for transfers between devices: 13.8 us -> 16.5 us
  starting transfers between devices: 24.3 us -> 23.3 us
    ppermute x12, waiting for transfers between devices: 13.8 us -> 16.5 us  [partner(): return lax.ppermute(x, axis, pairs)]
    ppermute x3, starting transfers between devices: 7.4 us -> 6.58 us  [per_device(): other.append(lax.ppermute(own[-1], 'head', [(0, 1), (1, 0)]))]
  transfers between devices with their start and end apart: 15 -> 15, of which waited for: 11 -> 8; matrix products, arithmetic and copies ran while one was open for 0% -> 0% of each run, Pallas kernels for 20% -> 19%
where the time goes in v6:
time: 66.3 us; the launch traced here: 66.2 us
  Pallas kernels  26 us (39%)
  starting transfers between devices  23.3 us (35%)
  waiting for transfers between devices  16.5 us (25%)
    ppermute x12, starting transfers between devices, partner(): return lax.ppermute(x, axis, pairs)  16.7 us
    ppermute x12, waiting for transfers between devices, partner(): return lax.ppermute(x, axis, pairs)  16.5 us
    pallas_call x1, Pallas kernels, head_stage(): pl.pallas_call(head_kernel, out_shape=[shape((tok, kd), BF16), shape((kd,...  9.34 us
    pallas_call x8, Pallas kernels, inner_stage(): pl.pallas_call(functools.partial(inner_kernel, slot, h), out_shape=[shape...  8.8 us
    ppermute x3, starting transfers between devices, per_device(): other.append(lax.ppermute(own[-1], 'head', [(0, 1), (1, 0)]))  6.58 us
    pallas_call x3, Pallas kernels, out_stage(): pl.pallas_call(functools.partial(out_kernel, places, last), out_shape=jax...  5.67 us
    pallas_call x3, Pallas kernels, outer_stage(): pl.pallas_call(functools.partial(outer_kernel, count), out_shape=jax.Shap...  1.83 us
  transfers between devices with their start and end apart: 15, of which 8 were waited for; matrix products, arithmetic and copies ran while one was open for 0% of the time, Pallas kernels for 19%

profile of v6, /device:TPU:1, one launch (start us, length us, event | category | flops | bytes accessed | tf_op | source)
XLA Modules:
  0.0 66.2 jit_solution(340040677451282117)
XLA Ops:
  0.0 0.0 copy-start
  0.0 9.3 %head_stage.1 = (bf16[1024,128]{1,0:T(8,128)(2,1)S(1)}, bf16[128,1024]{1,0:T(8,128)(2,1)S(1)}, bf16[4,1024,256]{2,1,0:T(8,128)(2,1)S(1)}, bf16[4,2,3,160,256]{4,...) custom-call(bf16[1024,2048]{1,0:T(8,128)(2,1)} %x_hbm.1, ...), custom_call_target="tpu_custom_call" | custom-call | flops 6000000000 | bytes 12582912 | tf_op jit(solution)/shard_map/head_stage/pallas_call | solution.py:167
  9.4 2.5 %collective-permute-start = (bf16[2,160,128]{2,1,0:T(8,128)(2,1)S(1)}, bf16[2,160,128]{2,1,0:T(8,128)(2,1)S(1)}, u32[]{:S(2)}, u32[]{:S(2)}) collective-permute-start(bf16[2,160,128]{2,1,0:T(8,128)(2,1)S(1)} %get-tuple-element.37), channel_id=1, source_target_pairs={{0,2},{2,0},{4,6},{6,4},{1,3},{3,1},{5,7},{7,5},{8,10},{10,8},{12,... | collective-permute-start | bytes 245768 | tf_op jit(solution)/shard_map/ppermute | solution.py:329
  11.9 3.3 %collective-permute-start.1 = (bf16[2,160,128]{2,1,0:T(8,128)(2,1)S(1)}, bf16[2,160,128]{2,1,0:T(8,128)(2,1)S(1)}, u32[]{:S(2)}, u32[]{:S(2)}) collective-permute-start(bf16[2,160,128]{2,1,0:T(8,128)(2,1)S(1)} %get-tuple-element.38), channel_id=1, source_target_pairs={{0,4},{2,6},{4,0},{6,2},{1,5},{3,7},{5,1},{7,3},{8,12},{10,14},{12... | collective-permute-start | bytes 245768 | tf_op jit(solution)/shard_map/ppermute | solution.py:329
  15.2 0.0 collective-permute-start.2
  15.2 0.0 copy-done
  15.2 1.1 %inner_stage.8 = (bf16[1024,160]{1,0:T(8,128)(2,1)S(1)}, f32[1024,256]{1,0:T(8,128)S(1)}) custom-call(bf16[1024,128]{1,0:T(8,128)(2,1)S(1)} %get-tuple-element.44.q_ref, bf16[128,1024]{1,0:T(8,128)(2,1)S(1)} %get-tuple-element.45.kt_ref, bf16[4,1024,256]{2,1,0:T(8,128)(2,1)S(1)} %get-tuple-element.46.val_ref, ...), custom_call_target="tpu_custom_call" | custom-call | flops 1000000000 | bytes 2097152 | tf_op jit(solution)/shard_map/inner_stage/pallas_call | solution.py:232
  16.3 0.0 collective-permute-done.p1
  16.3 2.2 %collective-permute-done.1.p2 = bf16[2,160,128]{2,1,0:T(8,128)(2,1)S(1)} collective-permute-done((bf16[2,160,128]{2,1,0:T(8,128)(2,1)S(1)}, bf16[2,160,128]{2,1,0:T(8,128)(2,1)S(1)}, u32[]{:S(2)}, u32[]{:S(2)}) %collective-permute-start.1) | collective-permute-done | bytes 81952 | tf_op jit(solution)/shard_map/ppermute | solution.py:329
  18.5 2.3 %collective-permute-done.2.p3 = bf16[2,160,128]{2,1,0:T(8,128)(2,1)S(1)} collective-permute-done((bf16[2,160,128]{2,1,0:T(8,128)(2,1)S(1)}, bf16[2,160,128]{2,1,0:T(8,128)(2,1)S(1)}, u32[]{:S(2)}, u32[]{:S(2)}) %collective-permute-start.2) | collective-permute-done | bytes 81952 | tf_op jit(solution)/shard_map/ppermute | solution.py:329
  20.9 1.4 %collective-permute-start.3 = (bf16[2,160,128]{2,1,0:T(8,128)(2,1)S(1)}, bf16[2,160,128]{2,1,0:T(8,128)(2,1)S(1)}, u32[]{:S(2)}, u32[]{:S(2)}) collective-permute-start(bf16[2,160,128]{2,1,0:T(8,128)(2,1)S(1)} %shard_map.64.own), channel_id=1, source_target_pairs={{0,8},{8,0},{16,24},{24,16},{1,9},{9,1},{17,25},{25,17},{2,10},{10... | collective-permute-start | bytes 245768 | tf_op jit(solution)/shard_map/ppermute | solution.py:329
  22.3 2.6 %collective-permute-start.4 = (bf16[2,160,128]{2,1,0:T(8,128)(2,1)S(1)}, bf16[2,160,128]{2,1,0:T(8,128)(2,1)S(1)}, u32[]{:S(2)}, u32[]{:S(2)}) collective-permute-start(bf16[2,160,128]{2,1,0:T(8,128)(2,1)S(1)} %shard_map.64.own), channel_id=1, source_target_pairs={{0,16},{8,24},{16,0},{24,8},{1,17},{9,25},{17,1},{25,9},{2,18},{10... | collective-permute-start | bytes 245768 | tf_op jit(solution)/shard_map/ppermute | solution.py:329
  24.9 0.0 collective-permute-start.5
  24.9 1.1 %inner_stage.9 = (bf16[1024,160]{1,0:T(8,128)(2,1)S(1)}, f32[1024,256]{1,0:T(8,128)S(1)}) custom-call(bf16[1024,128]{1,0:T(8,128)(2,1)S(1)} %get-tuple-element.44.q_ref, bf16[128,1024]{1,0:T(8,128)(2,1)S(1)} %get-tuple-element.45.kt_ref, bf16[4,1024,256]{2,1,0:T(8,128)(2,1)S(1)} %get-tuple-element.46.val_ref, ...), custom_call_target="tpu_custom_call" | custom-call | flops 1000000000 | bytes 2097152 | tf_op jit(solution)/shard_map/inner_stage/pallas_call | solution.py:232
  26.0 0.0 collective-permute-done.3.g0
  26.0 1.6 %collective-permute-done.4.g1 = bf16[2,160,128]{2,1,0:T(8,128)(2,1)S(1)} collective-permute-done((bf16[2,160,128]{2,1,0:T(8,128)(2,1)S(1)}, bf16[2,160,128]{2,1,0:T(8,128)(2,1)S(1)}, u32[]{:S(2)}, u32[]{:S(2)}) %collective-permute-start.4) | collective-permute-done | bytes 81952 | tf_op jit(solution)/shard_map/ppermute | solution.py:329
  27.6 2.6 %collective-permute-done.5.g2 = bf16[2,160,128]{2,1,0:T(8,128)(2,1)S(1)} collective-permute-done((bf16[2,160,128]{2,1,0:T(8,128)(2,1)S(1)}, bf16[2,160,128]{2,1,0:T(8,128)(2,1)S(1)}, u32[]{:S(2)}, u32[]{:S(2)}) %collective-permute-start.5) | collective-permute-done | bytes 81952 | tf_op jit(solution)/shard_map/ppermute | solution.py:329
  30.2 0.1 shard_map.65
  30.3 1.3 %collective-permute-start.6 = (bf16[2,160,128]{2,1,0:T(8,128)(2,1)S(1)}, bf16[2,160,128]{2,1,0:T(8,128)(2,1)S(1)}, u32[]{:S(2)}, u32[]{:S(2)}) collective-permute-start(bf16[2,160,128]{2,1,0:T(8,128)(2,1)S(1)} %get-tuple-element.40.own), channel_id=1, source_target_pairs={{0,32},{32,0},{64,96},{96,64},{1,33},{33,1},{65,97},{97,65},{2,34}... | collective-permute-start | bytes 245768 | tf_op jit(solution)/shard_map/ppermute | solution.py:329
  31.6 2.5 %collective-permute-start.7 = (bf16[2,160,128]{2,1,0:T(8,128)(2,1)S(1)}, bf16[2,160,128]{2,1,0:T(8,128)(2,1)S(1)}, u32[]{:S(2)}, u32[]{:S(2)}) collective-permute-start(bf16[2,160,128]{2,1,0:T(8,128)(2,1)S(1)} %get-tuple-element.40.own), channel_id=1, source_target_pairs={{0,64},{32,96},{64,0},{96,32},{1,65},{33,97},{65,1},{97,33},{2,66}... | collective-permute-start | bytes 245768 | tf_op jit(solution)/shard_map/ppermute | solution.py:329
  34.0 0.2 collective-permute-start.8
  34.3 1.1 %inner_stage.10 = (bf16[1024,160]{1,0:T(8,128)(2,1)S(1)}, f32[1024,256]{1,0:T(8,128)S(1)}) custom-call(bf16[1024,128]{1,0:T(8,128)(2,1)S(1)} %get-tuple-element.44.q_ref, bf16[128,1024]{1,0:T(8,128)(2,1)S(1)} %get-tuple-element.45.kt_ref, bf16[4,1024,256]{2,1,0:T(8,128)(2,1)S(1)} %get-tuple-element.46.val_ref, ...), custom_call_target="tpu_custom_call" | custom-call | flops 1000000000 | bytes 2097152 | tf_op jit(solution)/shard_map/inner_stage/pallas_call | solution.py:232
  35.4 0.0 collective-permute-done.6.g0
  35.4 1.4 %collective-permute-done.7.g1 = bf16[2,160,128]{2,1,0:T(8,128)(2,1)S(1)} collective-permute-done((bf16[2,160,128]{2,1,0:T(8,128)(2,1)S(1)}, bf16[2,160,128]{2,1,0:T(8,128)(2,1)S(1)}, u32[]{:S(2)}, u32[]{:S(2)}) %collective-permute-start.7) | collective-permute-done | bytes 81952 | tf_op jit(solution)/shard_map/ppermute | solution.py:329
  36.7 2.1 %collective-permute-done.8.g2 = bf16[2,160,128]{2,1,0:T(8,128)(2,1)S(1)} collective-permute-done((bf16[2,160,128]{2,1,0:T(8,128)(2,1)S(1)}, bf16[2,160,128]{2,1,0:T(8,128)(2,1)S(1)}, u32[]{:S(2)}, u32[]{:S(2)}) %collective-permute-start.8) | collective-permute-done | bytes 81952 | tf_op jit(solution)/shard_map/ppermute | solution.py:329
  38.9 0.3 shard_map.66
  39.1 0.1 collective-permute-start.9
  39.2 1.6 %collective-permute-start.10 = (bf16[2,160,128]{2,1,0:T(8,128)(2,1)S(1)}, bf16[2,160,128]{2,1,0:T(8,128)(2,1)S(1)}, u32[]{:S(2)}, u32[]{:S(2)}) collective-permute-start(bf16[2,160,128]{2,1,0:T(8,128)(2,1)S(1)} %get-tuple-element.43), channel_id=1, source_target_pairs={{0,2},{2,0},{4,6},{6,4},{1,3},{3,1},{5,7},{7,5},{8,10},{10,8},{12,... | collective-permute-start | bytes 245768 | tf_op jit(solution)/shard_map/ppermute | solution.py:329
  40.8 1.1 %inner_stage.11 = (bf16[1024,160]{1,0:T(8,128)(2,1)S(1)}, f32[1024,256]{1,0:T(8,128)S(1)}) custom-call(bf16[1024,128]{1,0:T(8,128)(2,1)S(1)} %get-tuple-element.44.q_ref, bf16[128,1024]{1,0:T(8,128)(2,1)S(1)} %get-tuple-element.45.kt_ref, bf16[4,1024,256]{2,1,0:T(8,128)(2,1)S(1)} %get-tuple-element.46.val_ref, ...), custom_call_target="tpu_custom_call" | custom-call | flops 1000000000 | bytes 2097152 | tf_op jit(solution)/shard_map/inner_stage/pallas_call | solution.py:232
  41.9 2.1 %collective-permute-done.9.refs_0_ = bf16[2,160,128]{2,1,0:T(8,128)(2,1)S(1)} collective-permute-done((bf16[2,160,128]{2,1,0:T(8,128)(2,1)S(1)}, bf16[2,160,128]{2,1,0:T(8,128)(2,1)S(1)}, u32[]{:S(2)}, u32[]{:S(2)}) %collective-permute-start.9) | collective-permute-done | bytes 81952 | tf_op jit(solution)/shard_map/ppermute | solution.py:329
  44.0 0.0 collective-permute-done.10.refs_1_
  44.0 0.8 %outer_stage.3.refs_0_ = bf16[1024,512]{1,0:T(8,128)(2,1)S(1)} custom-call(bf16[2,160,128]{2,1,0:T(8,128)(2,1)S(1)} %collective-permute-done.9.refs_0_, bf16[2,160,128]{2,1,0:T(8,128)(2,1)S(1)} %collective-permute-done.10.refs_1_, bf16[1024,160]{1,0:T(8,128)(2,1)S(1)} %get-tuple-element.48.refs_2_, bf16[1024,160]{1,0:T(8,128)(2,1)S(1)} %get-tuple-element.49.refs_3_, ...), custom_call_target="tpu_custom_call" | custom-call | flops 600000000 | bytes 2097152 | tf_op jit(solution)/shard_map/outer_stage/pallas_call | solution.py:265
  44.8 4.8 %collective-permute-start.11 = (bf16[1024,512]{1,0:T(8,128)(2,1)S(1)}, bf16[1024,512]{1,0:T(8,128)(2,1)S(1)}, u32[]{:S(2)}, u32[]{:S(2)}) collective-permute-start(bf16[1024,512]{1,0:T(8,128)(2,1)S(1)} %outer_stage.3.refs_0_), channel_id=1, source_target_pairs={{0,1},{1,0},{2,3},{3,2},{4,5},{5,4},{6,7},{7,6},{8,9},{9,8},{10,11... | collective-permute-start | bytes 3145736 | tf_op jit(solution)/shard_map/ppermute | solution.py:423
  49.6 1.1 %inner_stage.14 = (bf16[1024,160]{1,0:T(8,128)(2,1)S(1)}, f32[1024,256]{1,0:T(8,128)S(1)}) custom-call(bf16[1024,128]{1,0:T(8,128)(2,1)S(1)} %get-tuple-element.44.q_ref, bf16[128,1024]{1,0:T(8,128)(2,1)S(1)} %get-tuple-element.45.kt_ref, bf16[4,1024,256]{2,1,0:T(8,128)(2,1)S(1)} %get-tuple-element.46.val_ref, ...), custom_call_target="tpu_custom_call" | custom-call | flops 1000000000 | bytes 2097152 | tf_op jit(solution)/shard_map/inner_stage/pallas_call | solution.py:232
  50.7 1.1 %inner_stage.15 = (bf16[1024,160]{1,0:T(8,128)(2,1)S(1)}, f32[1024,256]{1,0:T(8,128)S(1)}) custom-call(bf16[1024,128]{1,0:T(8,128)(2,1)S(1)} %get-tuple-element.44.q_ref, bf16[128,1024]{1,0:T(8,128)(2,1)S(1)} %get-tuple-element.45.kt_ref, bf16[4,1024,256]{2,1,0:T(8,128)(2,1)S(1)} %get-tuple-element.46.val_ref, ...), custom_call_target="tpu_custom_call" | custom-call | flops 1000000000 | bytes 2097152 | tf_op jit(solution)/shard_map/inner_stage/pallas_call | solution.py:232
  51.8 0.5 outer_stage.5.refs_0_
  52.3 0.1 collective-permute-start.14
  52.4 1.1 %inner_stage.12 = (bf16[1024,160]{1,0:T(8,128)(2,1)S(1)}, f32[1024,256]{1,0:T(8,128)S(1)}) custom-call(bf16[1024,128]{1,0:T(8,128)(2,1)S(1)} %get-tuple-element.44.q_ref, bf16[128,1024]{1,0:T(8,128)(2,1)S(1)} %get-tuple-element.45.kt_ref, bf16[4,1024,256]{2,1,0:T(8,128)(2,1)S(1)} %get-tuple-element.46.val_ref, ...), custom_call_target="tpu_custom_call" | custom-call | flops 1000000000 | bytes 2097152 | tf_op jit(solution)/shard_map/inner_stage/pallas_call | solution.py:232
  53.5 1.2 %collective-permute-start.12 = (bf16[2,160,128]{2,1,0:T(8,128)(2,1)S(1)}, bf16[2,160,128]{2,1,0:T(8,128)(2,1)S(1)}, u32[]{:S(2)}, u32[]{:S(2)}) collective-permute-start(bf16[2,160,128]{2,1,0:T(8,128)(2,1)S(1)} %get-tuple-element.56), channel_id=1, source_target_pairs={{0,6},{2,4},{4,2},{6,0},{1,7},{3,5},{5,3},{7,1},{8,14},{10,12},{12... | collective-permute-start | bytes 245768 | tf_op jit(solution)/shard_map/ppermute | solution.py:329
  54.8 1.1 %inner_stage.13 = (bf16[1024,160]{1,0:T(8,128)(2,1)S(1)}, f32[1024,256]{1,0:T(8,128)S(1)}) custom-call(bf16[1024,128]{1,0:T(8,128)(2,1)S(1)} %get-tuple-element.44.q_ref, bf16[128,1024]{1,0:T(8,128)(2,1)S(1)} %get-tuple-element.45.kt_ref, bf16[4,1024,256]{2,1,0:T(8,128)(2,1)S(1)} %get-tuple-element.46.val_ref, ...), custom_call_target="tpu_custom_call" | custom-call | flops 1000000000 | bytes 2097152 | tf_op jit(solution)/shard_map/inner_stage/pallas_call | solution.py:232
  55.9 2.2 %collective-permute-done.12.refs_0_ = bf16[2,160,128]{2,1,0:T(8,128)(2,1)S(1)} collective-permute-done((bf16[2,160,128]{2,1,0:T(8,128)(2,1)S(1)}, bf16[2,160,128]{2,1,0:T(8,128)(2,1)S(1)}, u32[]{:S(2)}, u32[]{:S(2)}) %collective-permute-start.12) | collective-permute-done | bytes 81952 | tf_op jit(solution)/shard_map/ppermute | solution.py:329
  58.1 0.5 outer_stage.4.refs_1_
  58.6 1.7 %collective-permute-start.13 = (bf16[1024,256]{1,0:T(8,128)(2,1)S(1)}, bf16[1024,256]{1,0:T(8,128)(2,1)S(1)}, u32[]{:S(2)}, u32[]{:S(2)}) collective-permute-start(bf16[1024,256]{1,0:T(8,128)(2,1)S(1)} %outer_stage.4.refs_1_), channel_id=1, source_target_pairs={{0,1},{1,0},{2,3},{3,2},{4,5},{5,4},{6,7},{7,6},{8,9},{9,8},{10,11... | collective-permute-start | bytes 1572872 | tf_op jit(solution)/shard_map/ppermute | solution.py:423
  60.3 0.7 %out_stage.3.refs_4_ = f32[1024,1024]{1,0:T(8,128)S(1)} custom-call(bf16[1024,256]{1,0:T(8,128)(2,1)S(1)} %outer_stage.5.refs_0_, bf16[2,1024,1024]{2,1,0:T(8,128)(2,1)S(1)} %get-tuple-element.61.refs_1_.refs_3_.refs_2_), custom_call_target="tpu_custom_call" | custom-call | flops 536870912 | bytes 1048576 | tf_op jit(solution)/shard_map/out_stage/pallas_call | solution.py:311
  61.1 0.0 collective-permute-done.14.refs_2_
  61.1 2.3 %out_stage.4.refs_3_ = f32[1024,1024]{1,0:T(8,128)S(1)} custom-call(bf16[1024,512]{1,0:T(8,128)(2,1)S(1)} %outer_stage.3.refs_0_, bf16[1024,256]{1,0:T(8,128)(2,1)S(1)} %outer_stage.4.refs_1_, bf16[1024,256]{1,0:T(8,128)(2,1)S(1)} %collective-permute-done.14.refs_2_, bf16[2,1024,1024]{2,1,0:T(8,128)(2,1)S(1)} %get-tuple-element.61.refs_1_.refs_3_.refs_2_, ...), custom_call_target="tpu_custom_call" | custom-call | flops 2147483648 | bytes 1048576 | tf_op jit(solution)/shard_map/out_stage/pallas_call | solution.py:311
  63.4 0.0 collective-permute-done.13.refs_1_
  63.4 0.0 collective-permute-done.11.refs_0_
  63.4 2.6 %out_stage.5 = bf16[1024,1024]{1,0:T(8,128)(2,1)} custom-call(bf16[1024,512]{1,0:T(8,128)(2,1)S(1)} %collective-permute-done.11.refs_0_, bf16[1024,256]{1,0:T(8,128)(2,1)S(1)} %collective-permute-done.13.refs_1_, bf16[2,1024,1024]{2,1,0:T(8,128)(2,1)S(1)} %get-tuple-element.61.refs_1_.refs_3_.refs_2_, f32[1024,1024]{1,0:T(8,128)S(1)} %out_stage.4.refs_3_), custom_call_target="tpu_custom_call" | custom-call | flops 1610612736 | bytes 1048576 | tf_op jit(solution)/shard_map/out_stage/pallas_call | solution.py:311
  (1 shorter events, 0.0 us)
Async XLA Ops:
  0.0 15.2 %copy-start = (f32[8,160]{1,0:T(8,128)S(1)}, f32[8,160]{1,0:T(8,128)}, u32[]{:S(2)}) copy-start(f32[8,160]{1,0:T(8,128)} %constant.2.clone.table_ref) | copy-start | bytes 15364
  9.4 6.9 %collective-permute-start = (bf16[2,160,128]{2,1,0:T(8,128)(2,1)S(1)}, bf16[2,160,128]{2,1,0:T(8,128)(2,1)S(1)}, u32[]{:S(2)}, u32[]{:S(2)}) collective-permute-start(bf16[2,160,128]{2,1,0:T(8,128)(2,1)S(1)} %get-tuple-element.37), channel_id=1, source_target_pairs={{0,2},{2,0},{4,6},{6,4},{1,3},{3,1},{5,7},{7,5},{8,10},{10,8},{12,... | collective-permute-start | bytes 245768 | tf_op jit(solution)/shard_map/ppermute | solution.py:329
  11.9 6.6 %collective-permute-start.1 = (bf16[2,160,128]{2,1,0:T(8,128)(2,1)S(1)}, bf16[2,160,128]{2,1,0:T(8,128)(2,1)S(1)}, u32[]{:S(2)}, u32[]{:S(2)}) collective-permute-start(bf16[2,160,128]{2,1,0:T(8,128)(2,1)S(1)} %get-tuple-element.38), channel_id=1, source_target_pairs={{0,4},{2,6},{4,0},{6,2},{1,5},{3,7},{5,1},{7,3},{8,12},{10,14},{12... | collective-permute-start | bytes 245768 | tf_op jit(solution)/shard_map/ppermute | solution.py:329
  15.2 5.6 %collective-permute-start.2 = (bf16[2,160,128]{2,1,0:T(8,128)(2,1)S(1)}, bf16[2,160,128]{2,1,0:T(8,128)(2,1)S(1)}, u32[]{:S(2)}, u32[]{:S(2)}) collective-permute-start(bf16[2,160,128]{2,1,0:T(8,128)(2,1)S(1)} %get-tuple-element.39), channel_id=1, source_target_pairs={{0,6},{2,4},{4,2},{6,0},{1,7},{3,5},{5,3},{7,1},{8,14},{10,12},{12... | collective-permute-start | bytes 245768 | tf_op jit(solution)/shard_map/ppermute | solution.py:329
  20.9 5.1 %collective-permute-start.3 = (bf16[2,160,128]{2,1,0:T(8,128)(2,1)S(1)}, bf16[2,160,128]{2,1,0:T(8,128)(2,1)S(1)}, u32[]{:S(2)}, u32[]{:S(2)}) collective-permute-start(bf16[2,160,128]{2,1,0:T(8,128)(2,1)S(1)} %shard_map.64.own), channel_id=1, source_target_pairs={{0,8},{8,0},{16,24},{24,16},{1,9},{9,1},{17,25},{25,17},{2,10},{10... | collective-permute-start | bytes 245768 | tf_op jit(solution)/shard_map/ppermute | solution.py:329
  22.3 5.4 %collective-permute-start.4 = (bf16[2,160,128]{2,1,0:T(8,128)(2,1)S(1)}, bf16[2,160,128]{2,1,0:T(8,128)(2,1)S(1)}, u32[]{:S(2)}, u32[]{:S(2)}) collective-permute-start(bf16[2,160,128]{2,1,0:T(8,128)(2,1)S(1)} %shard_map.64.own), channel_id=1, source_target_pairs={{0,16},{8,24},{16,0},{24,8},{1,17},{9,25},{17,1},{25,9},{2,18},{10... | collective-permute-start | bytes 245768 | tf_op jit(solution)/shard_map/ppermute | solution.py:329
  24.9 5.3 %collective-permute-start.5 = (bf16[2,160,128]{2,1,0:T(8,128)(2,1)S(1)}, bf16[2,160,128]{2,1,0:T(8,128)(2,1)S(1)}, u32[]{:S(2)}, u32[]{:S(2)}) collective-permute-start(bf16[2,160,128]{2,1,0:T(8,128)(2,1)S(1)} %shard_map.64.own), channel_id=1, source_target_pairs={{0,24},{8,16},{16,8},{24,0},{1,25},{9,17},{17,9},{25,1},{2,26},{10... | collective-permute-start | bytes 245768 | tf_op jit(solution)/shard_map/ppermute | solution.py:329
  30.3 5.0 %collective-permute-start.6 = (bf16[2,160,128]{2,1,0:T(8,128)(2,1)S(1)}, bf16[2,160,128]{2,1,0:T(8,128)(2,1)S(1)}, u32[]{:S(2)}, u32[]{:S(2)}) collective-permute-start(bf16[2,160,128]{2,1,0:T(8,128)(2,1)S(1)} %get-tuple-element.40.own), channel_id=1, source_target_pairs={{0,32},{32,0},{64,96},{96,64},{1,33},{33,1},{65,97},{97,65},{2,34}... | collective-permute-start | bytes 245768 | tf_op jit(solution)/shard_map/ppermute | solution.py:329
  31.6 5.2 %collective-permute-start.7 = (bf16[2,160,128]{2,1,0:T(8,128)(2,1)S(1)}, bf16[2,160,128]{2,1,0:T(8,128)(2,1)S(1)}, u32[]{:S(2)}, u32[]{:S(2)}) collective-permute-start(bf16[2,160,128]{2,1,0:T(8,128)(2,1)S(1)} %get-tuple-element.40.own), channel_id=1, source_target_pairs={{0,64},{32,96},{64,0},{96,32},{1,65},{33,97},{65,1},{97,33},{2,66}... | collective-permute-start | bytes 245768 | tf_op jit(solution)/shard_map/ppermute | solution.py:329
  34.0 4.8 %collective-permute-start.8 = (bf16[2,160,128]{2,1,0:T(8,128)(2,1)S(1)}, bf16[2,160,128]{2,1,0:T(8,128)(2,1)S(1)}, u32[]{:S(2)}, u32[]{:S(2)}) collective-permute-start(bf16[2,160,128]{2,1,0:T(8,128)(2,1)S(1)} %get-tuple-element.40.own), channel_id=1, source_target_pairs={{0,96},{32,64},{64,32},{96,0},{1,97},{33,65},{65,33},{97,1},{2,98}... | collective-permute-start | bytes 245768 | tf_op jit(solution)/shard_map/ppermute | solution.py:329
  39.1 4.9 %collective-permute-start.9 = (bf16[2,160,128]{2,1,0:T(8,128)(2,1)S(1)}, bf16[2,160,128]{2,1,0:T(8,128)(2,1)S(1)}, u32[]{:S(2)}, u32[]{:S(2)}) collective-permute-start(bf16[2,160,128]{2,1,0:T(8,128)(2,1)S(1)} %get-tuple-element.42), channel_id=1, source_target_pairs={{0,4},{2,6},{4,0},{6,2},{1,5},{3,7},{5,1},{7,3},{8,12},{10,14},{12... | collective-permute-start | bytes 245768 | tf_op jit(solution)/shard_map/ppermute | solution.py:329
  39.2 4.8 %collective-permute-start.10 = (bf16[2,160,128]{2,1,0:T(8,128)(2,1)S(1)}, bf16[2,160,128]{2,1,0:T(8,128)(2,1)S(1)}, u32[]{:S(2)}, u32[]{:S(2)}) collective-permute-start(bf16[2,160,128]{2,1,0:T(8,128)(2,1)S(1)} %get-tuple-element.43), channel_id=1, source_target_pairs={{0,2},{2,0},{4,6},{6,4},{1,3},{3,1},{5,7},{7,5},{8,10},{10,8},{12,... | collective-permute-start | bytes 245768 | tf_op jit(solution)/shard_map/ppermute | solution.py:329
  44.8 18.6 %collective-permute-start.11 = (bf16[1024,512]{1,0:T(8,128)(2,1)S(1)}, bf16[1024,512]{1,0:T(8,128)(2,1)S(1)}, u32[]{:S(2)}, u32[]{:S(2)}) collective-permute-start(bf16[1024,512]{1,0:T(8,128)(2,1)S(1)} %outer_stage.3.refs_0_), channel_id=1, source_target_pairs={{0,1},{1,0},{2,3},{3,2},{4,5},{5,4},{6,7},{7,6},{8,9},{9,8},{10,11... | collective-permute-start | bytes 3145736 | tf_op jit(solution)/shard_map/ppermute | solution.py:423
  52.3 8.7 %collective-permute-start.14 = (bf16[1024,256]{1,0:T(8,128)(2,1)S(1)}, bf16[1024,256]{1,0:T(8,128)(2,1)S(1)}, u32[]{:S(2)}, u32[]{:S(2)}) collective-permute-start(bf16[1024,256]{1,0:T(8,128)(2,1)S(1)} %outer_stage.5.refs_0_), channel_id=1, source_target_pairs={{0,1},{1,0},{2,3},{3,2},{4,5},{5,4},{6,7},{7,6},{8,9},{9,8},{10,11... | collective-permute-start | bytes 1572872 | tf_op jit(solution)/shard_map/ppermute | solution.py:423
  53.5 4.6 %collective-permute-start.12 = (bf16[2,160,128]{2,1,0:T(8,128)(2,1)S(1)}, bf16[2,160,128]{2,1,0:T(8,128)(2,1)S(1)}, u32[]{:S(2)}, u32[]{:S(2)}) collective-permute-start(bf16[2,160,128]{2,1,0:T(8,128)(2,1)S(1)} %get-tuple-element.56), channel_id=1, source_target_pairs={{0,6},{2,4},{4,2},{6,0},{1,7},{3,5},{5,3},{7,1},{8,14},{10,12},{12... | collective-permute-start | bytes 245768 | tf_op jit(solution)/shard_map/ppermute | solution.py:329
  58.6 4.8 %collective-permute-start.13 = (bf16[1024,256]{1,0:T(8,128)(2,1)S(1)}, bf16[1024,256]{1,0:T(8,128)(2,1)S(1)}, u32[]{:S(2)}, u32[]{:S(2)}) collective-permute-start(bf16[1024,256]{1,0:T(8,128)(2,1)S(1)} %outer_stage.4.refs_1_), channel_id=1, source_target_pairs={{0,1},{1,0},{2,3},{3,2},{4,5},{5,4},{6,7},{7,6},{8,9},{9,8},{10,11... | collective-permute-start | bytes 1572872 | tf_op jit(solution)/shard_map/ppermute | solution.py:423
